TPU v7x, 32 devices: a whole 2x2x4 slice. The times are simulated.
32 devices in a mesh: span: 32 (over z, y, x, core).
Axes of the slice: x: 2, y: 2, z: 4, core: 2. Of those that a mesh axis runs over, the one named last changes fastest.
Arguments:
- random_slabs: bfloat16 [1024, 4, 3, 2048], P('span'), may hold values from -6 to 6
- span_weights: float32 [513], replicated, may hold values from 0.1 to 2
- wall_filter: bfloat16 [2048, 2048], replicated, may hold values from -0.125 to 0.125
- prev_state: float32 [1024, 3, 2048], P('span'), may hold values from -6 to 6
- time_scale: float32 [3, 2048], replicated, may hold values from 1 to 32
- mean_velocity: float32 [2048], replicated, may hold values from 0 to 2
- lund_diag: float32 [3, 2048], replicated, may hold values from 0.3 to 3
- lund_off: float32 [3, 2048], replicated, may hold values from -1 to 1
Outputs:
- velocity: bfloat16 [1024, 4, 3, 2048], P('span')
- new_state: float32 [1024, 3, 2048], P('span')
All inputs are finite; a program needn't handle non-finite values.
Results may differ from a plain program's by a relative error of at most 0.0051.
Values may be sent and summed in bfloat16 or wider, within the bound.
No kernel may reach another device: no remote copies, remote signals or barrier semaphores. Data moves between devices by JAX's collectives and lax.ppermute only.
A program may use at most 128 MiB of HBM per device.

v0:
```python
import jax
import jax.numpy as jnp
from jax import lax
from jax.sharding import PartitionSpec as P


def from_partner(value, axis, bit):
    return lax.ppermute(value, axis, [(i, i ^ 1 << bit) for i in range(lax.axis_size(axis))])


def band_matrix(taps, height):
    reach = taps.shape[0]
    padded = jnp.concatenate([taps, jnp.zeros((height,), taps.dtype)])
    length = reach + height
    tiled = jnp.tile(padded, height)[: height * (length - 1)]
    return tiled.reshape(height, length - 1)


def butterfly(held, forward):
    count = lax.axis_size("span")
    device = lax.axis_index("span")
    levels = count.bit_length() - 1
    for level in range(levels - 1, -1, -1):
        groups, inner_first, targets, inner_last = held.shape
        halves = held.reshape(groups, inner_first, 2, targets // 2, inner_last)
        lower = halves[:, :, 0]
        higher = halves[:, :, 1]
        upper = device >> level & 1 == 1
        kept = jnp.where(upper, higher, lower)
        given = jnp.where(upper, lower, higher)
        if forward:
            taken = from_partner(given, "span", level)
        else:
            taken = from_partner(given, "span", level)
        first = jnp.where(upper, taken, kept)
        second = jnp.where(upper, kept, taken)
        held = jnp.stack([first, second], axis=1).reshape(
            groups * 2, inner_first, targets // 2, inner_last
        )
    return held


def body(
    random_slabs,
    span_weights,
    wall_filter,
    prev_state,
    time_scale,
    mean_velocity,
    lund_diag,
    lund_off,
):
    rows = random_slabs.shape[0]
    planes = random_slabs.shape[1]
    width = random_slabs.shape[3]
    columns = planes * 3 * width
    flat = random_slabs.reshape(rows, columns)
    scaling = jnp.sqrt(jnp.sum(span_weights * span_weights))
    taps = (span_weights / scaling).astype(jnp.bfloat16)
    reach = (span_weights.shape[0] - 1) // 2
    count = lax.axis_size("span")
    slim = columns // count
    held = butterfly(flat.reshape(1, rows, count, slim), True)
    total = rows * count
    whole = held.reshape(total, slim)
    height = min(512, total)
    matrix = band_matrix(taps, height)
    wrapped = jnp.concatenate([whole[total - reach :], whole, whole[:reach]], axis=0)

    def one_block(start):
        window = lax.dynamic_slice_in_dim(wrapped, start, height + 2 * reach, 0)
        return jnp.dot(matrix, window, preferred_element_type=jnp.float32)

    starts = jnp.arange(total // height) * height
    summed_cols = lax.map(one_block, starts).reshape(total, slim)
    rounded = summed_cols.astype(jnp.bfloat16)
    returned = butterfly(rounded.reshape(1, 1, count, rows * slim), False)
    spanned = returned.reshape(count, rows, slim).transpose(1, 0, 2).reshape(rows, planes, 3, width)
    filtered = lax.dot_general(
        spanned, wall_filter, (((3,), (1,)), ((), ())), preferred_element_type=jnp.float32
    )
    decay = jnp.exp(-jnp.pi / (2.0 * time_scale))
    inject = jnp.sqrt(1.0 - jnp.exp(-jnp.pi / time_scale))
    state = prev_state
    outputs = []
    for plane in range(planes):
        state = decay * state + inject * filtered[:, plane]
        along = state[:, 0]
        normal = state[:, 1]
        spanwise = state[:, 2]
        first = mean_velocity + lund_diag[0] * along
        second = lund_off[0] * along + lund_diag[1] * normal
        third = lund_off[1] * along + lund_off[2] * normal + lund_diag[2] * spanwise
        outputs.append(jnp.stack([first, second, third], axis=1).astype(jnp.bfloat16))
    velocity = jnp.stack(outputs, axis=1)
    return (velocity, state)


def solution(mesh):
    placed = (P("span", None, None, None), P(), P(), P("span", None, None), P(), P(), P(), P())
    return jax.shard_map(
        body,
        mesh=mesh,
        in_specs=placed,
        out_specs=(P("span", None, None, None), P("span", None, None)),
        check_vma=False,
    )
```

profile of v0, /device:TPU:0, one launch (start us, length us, event | category | flops | bytes accessed | tf_op | source)
XLA Modules:
  0.0 253.5 jit_solution(12371556991977251959)
XLA Ops:
  0.6 4.2 %copy.148 = bf16[32,4,3,2048]{3,2,1,0:T(4,128)(2,1)} copy(bf16[32,4,3,2048]{3,1,2,0:T(4,128)(2,1)} %param.10) | data formatting | bytes 3145728 | tf_op args[0]
  4.9 4.2 %reshape_reshape_reshape.3 = bf16[1,32,2,16,768]{4,3,2,1,0:T(8,128)(2,1)S(1)} reshape(bf16[32,4,3,2048]{3,2,1,0:T(4,128)(2,1)} %copy.148) | data formatting | bytes 3145728 | tf_op jit(solution)/shard_map/reshape;reshape;reshape | solution.py:25
  9.2 4.1 %collective-permute-start = (bf16[1,32,16,768]{3,2,1,0:T(8,128)(2,1)S(1)}, bf16[1,32,16,768]{3,2,1,0:T(8,128)(2,1)S(1)}, u32[]{:S(2)}, u32[]{:S(2)}) collective-permute-start(bf16[1,32,16,768]{3,2,1,0:T(8,128)(2,1)S(1)} %fusion.28), channel_id=1, source_target_pairs={{0,16},{1,17},{2,18},{3,19},{4,20},{5,21},{6,22},{7,23},{8,24},{9,... | collective-permute-start | bytes 2359304 | tf_op jit(solution)/shard_map/ppermute | solution.py:8
  13.3 34.4 %collective-permute-done = bf16[1,32,16,768]{3,2,1,0:T(8,128)(2,1)S(1)} collective-permute-done((bf16[1,32,16,768]{3,2,1,0:T(8,128)(2,1)S(1)}, bf16[1,32,16,768]{3,2,1,0:T(8,128)(2,1)S(1)}, u32[]{:S(2)}, u32[]{:S(2)}) %collective-permute-start) | collective-permute-done | bytes 786464 | tf_op jit(solution)/shard_map/ppermute | solution.py:8
  49.2 18.0 %collective-permute-done.1 = bf16[2,32,8,768]{3,1,2,0:T(8,128)(2,1)S(1)} collective-permute-done((bf16[2,32,8,768]{3,1,2,0:T(8,128)(2,1)S(1)}, bf16[2,32,8,768]{3,1,2,0:T(8,128)(2,1)S(1)}, u32[]{:S(2)}, u32[]{:S(2)}) %collective-permute-start.1) | collective-permute-done | bytes 786464 | tf_op jit(solution)/shard_map/ppermute | solution.py:8
  67.5 1.4 collective-permute-start.2
  68.9 16.5 %collective-permute-done.2 = bf16[4,32,4,768]{3,1,2,0:T(8,128)(2,1)S(1)} collective-permute-done((bf16[4,32,4,768]{3,1,2,0:T(8,128)(2,1)S(1)}, bf16[4,32,4,768]{3,1,2,0:T(8,128)(2,1)S(1)}, u32[]{:S(2)}, u32[]{:S(2)}) %collective-permute-start.2) | collective-permute-done | bytes 786464 | tf_op jit(solution)/shard_map/ppermute | solution.py:8
  86.0 1.3 collective-permute-start.3
  87.3 15.7 %collective-permute-done.3 = bf16[8,32,2,768]{3,1,2,0:T(8,128)(2,1)S(1)} collective-permute-done((bf16[8,32,2,768]{3,1,2,0:T(8,128)(2,1)S(1)}, bf16[8,32,2,768]{3,1,2,0:T(8,128)(2,1)S(1)}, u32[]{:S(2)}, u32[]{:S(2)}) %collective-permute-start.3) | collective-permute-done | bytes 786464 | tf_op jit(solution)/shard_map/ppermute | solution.py:8
  105.7 2.3 tile.10
  109.2 1.3 reshape.697
  110.5 1.3 select_bitcast_fusion.6
  113.4 9.2 %while.10 = (s32[]{:T(128)}, bf16[2,512,768]{1,2,0:T(8,128)(2,1)}, s32[2]{0:T(128)S(1)}, bf16[1536,768]{1,0:T(8,128)(2,1)S(1)}, bf16[512,1024]{1,0:T(8,128)(2,1)S(1)}, /*index=5*/s32[]{:T(128)}, s32[]{:T(128)}, s32[]{:T(128)}) while((s32[]{:T(128)}, bf16[2,512,768]{1,2,0:T(8,128)(2,1)}, s32[2]{0:T(128)S(1)}, bf16[1536,768]{1,0:T(8,128)(2,1)S(1)}, ...), condition=%wide.region_2.3_spmd, body=%wide.region_1.2_spmd.sunk | while | flops 805306368 | bytes 4194951 | solution.py:75
  116.1 1.9 bitcast_dynamic-update-slice_fusion.2
  120.7 1.9 bitcast_dynamic-update-slice_fusion.2
  122.6 1.7 copy.173
  125.2 5.3 %collective-permute-start.5 = (bf16[1,1,16,24576]{3,2,1,0:T(8,128)(2,1)S(1)}, bf16[1,1,16,24576]{3,2,1,0:T(8,128)(2,1)S(1)}, u32[]{:S(2)}, u32[]{:S(2)}) collective-permute-start(bf16[1,1,16,24576]{3,2,1,0:T(8,128)(2,1)S(1)} %select_bitcast_fusion.5), channel_id=1, source_target_pairs={{0,16},{1,17},{2,18},{3,19},{4,20},{5,21},{6,22},{7,23},{8,24},{9,... | collective-permute-start | bytes 2359304 | tf_op jit(solution)/shard_map/ppermute | solution.py:8
  130.4 34.6 %collective-permute-done.5 = bf16[1,1,16,24576]{3,2,1,0:T(8,128)(2,1)S(1)} collective-permute-done((bf16[1,1,16,24576]{3,2,1,0:T(8,128)(2,1)S(1)}, bf16[1,1,16,24576]{3,2,1,0:T(8,128)(2,1)S(1)}, u32[]{:S(2)}, u32[]{:S(2)}) %collective-permute-start.5) | collective-permute-done | bytes 786464 | tf_op jit(solution)/shard_map/ppermute | solution.py:8
  165.8 18.4 %collective-permute-done.6 = bf16[2,1,8,24576]{3,2,0,1:T(8,128)(2,1)S(1)} collective-permute-done((bf16[2,1,8,24576]{3,2,0,1:T(8,128)(2,1)S(1)}, bf16[2,1,8,24576]{3,2,0,1:T(8,128)(2,1)S(1)}, u32[]{:S(2)}, u32[]{:S(2)}) %collective-permute-start.6) | collective-permute-done | bytes 786464 | tf_op jit(solution)/shard_map/ppermute | solution.py:8
  185.9 1.6 collective-permute-start.7
  187.4 16.5 %collective-permute-done.7 = bf16[4,1,4,24576]{3,2,0,1:T(4,128)(2,1)S(1)} collective-permute-done((bf16[4,1,4,24576]{3,2,0,1:T(4,128)(2,1)S(1)}, bf16[4,1,4,24576]{3,2,0,1:T(4,128)(2,1)S(1)}, u32[]{:S(2)}, u32[]{:S(2)}) %collective-permute-start.7) | collective-permute-done | bytes 786464 | tf_op jit(solution)/shard_map/ppermute | solution.py:8
  205.8 1.6 copy.183
  208.2 1.5 collective-permute-start.8
  209.8 15.7 %collective-permute-done.8 = bf16[8,1,2,24576]{3,0,2,1:T(8,128)(2,1)S(1)} collective-permute-done((bf16[8,1,2,24576]{3,0,2,1:T(8,128)(2,1)S(1)}, bf16[8,1,2,24576]{3,0,2,1:T(8,128)(2,1)S(1)}, u32[]{:S(2)}, u32[]{:S(2)}) %collective-permute-start.8) | collective-permute-done | bytes 786464 | tf_op jit(solution)/shard_map/ppermute | solution.py:8
  225.7 1.6 copy.184
  227.3 3.7 %broadcast_select_fusion = (bf16[16,1,1,1,24576]{4,2,0,3,1:T(2,128)(2,1)S(1)}, bf16[16,1,1,1,24576]{4,2,0,3,1:T(2,128)(2,1)S(1)}) fusion(pred[]{:T(512)S(6)} %eq.20, bf16[16,1,2,1,24576]{4,2,0,3,1:T(2,128)(2,1)S(1)} %bitcast.319), kind=kLoop, calls=%fused_computation.6 | loop fusion | flops 786432 | bytes 3145729 | tf_op jit(solution)/shard_map/jit(_where)/select_n | solution.py:29
  232.2 2.2 collective-permute-done.9
  235.3 1.6 copy.185
  237.0 1.3 reshape_reshape.34
  239.1 2.3 reshape.698
  241.4 8.1 %fusion.5 = f32[32,4,3,2048]{3,0,2,1:T(8,128)S(1)} fusion(bf16[2048,2048]{1,0:T(8,128)(2,1)} %param.12, bf16[32,4,3,2048]{3,2,1,0:T(4,128)(2,1)} %reshape.698), kind=kOutput, calls=%fused_computation.4 | convolution fusion | flops 3221225472 | bytes 13107200 | tf_op jit(solution)/shard_map/dot_general | solution.py:79
  251.1 2.4 copy.188
  (79 shorter events, 19.0 us)
Async XLA Ops:
  9.2 38.5 %collective-permute-start = (bf16[1,32,16,768]{3,2,1,0:T(8,128)(2,1)S(1)}, bf16[1,32,16,768]{3,2,1,0:T(8,128)(2,1)S(1)}, u32[]{:S(2)}, u32[]{:S(2)}) collective-permute-start(bf16[1,32,16,768]{3,2,1,0:T(8,128)(2,1)S(1)} %fusion.28), channel_id=1, source_target_pairs={{0,16},{1,17},{2,18},{3,19},{4,20},{5,21},{6,22},{7,23},{8,24},{9,... | collective-permute-start | bytes 2359304 | tf_op jit(solution)/shard_map/ppermute | solution.py:8
  48.4 18.8 %collective-permute-start.1 = (bf16[2,32,8,768]{3,1,2,0:T(8,128)(2,1)S(1)}, bf16[2,32,8,768]{3,1,2,0:T(8,128)(2,1)S(1)}, u32[]{:S(2)}, u32[]{:S(2)}) collective-permute-start(bf16[2,32,8,768]{3,1,2,0:T(8,128)(2,1)S(1)} %select_bitcast_fusion.12), channel_id=1, source_target_pairs={{0,8},{1,9},{2,10},{3,11},{4,12},{5,13},{6,14},{7,15},{8,0},{9,1},... | collective-permute-start | bytes 2359304 | tf_op jit(solution)/shard_map/ppermute | solution.py:8
  67.5 17.9 %collective-permute-start.2 = (bf16[4,32,4,768]{3,1,2,0:T(8,128)(2,1)S(1)}, bf16[4,32,4,768]{3,1,2,0:T(8,128)(2,1)S(1)}, u32[]{:S(2)}, u32[]{:S(2)}) collective-permute-start(bf16[4,32,4,768]{3,1,2,0:T(8,128)(2,1)S(1)} %fusion.27), channel_id=1, source_target_pairs={{0,4},{1,5},{2,6},{3,7},{4,0},{5,1},{6,2},{7,3},{8,12},{9,13},{10,... | collective-permute-start | bytes 2359304 | tf_op jit(solution)/shard_map/ppermute | solution.py:8
  86.0 17.1 %collective-permute-start.3 = (bf16[8,32,2,768]{3,1,2,0:T(8,128)(2,1)S(1)}, bf16[8,32,2,768]{3,1,2,0:T(8,128)(2,1)S(1)}, u32[]{:S(2)}, u32[]{:S(2)}) collective-permute-start(bf16[8,32,2,768]{3,1,2,0:T(8,128)(2,1)S(1)} %fusion.26), channel_id=1, source_target_pairs={{0,2},{1,3},{2,0},{3,1},{4,6},{5,7},{6,4},{7,5},{8,10},{9,11},{10,... | collective-permute-start | bytes 2359304 | tf_op jit(solution)/shard_map/ppermute | solution.py:8
  103.5 0.7 copy-start.7
  103.6 6.9 %collective-permute-start.4 = (bf16[16,32,1,768]{3,1,0,2:T(8,128)(2,1)S(1)}, bf16[16,32,1,768]{3,1,0,2:T(8,128)(2,1)}, u32[]{:S(2)}, u32[]{:S(2)}) collective-permute-start(bf16[16,32,1,768]{3,1,0,2:T(8,128)(2,1)S(1)} %fusion.25), channel_id=1, source_target_pairs={{0,1},{1,0},{2,3},{3,2},{4,5},{5,4},{6,7},{7,6},{8,9},{9,8},{10,11... | collective-permute-start | bytes 2359304 | tf_op jit(solution)/shard_map/ppermute | solution.py:8
  108.0 1.2 slice-start
  112.2 1.2 copy-start.1
  125.2 39.8 %collective-permute-start.5 = (bf16[1,1,16,24576]{3,2,1,0:T(8,128)(2,1)S(1)}, bf16[1,1,16,24576]{3,2,1,0:T(8,128)(2,1)S(1)}, u32[]{:S(2)}, u32[]{:S(2)}) collective-permute-start(bf16[1,1,16,24576]{3,2,1,0:T(8,128)(2,1)S(1)} %select_bitcast_fusion.5), channel_id=1, source_target_pairs={{0,16},{1,17},{2,18},{3,19},{4,20},{5,21},{6,22},{7,23},{8,24},{9,... | collective-permute-start | bytes 2359304 | tf_op jit(solution)/shard_map/ppermute | solution.py:8
  165.3 18.9 %collective-permute-start.6 = (bf16[2,1,8,24576]{3,2,0,1:T(8,128)(2,1)S(1)}, bf16[2,1,8,24576]{3,2,0,1:T(8,128)(2,1)S(1)}, u32[]{:S(2)}, u32[]{:S(2)}) collective-permute-start(bf16[2,1,8,24576]{3,2,0,1:T(8,128)(2,1)S(1)} %fusion.24), channel_id=1, source_target_pairs={{0,8},{1,9},{2,10},{3,11},{4,12},{5,13},{6,14},{7,15},{8,0},{9,1},... | collective-permute-start | bytes 2359304 | tf_op jit(solution)/shard_map/ppermute | solution.py:8
  185.9 18.1 %collective-permute-start.7 = (bf16[4,1,4,24576]{3,2,0,1:T(4,128)(2,1)S(1)}, bf16[4,1,4,24576]{3,2,0,1:T(4,128)(2,1)S(1)}, u32[]{:S(2)}, u32[]{:S(2)}) collective-permute-start(bf16[4,1,4,24576]{3,2,0,1:T(4,128)(2,1)S(1)} %fusion.23), channel_id=1, source_target_pairs={{0,4},{1,5},{2,6},{3,7},{4,0},{5,1},{6,2},{7,3},{8,12},{9,13},{10,... | collective-permute-start | bytes 2359304 | tf_op jit(solution)/shard_map/ppermute | solution.py:8
  208.1 1.7 copy-start.5
  208.2 17.2 %collective-permute-start.8 = (bf16[8,1,2,24576]{3,0,2,1:T(8,128)(2,1)S(1)}, bf16[8,1,2,24576]{3,0,2,1:T(8,128)(2,1)S(1)}, u32[]{:S(2)}, u32[]{:S(2)}) collective-permute-start(bf16[8,1,2,24576]{3,0,2,1:T(8,128)(2,1)S(1)} %select_bitcast_fusion), channel_id=1, source_target_pairs={{0,2},{1,3},{2,0},{3,1},{4,6},{5,7},{6,4},{7,5},{8,10},{9,11},{10,... | collective-permute-start | bytes 2359304 | tf_op jit(solution)/shard_map/ppermute | solution.py:8
  231.1 1.0 copy-start.6
  231.1 1.0 copy-start.4
  232.0 2.4 collective-permute-start.9
  241.4 8.1 %copy-start.2 = (f32[32,3,2048]{2,0,1:T(8,128)S(1)}, f32[32,3,2048]{2,0,1:T(8,128)}, u32[]{:S(2)}) copy-start(f32[32,3,2048]{2,0,1:T(8,128)} %param.13) | copy-start | bytes 2359300
  249.5 0.7 copy-start.3
  250.0 0.9 copy-start
where the time goes:
time: 254 us; the launch traced here: 253 us
  waiting for transfers between devices  172 us (68%)
  local copies, waits for them, and re-layouts  34 us (13%)
  starting transfers between devices  16.6 us (7%)
  other arithmetic  13 us (5%)
  matrix products  12 us (5%)
  loops' own time  4.05 us (2%)
    ppermute x10, waiting for transfers between devices, from_partner(): lax.ppermute(value, axis, [(i, i ^ 1 << bit) for i in range(lax.axis_size...  172 us
    ppermute x10, starting transfers between devices, from_partner(): lax.ppermute(value, axis, [(i, i ^ 1 << bit) for i in range(lax.axis_size...  16.6 us
    unnamed x20, local copies, waits for them, and re-layouts  9.68 us
    dot_general x1, matrix products, body(): lax.dot_general(spanned, wall_filter, (((3,), (1,)), ((), ())), preferred...  8.12 us
    another operation x19, other arithmetic, butterfly(): jnp.stack([first, second], axis=1)  6.09 us
    another operation x3, local copies, waits for them, and re-layouts, butterfly(): halves = held.reshape(groups, inner_first, 2, targets // 2, inner_last)  5.62 us
    another operation x8, local copies, waits for them, and re-layouts, butterfly(): jnp.stack([first, second], axis=1)  5.58 us
  transfers between devices with their start and end apart: 10, of which 9 were waited for; matrix products, arithmetic and copies ran while one was open for 2% of the time, Pallas kernels for 0%

commit v1 on v0

v1 whole, which is shorter than its diff:
```python
import jax
import jax.numpy as jnp
from jax import lax
from jax.experimental import pallas as pl
from jax.experimental.pallas import tpu as pltpu
from jax.sharding import PartitionSpec as P

LANES = 128
VMEM = pl.BlockSpec(memory_space=pltpu.VMEM)
SMEM = pl.BlockSpec(memory_space=pltpu.SMEM)
HBM = pl.BlockSpec(memory_space=pltpu.HBM)


def team_size(count, rows, reach):
    for size in range(1, count + 1):
        if count % size == 0 and rows * size >= reach:
            return size
    return count


def shifted(value, team, by):
    count = lax.axis_size("span")
    return lax.ppermute(value, "span", [(i, (i + by * team) % count) for i in range(count)])


def crossed(value, team, x):
    count = lax.axis_size("span")
    return lax.ppermute(value, "span", [(i, (i // team ^ x) * team + i % team) for i in range(count)])


def within(value, team):
    count = lax.axis_size("span")
    teams = [[first + i for i in range(team)] for first in range(0, count, team)]
    return lax.all_to_all(value, "span", 0, 0, axis_index_groups=teams, tiled=True)


def behind(value, earlier):
    return lax.optimization_barrier((value, earlier))[0]


def kernel_call(body, inputs, outputs, in_specs=None, out_specs=None, scratch=(), flops=1e6, limit=16 << 20):
    moved = sum(a.size * a.dtype.itemsize for a in (*inputs, *outputs))
    return pl.pallas_call(
        body,
        in_specs=in_specs or [VMEM] * len(inputs),
        out_specs=out_specs or [VMEM] * len(outputs),
        out_shape=outputs,
        scratch_shapes=scratch,
        cost_estimate=pl.CostEstimate(flops=int(flops), bytes_accessed=moved, transcendentals=0),
        compiler_params=pltpu.CompilerParams(vmem_limit_bytes=limit),
    )(*inputs)


def band_kernel(taps_ref, band_ref):
    height, length = band_ref.shape
    spread = jnp.broadcast_to(taps_ref[...], (height, length))
    band_ref[...] = pltpu.roll(spread, 0, 1, stride=1, stride_axis=0).astype(jnp.bfloat16)


def band_of(taps, height, reach):
    lead = height - reach
    padded = jnp.pad(taps.astype(jnp.float32), (lead, 3 * height - lead - taps.shape[0]))
    shape = jax.ShapeDtypeStruct((height, 3 * height), jnp.bfloat16)
    return kernel_call(band_kernel, [padded[None]], [shape])[0]


def turned(slabs_ref, turned_ref, put):
    rows, parts, planes, width = slabs_ref.shape
    for part in range(parts):
        for column in range(width // LANES):
            at = slice(column * LANES, (column + 1) * LANES)
            held = turned_ref.at[(part * (width // LANES) + column) % turned_ref.shape[0]]
            for row in range(rows):
                held[pl.ds(row, planes, stride=rows), :] = slabs_ref[row, part, :, at].astype(jnp.float32)
            put(part, column, lambda plane: held[plane * rows : (plane + 1) * rows, :].astype(jnp.bfloat16))


def near_pack_kernel(early, slabs_ref, near_ref, turned_ref):
    parts = slabs_ref.shape[1]
    strip = near_ref.shape[3]

    def put(part, column, value):
        team, inner = divmod(column * LANES, strip)
        for plane in range(early):
            near_ref[team, plane * parts + part, :, inner : inner + LANES] = value(plane)

    turned(slabs_ref, turned_ref, put)


def far_pack_kernel(early, group_ref, slabs_ref, far_ref, turned_ref):
    planes, width = slabs_ref.shape[2:]
    slots = width // far_ref.shape[0] // LANES
    me = group_ref[0]

    def put(part, column, value):
        group, slot = divmod(column, slots)
        for plane in range(early, planes):
            far_ref[me ^ group, (plane - early) * slots + slot, part] = value(plane)

    turned(slabs_ref, turned_ref, put)


def banded(band_ref, blocks):
    height = band_ref.shape[0]
    total = None
    for i, block in enumerate(blocks):
        block = block.reshape(height, block.shape[-1])
        part = jnp.dot(band_ref[:, i * height : (i + 1) * height], block, preferred_element_type=jnp.float32)
        total = part if total is None else total + part
    return total


def near_kernel(band_ref, before_ref, after_ref, own_ref, out_ref):
    for u in range(own_ref.shape[1]):
        total = banded(band_ref, [before_ref[:, u], own_ref[:, u], after_ref[:, u]])
        out_ref[:, u] = total.astype(out_ref.dtype).reshape(out_ref[:, u].shape)


def far_kernel(group_ref, band_ref, held_ref, sent_ref, out_ref, sems):
    groups, units = held_ref.shape[1:3]
    copies = []
    me = group_ref[0]
    height = band_ref.shape[0]
    for q in range(groups):
        blocks = []
        for i in range(3):
            slot = me ^ ((q + i - 1) % groups)
            wide = [held_ref[:, slot, u].reshape(height, LANES) for u in range(units)]
            blocks.append(jnp.concatenate(wide, axis=1))
        total = banded(band_ref, blocks).astype(out_ref.dtype)
        for u in range(units):
            out_ref[:, me ^ q, u] = total[:, u * LANES : (u + 1) * LANES].reshape(out_ref.shape[0], -1, LANES)
        copies.append(pltpu.make_async_copy(out_ref.at[:, me ^ q], sent_ref.at[:, me ^ q], sems.at[q]))
        copies[-1].start()
    for copy in copies:
        copy.wait()


def contract(rows, wall):
    return lax.dot_general(rows, wall, (((1,), (1,)), ((), ())), preferred_element_type=jnp.float32)


def advance(state, fresh, at, scale_ref, mean_ref, diag_ref, off_ref):
    def line(ref, i):
        return ref[i : i + 1, at]

    for i in range(len(state)):
        scale = line(scale_ref, i)
        decay = jnp.exp(-jnp.pi / (2.0 * scale))
        inject = jnp.sqrt(1.0 - jnp.exp(-jnp.pi / scale))
        state[i] = decay * state[i] + inject * fresh[i]
    along, normal, spanwise = state
    first = line(mean_ref, 0) + line(diag_ref, 0) * along
    second = line(off_ref, 0) * along + line(diag_ref, 1) * normal
    third = line(off_ref, 1) * along + line(off_ref, 2) * normal + line(diag_ref, 2) * spanwise
    return state, (first, second, third)


def near_wall_kernel(
    planes, near_ref, wall_ref, state_ref, scale_ref, mean_ref, diag_ref, off_ref, velocity_ref, next_ref, held_ref, sems
):
    team, units, rows, strip = near_ref.shape
    parts = state_ref.shape[0]
    width = wall_ref.shape[0]
    block = 2 * LANES
    copies = []
    for step, start in enumerate(range(0, width, block)):
        at = pl.ds(start, block)
        copies.append(pltpu.make_async_copy(wall_ref.at[at], held_ref.at[at], sems.at[step]))
        copies[-1].start()
    for step, start in enumerate(range(0, width, block)):
        at = slice(start, start + block)
        total = None
        copies[step].wait()
        for i in range(team):
            part = contract(near_ref[i].reshape(units * rows, strip), held_ref[at, i * strip : (i + 1) * strip])
            total = part if total is None else total + part
        state = [state_ref[i, :, at] for i in range(parts)]
        for plane in range(planes):
            fresh = [total[(plane * parts + i) * rows :][:rows] for i in range(parts)]
            state, speeds = advance(state, fresh, at, scale_ref, mean_ref, diag_ref, off_ref)
            for i in range(parts):
                velocity_ref[i, plane * rows : (plane + 1) * rows, at] = speeds[i]
        for i in range(parts):
            next_ref[i, :, at] = state[i]


def far_wall_kernel(
    late, group_ref, *refs
):
    groups = len(refs) - 13
    far_refs = refs[:groups]
    wall_ref, state_ref, early_ref, scale_ref, mean_ref, diag_ref, off_ref = refs[groups : groups + 7]
    velocity_ref, last_ref, turned_ref, speed_ref, final_ref, sems = refs[groups + 7 :]
    parts, rows, width = state_ref.shape
    planes = velocity_ref.shape[2]
    early = planes - late
    slots = far_refs[0].shape[0] // late
    me = group_ref[0]
    block = 2 * LANES
    copies = []
    for step, start in enumerate(range(0, width, block)):
        at = slice(start, start + block)
        total = None
        for k in range(groups):
            for slot in range(0, slots, 2):
                pair = [
                    jnp.concatenate([far_refs[k][p * slots + slot + i].reshape(parts * rows, LANES) for i in range(2)], axis=1)
                    for p in range(late)
                ]
                where = pl.multiple_of((me ^ k) * (slots * LANES) + slot * LANES, 2 * LANES)
                part = contract(jnp.concatenate(pair, axis=0), wall_ref[at, pl.ds(where, 2 * LANES)])
                total = part if total is None else total + part
        state = [state_ref[i, :, at] for i in range(parts)]
        for plane in range(late):
            fresh = [total[(plane * parts + i) * rows :][:rows] for i in range(parts)]
            state, speeds = advance(state, fresh, at, scale_ref, mean_ref, diag_ref, off_ref)
            for i in range(parts):
                for j in range(2):
                    lanes = slice(j * LANES, (j + 1) * LANES)
                    turned_ref[step % 2, i, j, (early + plane) * rows : (early + plane + 1) * rows, :] = speeds[i][:, lanes]
        for i in range(parts):
            final_ref[i, :, at] = state[i]
            for j in range(2):
                lanes = slice(start + j * LANES, start + (j + 1) * LANES)
                turned_ref[step % 2, i, j, : early * rows, :] = early_ref[i, :, lanes]
                for row in range(rows):
                    column = turned_ref[step % 2, i, j, pl.ds(row, planes, stride=rows), :]
                    speed_ref[row, i, :, lanes] = column.astype(speed_ref.dtype)
        here = pltpu.make_async_copy(speed_ref.at[:, :, :, at], velocity_ref.at[:, :, :, at], sems.at[0, step])
        here.start()
        also = pltpu.make_async_copy(final_ref.at[:, :, at], last_ref.at[:, :, at], sems.at[1, step])
        also.start()
        copies += [here, also]
    for copy in copies:
        copy.wait()


def plain(slabs, band, wall_filter, prev_state, time_scale, mean_velocity, lund_diag, lund_off):
    rows, planes, parts, width = slabs.shape
    height = band.shape[0]
    team = height // rows
    strip = width // team
    near = slabs.reshape(rows, planes, parts, team, strip).transpose(3, 1, 2, 0, 4)
    near = within(near.reshape(team, planes * parts, rows, strip), team)
    after = shifted(near, team, -1)
    before = shifted(near, team, 1)
    shape = jax.ShapeDtypeStruct(near.shape, near.dtype)
    near = kernel_call(near_kernel, [band, before, after, near], [shape], limit=32 << 20)[0]
    near = within(near, team).reshape(team, planes, parts, rows, strip)
    near = near.transpose(1, 2, 3, 0, 4).reshape(planes, parts, rows, width)
    filtered = lax.dot_general(near, wall_filter, (((3,), (1,)), ((), ())), preferred_element_type=jnp.float32)
    decay = jnp.exp(-jnp.pi / (2.0 * time_scale))[:, None]
    inject = jnp.sqrt(1.0 - jnp.exp(-jnp.pi / time_scale))[:, None]
    state = prev_state.transpose(1, 0, 2)
    outputs = []
    for plane in range(planes):
        state = decay * state + inject * filtered[plane]
        first = mean_velocity + lund_diag[0] * state[0]
        second = lund_off[0] * state[0] + lund_diag[1] * state[1]
        third = lund_off[1] * state[0] + lund_off[2] * state[1] + lund_diag[2] * state[2]
        outputs.append(jnp.stack([first, second, third]).astype(jnp.bfloat16))
    return (jnp.stack(outputs).transpose(2, 0, 1, 3), state.transpose(1, 0, 2))


def body(
    random_slabs,
    span_weights,
    wall_filter,
    prev_state,
    time_scale,
    mean_velocity,
    lund_diag,
    lund_off,
):
    rows, planes, parts, width = random_slabs.shape
    reach = (span_weights.shape[0] - 1) // 2
    count = lax.axis_size("span")
    team = team_size(count, rows, reach)
    groups = count // team
    height = rows * team
    scaling = jnp.sqrt(jnp.sum(span_weights * span_weights))
    taps = (span_weights / scaling).astype(jnp.bfloat16)
    band = band_of(taps, height, reach)
    group = (lax.axis_index("span") // team).astype(jnp.int32)[None]

    late = planes // 2
    if width != groups * (team // late) * LANES or groups > 4:
        return plain(random_slabs, band, wall_filter, prev_state, time_scale, mean_velocity, lund_diag, lund_off)
    early = planes - late
    strip = width // team
    units = early * parts
    slabs = random_slabs.transpose(0, 2, 1, 3)
    state = prev_state.transpose(1, 0, 2)
    lines = [time_scale, mean_velocity[None], lund_diag, lund_off]
    shape = jax.ShapeDtypeStruct

    turning = [pltpu.VMEM((4, planes * rows, LANES), jnp.float32)]
    far = kernel_call(
        lambda *refs: far_pack_kernel(early, *refs),
        [group, slabs],
        [shape((groups, team, parts, rows, LANES), slabs.dtype)],
        in_specs=[SMEM, VMEM],
        scratch=turning,
    )[0]
    near = kernel_call(
        lambda *refs: near_pack_kernel(early, *refs),
        [slabs],
        [shape((team, units, rows, strip), slabs.dtype)],
        scratch=turning,
    )[0]
    near = within(near, team)
    after = shifted(near, team, -1)
    before = shifted(near, team, 1)
    far = [far[0]] + [crossed(far[x], team, x) for x in range(1, groups)]
    far = within(behind(jnp.stack(far, axis=1), near), team)
    far = kernel_call(
        far_kernel,
        [group, band, far],
        [shape(far.shape, far.dtype)],
        in_specs=[SMEM, VMEM, VMEM],
        out_specs=[HBM],
        scratch=[pltpu.VMEM(far.shape, far.dtype), pltpu.SemaphoreType.DMA((groups,))],
        flops=2 * band.size * far.size // height,
    )[0]
    far = within(far, team)
    near = kernel_call(
        near_kernel,
        [band, before, after, near],
        [shape(near.shape, near.dtype)],
        flops=2 * band.size * near.size // height,
    )[0]
    near = within(behind(near, far), team)
    far = [far[:, 0]] + [crossed(far[:, x], team, x) for x in range(1, groups)]
    speeds, state, wall = kernel_call(
        lambda *refs: near_wall_kernel(early, *refs),
        [near, wall_filter, state, *lines],
        [
            shape((parts, early * rows, width), jnp.float32),
            shape(state.shape, state.dtype),
            shape(wall_filter.shape, wall_filter.dtype),
        ],
        in_specs=[VMEM, HBM] + [VMEM] * 5,
        scratch=[pltpu.SemaphoreType.DMA((width // (2 * LANES),))],
        flops=2 * wall_filter.size * units * rows,
        limit=42 << 20,
    )
    velocity, state = kernel_call(
        lambda *refs: far_wall_kernel(late, *refs),
        [group, *far, wall, state, speeds, *lines],
        [shape(slabs.shape, slabs.dtype), shape(state.shape, state.dtype)],
        in_specs=[SMEM] + [VMEM] * (groups + 7),
        out_specs=[HBM, HBM],
        scratch=[
            pltpu.VMEM((2, parts, 2, planes * rows, LANES), jnp.float32),
            pltpu.VMEM(slabs.shape, slabs.dtype),
            pltpu.VMEM(state.shape, state.dtype),
            pltpu.SemaphoreType.DMA((2, width // (2 * LANES))),
        ],
        flops=2 * wall_filter.size * late * parts * rows,
        limit=24 << 20,
    )
    return (velocity.transpose(0, 2, 1, 3), state.transpose(1, 0, 2))


def solution(mesh):
    placed = (P("span", None, None, None), P(), P(), P("span", None, None), P(), P(), P(), P())
    return jax.shard_map(
        body,
        mesh=mesh,
        in_specs=placed,
        out_specs=(P("span", None, None, None), P("span", None, None)),
        check_vma=False,
    )
```

time: 254 us -> 112 us (0.44)
  waiting for transfers between devices: 172 us -> 54.8 us
  local copies, waits for them, and re-layouts: 34 us -> 2.32 us
  Pallas kernels: 0 us -> 22.8 us
  matrix products: 12 us -> 0 us
  starting transfers between devices: 16.6 us -> 28.3 us
  other arithmetic: 13 us -> 1.59 us
  loops' own time: 4.05 us -> 0 us
    ppermute x10 -> x8, waiting for transfers between devices: 172 us -> 38.8 us  [the longest x2 19.8 us: shifted(): lax.ppermute(value, 'span', [(i, (i + by * team) % count) for i in range(...]
    pallas_call x0 -> x7, Pallas kernels: none -> 22.8 us  [kernel_call(): pl.pallas_call(body, in_specs=in_specs or [VMEM] * len(inputs), out_specs...]
    all_to_all x0 -> x4, starting transfers between devices: none -> 17 us  [within(): lax.all_to_all(value, 'span', 0, 0, axis_index_groups=teams, tiled=True)]
    all_to_all x0 -> x4, waiting for transfers between devices: none -> 16 us  [within(): lax.all_to_all(value, 'span', 0, 0, axis_index_groups=teams, tiled=True)]
    another operation x14 -> x1, local copies, waits for them, and re-layouts: 14.8 us -> 0.07 us  [body(): far = within(behind(jnp.stack(far, axis=1), near), team)]
    dot_general x3 -> x0, matrix products: 12 us -> none  [the longest x1 8.12 us: body(): lax.dot_general(spanned, wall_filter, (((3,), (1,)), ((), ())), preferred...]
    unnamed x20 -> x16, local copies, waits for them, and re-layouts: 9.68 us -> 1.43 us
    another operation x22 -> x1, other arithmetic: 6.79 us -> 0.98 us  [body(): far = within(behind(jnp.stack(far, axis=1), near), team)]
  transfers between devices with their start and end apart: 10 -> 12, of which waited for: 9 -> 7; matrix products, arithmetic and copies ran while one was open for 2% -> 2% of each run, Pallas kernels for 0% -> 12%
where the time goes in v1:
time: 112 us; the launch traced here: 111 us
  waiting for transfers between devices  54.8 us (49%)
  starting transfers between devices  28.3 us (25%)
  Pallas kernels  22.8 us (20%)
  local copies, waits for them, and re-layouts  2.32 us (2%)
  between operations  1.62 us (1%)
  other arithmetic  1.59 us (1%)
    pallas_call x7, Pallas kernels, kernel_call(): pl.pallas_call(body, in_specs=in_specs or [VMEM] * len(inputs), out_specs...  22.8 us
    ppermute x2, waiting for transfers between devices, shifted(): lax.ppermute(value, 'span', [(i, (i + by * team) % count) for i in range(...  19.8 us
    ppermute x6, waiting for transfers between devices, crossed(): lax.ppermute(value, 'span', [(i, (i // team ^ x) * team + i % team) for i...  19 us
    all_to_all x4, starting transfers between devices, within(): lax.all_to_all(value, 'span', 0, 0, axis_index_groups=teams, tiled=True)  17 us
    all_to_all x4, waiting for transfers between devices, within(): lax.all_to_all(value, 'span', 0, 0, axis_index_groups=teams, tiled=True)  16 us
    ppermute x6, starting transfers between devices, crossed(): lax.ppermute(value, 'span', [(i, (i // team ^ x) * team + i % team) for i...  8.84 us
    ppermute x2, starting transfers between devices, shifted(): lax.ppermute(value, 'span', [(i, (i + by * team) % count) for i in range(...  2.53 us
  transfers between devices with their start and end apart: 12, of which 7 were waited for; matrix products, arithmetic and copies ran while one was open for 2% of the time, Pallas kernels for 12%

profile of v1, /device:TPU:0, one launch (start us, length us, event | category | flops | bytes accessed | tf_op | source)
XLA Modules:
  0.0 111.5 jit_solution(15760361813162402682)
XLA Ops:
  0.6 1.4 %copy-done = bf16[32,4,3,2048]{3,1,2,0:T(4,128)(2,1)S(1)} copy-done((bf16[32,4,3,2048]{3,1,2,0:T(4,128)(2,1)S(1)}, bf16[32,4,3,2048]{3,1,2,0:T(4,128)(2,1)}, u32[]{:S(2)}) %copy-start) | copy-done | bytes 1572888
  2.0 2.3 %shard_map.97 = bf16[8,6,32,256]{3,2,1,0:T(8,128)(2,1)} custom-call(bf16[32,3,4,2048]{3,2,1,0:T(4,128)(2,1)S(1)} %bitcast.33), custom_call_target="tpu_custom_call" | custom-call | flops 1000000 | bytes 2359296 | tf_op jit(solution)/shard_map/pallas_call | solution.py:43
  4.4 5.2 %all-to-all-start = ((bf16[8,6,32,256]{3,2,1,0:T(8,128)(2,1)}), bf16[8,6,32,256]{3,2,1,0:T(8,128)(2,1)S(1)}, u32[]{:S(2)}, u32[]{:S(2)}) async-start(bf16[8,6,32,256]{3,2,1,0:T(8,128)(2,1)} %shard_map.97), calls=%async_computation | async-start | bytes 1572864 | tf_op jit(solution)/shard_map/all_to_all | solution.py:34
  9.6 1.4 %shard_map.96 = bf16[4,8,3,32,128]{4,3,2,1,0:T(8,128)(2,1)S(1)} custom-call(s32[1]{0:T(128)} %bitcast.refs_0_.group_ref, bf16[32,3,4,2048]{3,2,1,0:T(4,128)(2,1)S(1)} %bitcast.34), custom_call_target="tpu_custom_call" | custom-call | flops 1000000 | bytes 2359300 | tf_op jit(solution)/shard_map/pallas_call | solution.py:43
  11.0 0.1 slice_bitcast_fusion.7
  11.0 3.7 %collective-permute-start.2 = (bf16[8,3,32,128]{3,2,1,0:T(8,128)(2,1)S(1)}, bf16[8,3,32,128]{3,2,1,0:T(8,128)(2,1)S(1)}, u32[]{:S(2)}, u32[]{:S(2)}) collective-permute-start(bf16[8,3,32,128]{3,2,1,0:T(8,128)(2,1)S(1)} %get-tuple-element.21), channel_id=1, source_target_pairs={{0,24},{1,25},{2,26},{3,27},{4,28},{5,29},{6,30},{7,31},{8,16},{9,... | collective-permute-start | bytes 589832 | tf_op jit(solution)/shard_map/ppermute | solution.py:28
  14.7 0.8 collective-permute-start
  15.5 5.3 %collective-permute-done.2 = bf16[8,3,32,128]{3,2,1,0:T(8,128)(2,1)S(1)} collective-permute-done((bf16[8,3,32,128]{3,2,1,0:T(8,128)(2,1)S(1)}, bf16[8,3,32,128]{3,2,1,0:T(8,128)(2,1)S(1)}, u32[]{:S(2)}, u32[]{:S(2)}) %collective-permute-start.2) | collective-permute-done | bytes 196640 | tf_op jit(solution)/shard_map/ppermute | solution.py:28
  20.8 11.2 %collective-permute-done.1 = bf16[8,3,32,128]{3,2,1,0:T(8,128)(2,1)S(1)} collective-permute-done((bf16[8,3,32,128]{3,2,1,0:T(8,128)(2,1)S(1)}, bf16[8,3,32,128]{3,2,1,0:T(8,128)(2,1)S(1)}, u32[]{:S(2)}, u32[]{:S(2)}) %collective-permute-start.1) | collective-permute-done | bytes 196640 | tf_op jit(solution)/shard_map/ppermute | solution.py:28
  32.1 1.0 pad_maximum_fusion
  33.1 4.2 %all-to-all-start.1 = ((bf16[8,4,3,32,128]{4,3,2,1,0:T(8,128)(2,1)}), bf16[8,4,3,32,128]{4,3,2,1,0:T(8,128)(2,1)}, u32[]{:S(2)}, u32[]{:S(2)}) async-start(bf16[8,4,3,32,128]{4,3,2,1,0:T(8,128)(2,1)} %pad_maximum_fusion), calls=%async_computation.1 | async-start | bytes 1572864 | tf_op jit(solution)/shard_map/all_to_all | solution.py:34
  37.3 0.6 multiply_reduce_fusion
  38.6 2.5 %collective-permute-start.7 = (bf16[8,6,32,256]{3,2,1,0:T(8,128)(2,1)S(1)}, bf16[8,6,32,256]{3,2,1,0:T(8,128)(2,1)S(1)}, u32[]{:S(2)}, u32[]{:S(2)}) collective-permute-start(bf16[8,6,32,256]{3,2,1,0:T(8,128)(2,1)S(1)} %all-to-all-done.own_ref), channel_id=1, source_target_pairs={{0,24},{1,25},{2,26},{3,27},{4,28},{5,29},{6,30},{7,31},{8,0},{9,1... | collective-permute-start | bytes 2359304 | tf_op jit(solution)/shard_map/ppermute | solution.py:23
  41.1 0.1 shard_map.95.band_ref
  41.3 8.6 %all-to-all-done.1.held_ref = bf16[8,4,3,32,128]{4,3,2,1,0:T(8,128)(2,1)} async-done(((bf16[8,4,3,32,128]{4,3,2,1,0:T(8,128)(2,1)}), bf16[8,4,3,32,128]{4,3,2,1,0:T(8,128)(2,1)}, u32[]{:S(2)}, u32[]{:S(2)}) %all-to-all-start.1) | async-done | bytes 786464 | tf_op jit(solution)/shard_map/all_to_all | solution.py:34
  49.9 2.8 %shard_map.98 = bf16[8,4,3,32,128]{4,3,2,1,0:T(8,128)(2,1)} custom-call(s32[1]{0:T(128)} %bitcast.refs_0_.group_ref, bf16[256,768]{1,0:T(8,128)(2,1)S(1)} %shard_map.95.band_ref, bf16[8,4,3,32,128]{4,3,2,1,0:T(8,128)(2,1)} %all-to-all-done.1.held_ref), custom_call_target="tpu_custom_call" | custom-call | flops 603979776 | bytes 1966084 | tf_op jit(solution)/shard_map/pallas_call | solution.py:43
  52.7 3.6 %all-to-all-start.2 = ((bf16[8,4,3,32,128]{4,3,2,1,0:T(8,128)(2,1)}), bf16[8,4,3,32,128]{4,3,2,1,0:T(8,128)(2,1)S(1)}, u32[]{:S(2)}, u32[]{:S(2)}) async-start(bf16[8,4,3,32,128]{4,3,2,1,0:T(8,128)(2,1)} %shard_map.98), calls=%async_computation.2 | async-start | bytes 1572864 | tf_op jit(solution)/shard_map/all_to_all | solution.py:34
  56.3 2.8 %collective-permute-done.7.after_ref = bf16[8,6,32,256]{3,2,1,0:T(8,128)(2,1)S(1)} collective-permute-done((bf16[8,6,32,256]{3,2,1,0:T(8,128)(2,1)S(1)}, bf16[8,6,32,256]{3,2,1,0:T(8,128)(2,1)S(1)}, u32[]{:S(2)}, u32[]{:S(2)}) %collective-permute-start.7) | collective-permute-done | bytes 786464 | tf_op jit(solution)/shard_map/ppermute | solution.py:23
  59.1 17.0 %collective-permute-done.6.before_ref = bf16[8,6,32,256]{3,2,1,0:T(8,128)(2,1)S(1)} collective-permute-done((bf16[8,6,32,256]{3,2,1,0:T(8,128)(2,1)S(1)}, bf16[8,6,32,256]{3,2,1,0:T(8,128)(2,1)S(1)}, u32[]{:S(2)}, u32[]{:S(2)}) %collective-permute-start.6) | collective-permute-done | bytes 786464 | tf_op jit(solution)/shard_map/ppermute | solution.py:23
  76.1 1.7 %shard_map.99 = bf16[8,6,32,256]{3,2,1,0:T(8,128)(2,1)} custom-call(bf16[256,768]{1,0:T(8,128)(2,1)S(1)} %shard_map.95.band_ref, bf16[8,6,32,256]{3,2,1,0:T(8,128)(2,1)S(1)} %collective-permute-done.6.before_ref, bf16[8,6,32,256]{3,2,1,0:T(8,128)(2,1)S(1)} %collective-permute-done.7.after_ref, bf16[8,6,32,256]{3,2,1,0:T(8,128)(2,1)S(1)} %all-to-all-done.own_ref), custom_call_target="tpu_custom_call" | custom-call | flops 603979776 | bytes 3538944 | tf_op jit(solution)/shard_map/pallas_call | solution.py:43
  77.7 0.0 copy-start.6
  77.7 4.0 %all-to-all-start.3 = ((bf16[8,6,32,256]{3,2,1,0:T(8,128)(2,1)}), bf16[8,6,32,256]{3,2,1,0:T(8,128)(2,1)S(1)}, u32[]{:S(2)}, u32[]{:S(2)}) async-start(bf16[8,6,32,256]{3,2,1,0:T(8,128)(2,1)} %shard_map.99), calls=%async_computation.3 | async-start | bytes 1572864 | tf_op jit(solution)/shard_map/all_to_all | solution.py:34
  81.7 0.8 slice_bitcast_fusion
  82.6 1.8 %collective-permute-start.5 = (bf16[8,3,32,128]{3,2,1,0:T(8,128)(2,1)}, bf16[8,3,32,128]{3,2,1,0:T(8,128)(2,1)S(1)}, u32[]{:S(2)}, u32[]{:S(2)}) collective-permute-start(bf16[8,3,32,128]{3,2,1,0:T(8,128)(2,1)} %get-tuple-element.16), channel_id=1, source_target_pairs={{0,24},{1,25},{2,26},{3,27},{4,28},{5,29},{6,30},{7,31},{8,16},{9,... | collective-permute-start | bytes 589832 | tf_op jit(solution)/shard_map/ppermute | solution.py:28
  84.4 1.4 %collective-permute-start.4 = (bf16[8,3,32,128]{3,2,1,0:T(8,128)(2,1)}, bf16[8,3,32,128]{3,2,1,0:T(8,128)(2,1)S(1)}, u32[]{:S(2)}, u32[]{:S(2)}) collective-permute-start(bf16[8,3,32,128]{3,2,1,0:T(8,128)(2,1)} %get-tuple-element.17), channel_id=1, source_target_pairs={{0,16},{1,17},{2,18},{3,19},{4,20},{5,21},{6,22},{7,23},{8,24},{9,... | collective-permute-start | bytes 589832 | tf_op jit(solution)/shard_map/ppermute | solution.py:28
  85.8 1.1 %collective-permute-start.3 = (bf16[8,3,32,128]{3,2,1,0:T(8,128)(2,1)S(1)}, bf16[8,3,32,128]{3,2,1,0:T(8,128)(2,1)S(1)}, u32[]{:S(2)}, u32[]{:S(2)}) collective-permute-start(bf16[8,3,32,128]{3,2,1,0:T(8,128)(2,1)S(1)} %get-tuple-element.18), channel_id=1, source_target_pairs={{0,8},{1,9},{2,10},{3,11},{4,12},{5,13},{6,14},{7,15},{8,0},{9,1},... | collective-permute-start | bytes 589832 | tf_op jit(solution)/shard_map/ppermute | solution.py:28
  86.9 7.4 %all-to-all-done.3.refs_0_ = bf16[8,6,32,256]{3,2,1,0:T(8,128)(2,1)S(1)} async-done(((bf16[8,6,32,256]{3,2,1,0:T(8,128)(2,1)}), bf16[8,6,32,256]{3,2,1,0:T(8,128)(2,1)S(1)}, u32[]{:S(2)}, u32[]{:S(2)}) %all-to-all-start.3) | async-done | bytes 786464 | tf_op jit(solution)/shard_map/all_to_all | solution.py:34
  94.3 7.1 %shard_map.100 = (f32[3,64,2048]{2,1,0:T(8,128)S(1)}, f32[3,32,2048]{2,1,0:T(8,128)S(1)}, bf16[2048,2048]{1,0:T(8,128)(2,1)S(1)}) custom-call(bf16[8,6,32,256]{3,2,1,0:T(8,128)(2,1)S(1)} %all-to-all-done.3.refs_0_, bf16[2048,2048]{1,0:T(8,128)(2,1)} %refs_1_.1, f32[3,32,2048]{2,1,0:T(8,128)S(1)} %bitcast.35, f32[3,2048]{1,0:T(4,128)S(1)} %copy-done.3, ...), custom_call_target="tpu_custom_call" | custom-call | flops 1610612736 | bytes 20791296 | tf_op jit(solution)/shard_map/pallas_call | solution.py:43
  101.5 0.0 collective-permute-done.5.refs_4_
  101.5 2.5 %collective-permute-done.4.refs_3_ = bf16[8,3,32,128]{3,2,1,0:T(8,128)(2,1)S(1)} collective-permute-done((bf16[8,3,32,128]{3,2,1,0:T(8,128)(2,1)}, bf16[8,3,32,128]{3,2,1,0:T(8,128)(2,1)S(1)}, u32[]{:S(2)}, u32[]{:S(2)}) %collective-permute-start.4) | collective-permute-done | bytes 196640 | tf_op jit(solution)/shard_map/ppermute | solution.py:28
  103.9 0.0 collective-permute-done.3.refs_2_
  103.9 7.4 %shard_map.101 = (bf16[32,3,4,2048]{3,2,1,0:T(4,128)(2,1)}, f32[3,32,2048]{2,1,0:T(8,128)}) custom-call(s32[1]{0:T(128)} %bitcast.refs_0_.group_ref, bf16[8,3,32,128]{3,2,1,0:T(8,128)(2,1)S(1)} %get-tuple-element.19.refs_1_, bf16[8,3,32,128]{3,2,1,0:T(8,128)(2,1)S(1)} %collective-permute-done.3.refs_2_, ...), custom_call_target="tpu_custom_call" | custom-call | flops 1610612736 | bytes 13975556 | tf_op jit(solution)/shard_map/pallas_call | solution.py:43
  (22 shorter events, 0.1 us)
Async XLA Ops:
  0.6 1.4 %copy-start = (bf16[32,4,3,2048]{3,1,2,0:T(4,128)(2,1)S(1)}, bf16[32,4,3,2048]{3,1,2,0:T(4,128)(2,1)}, u32[]{:S(2)}) copy-start(bf16[32,4,3,2048]{3,1,2,0:T(4,128)(2,1)} %param.8) | copy-start | bytes 4718596
  2.0 7.5 %copy-start.1 = (bf16[32,4,3,2048]{3,1,2,0:T(4,128)(2,1)S(1)}, bf16[32,4,3,2048]{3,1,2,0:T(4,128)(2,1)}, u32[]{:S(2)}) copy-start(bf16[32,4,3,2048]{3,1,2,0:T(4,128)(2,1)} %param.8) | copy-start | bytes 4718596
  4.4 28.7 %all-to-all-start = ((bf16[8,6,32,256]{3,2,1,0:T(8,128)(2,1)}), bf16[8,6,32,256]{3,2,1,0:T(8,128)(2,1)S(1)}, u32[]{:S(2)}, u32[]{:S(2)}) async-start(bf16[8,6,32,256]{3,2,1,0:T(8,128)(2,1)} %shard_map.97), calls=%async_computation | async-start | bytes 1572864 | tf_op jit(solution)/shard_map/all_to_all | solution.py:34
  11.0 9.8 %collective-permute-start.2 = (bf16[8,3,32,128]{3,2,1,0:T(8,128)(2,1)S(1)}, bf16[8,3,32,128]{3,2,1,0:T(8,128)(2,1)S(1)}, u32[]{:S(2)}, u32[]{:S(2)}) collective-permute-start(bf16[8,3,32,128]{3,2,1,0:T(8,128)(2,1)S(1)} %get-tuple-element.21), channel_id=1, source_target_pairs={{0,24},{1,25},{2,26},{3,27},{4,28},{5,29},{6,30},{7,31},{8,16},{9,... | collective-permute-start | bytes 589832 | tf_op jit(solution)/shard_map/ppermute | solution.py:28
  14.7 17.4 %collective-permute-start.1 = (bf16[8,3,32,128]{3,2,1,0:T(8,128)(2,1)S(1)}, bf16[8,3,32,128]{3,2,1,0:T(8,128)(2,1)S(1)}, u32[]{:S(2)}, u32[]{:S(2)}) collective-permute-start(bf16[8,3,32,128]{3,2,1,0:T(8,128)(2,1)S(1)} %get-tuple-element.22), channel_id=1, source_target_pairs={{0,16},{1,17},{2,18},{3,19},{4,20},{5,21},{6,22},{7,23},{8,24},{9,... | collective-permute-start | bytes 589832 | tf_op jit(solution)/shard_map/ppermute | solution.py:28
  14.7 17.4 %collective-permute-start = (bf16[8,3,32,128]{3,2,1,0:T(8,128)(2,1)S(1)}, bf16[8,3,32,128]{3,2,1,0:T(8,128)(2,1)S(1)}, u32[]{:S(2)}, u32[]{:S(2)}) collective-permute-start(bf16[8,3,32,128]{3,2,1,0:T(8,128)(2,1)S(1)} %get-tuple-element.23), channel_id=1, source_target_pairs={{0,8},{1,9},{2,10},{3,11},{4,12},{5,13},{6,14},{7,15},{8,0},{9,1},... | collective-permute-start | bytes 589832 | tf_op jit(solution)/shard_map/ppermute | solution.py:28
  32.1 5.2 %copy-start.7 = (f32[513]{0:T(1024)S(1)}, f32[513]{0:T(1024)}, u32[]{:S(2)}) copy-start(f32[513]{0:T(1024)} %param.9) | copy-start | bytes 6160
  33.1 16.8 %all-to-all-start.1 = ((bf16[8,4,3,32,128]{4,3,2,1,0:T(8,128)(2,1)}), bf16[8,4,3,32,128]{4,3,2,1,0:T(8,128)(2,1)}, u32[]{:S(2)}, u32[]{:S(2)}) async-start(bf16[8,4,3,32,128]{4,3,2,1,0:T(8,128)(2,1)} %pad_maximum_fusion), calls=%async_computation.1 | async-start | bytes 1572864 | tf_op jit(solution)/shard_map/all_to_all | solution.py:34
  38.6 20.5 %collective-permute-start.7 = (bf16[8,6,32,256]{3,2,1,0:T(8,128)(2,1)S(1)}, bf16[8,6,32,256]{3,2,1,0:T(8,128)(2,1)S(1)}, u32[]{:S(2)}, u32[]{:S(2)}) collective-permute-start(bf16[8,6,32,256]{3,2,1,0:T(8,128)(2,1)S(1)} %all-to-all-done.own_ref), channel_id=1, source_target_pairs={{0,24},{1,25},{2,26},{3,27},{4,28},{5,29},{6,30},{7,31},{8,0},{9,1... | collective-permute-start | bytes 2359304 | tf_op jit(solution)/shard_map/ppermute | solution.py:23
  41.1 34.9 %collective-permute-start.6 = (bf16[8,6,32,256]{3,2,1,0:T(8,128)(2,1)S(1)}, bf16[8,6,32,256]{3,2,1,0:T(8,128)(2,1)S(1)}, u32[]{:S(2)}, u32[]{:S(2)}) collective-permute-start(bf16[8,6,32,256]{3,2,1,0:T(8,128)(2,1)S(1)} %all-to-all-done.own_ref), channel_id=1, source_target_pairs={{0,8},{1,9},{2,10},{3,11},{4,12},{5,13},{6,14},{7,15},{8,16},{9,17... | collective-permute-start | bytes 2359304 | tf_op jit(solution)/shard_map/ppermute | solution.py:23
  52.7 25.0 %all-to-all-start.2 = ((bf16[8,4,3,32,128]{4,3,2,1,0:T(8,128)(2,1)}), bf16[8,4,3,32,128]{4,3,2,1,0:T(8,128)(2,1)S(1)}, u32[]{:S(2)}, u32[]{:S(2)}) async-start(bf16[8,4,3,32,128]{4,3,2,1,0:T(8,128)(2,1)} %shard_map.98), calls=%async_computation.2 | async-start | bytes 1572864 | tf_op jit(solution)/shard_map/all_to_all | solution.py:34
  77.7 16.6 %copy-start.2 = (f32[32,3,2048]{2,0,1:T(8,128)S(1)}, f32[32,3,2048]{2,0,1:T(8,128)}, u32[]{:S(2)}) copy-start(f32[32,3,2048]{2,0,1:T(8,128)} %param.11) | copy-start | bytes 2359300
  77.7 16.6 %copy-start.3 = (f32[3,2048]{1,0:T(4,128)S(1)}, f32[3,2048]{1,0:T(4,128)}, u32[]{:S(2)}) copy-start(f32[3,2048]{1,0:T(4,128)} %refs_8_.1) | copy-start | bytes 73732
  77.7 16.6 %copy-start.4 = (f32[3,2048]{1,0:T(4,128)S(1)}, f32[3,2048]{1,0:T(4,128)}, u32[]{:S(2)}) copy-start(f32[3,2048]{1,0:T(4,128)} %refs_10_.1) | copy-start | bytes 73732
  77.7 16.6 %copy-start.5 = (f32[3,2048]{1,0:T(4,128)S(1)}, f32[3,2048]{1,0:T(4,128)}, u32[]{:S(2)}) copy-start(f32[3,2048]{1,0:T(4,128)} %refs_11_.1) | copy-start | bytes 73732
  77.7 16.6 %copy-start.6 = (f32[2048]{0:T(1024)S(1)}, f32[2048]{0:T(1024)}, u32[]{:S(2)}) copy-start(f32[2048]{0:T(1024)} %param.13) | copy-start | bytes 24580
  77.7 16.6 %all-to-all-start.3 = ((bf16[8,6,32,256]{3,2,1,0:T(8,128)(2,1)}), bf16[8,6,32,256]{3,2,1,0:T(8,128)(2,1)S(1)}, u32[]{:S(2)}, u32[]{:S(2)}) async-start(bf16[8,6,32,256]{3,2,1,0:T(8,128)(2,1)} %shard_map.99), calls=%async_computation.3 | async-start | bytes 1572864 | tf_op jit(solution)/shard_map/all_to_all | solution.py:34
  82.6 18.9 %collective-permute-start.5 = (bf16[8,3,32,128]{3,2,1,0:T(8,128)(2,1)}, bf16[8,3,32,128]{3,2,1,0:T(8,128)(2,1)S(1)}, u32[]{:S(2)}, u32[]{:S(2)}) collective-permute-start(bf16[8,3,32,128]{3,2,1,0:T(8,128)(2,1)} %get-tuple-element.16), channel_id=1, source_target_pairs={{0,24},{1,25},{2,26},{3,27},{4,28},{5,29},{6,30},{7,31},{8,16},{9,... | collective-permute-start | bytes 589832 | tf_op jit(solution)/shard_map/ppermute | solution.py:28
  84.4 19.6 %collective-permute-start.4 = (bf16[8,3,32,128]{3,2,1,0:T(8,128)(2,1)}, bf16[8,3,32,128]{3,2,1,0:T(8,128)(2,1)S(1)}, u32[]{:S(2)}, u32[]{:S(2)}) collective-permute-start(bf16[8,3,32,128]{3,2,1,0:T(8,128)(2,1)} %get-tuple-element.17), channel_id=1, source_target_pairs={{0,16},{1,17},{2,18},{3,19},{4,20},{5,21},{6,22},{7,23},{8,24},{9,... | collective-permute-start | bytes 589832 | tf_op jit(solution)/shard_map/ppermute | solution.py:28
  85.8 18.1 %collective-permute-start.3 = (bf16[8,3,32,128]{3,2,1,0:T(8,128)(2,1)S(1)}, bf16[8,3,32,128]{3,2,1,0:T(8,128)(2,1)S(1)}, u32[]{:S(2)}, u32[]{:S(2)}) collective-permute-start(bf16[8,3,32,128]{3,2,1,0:T(8,128)(2,1)S(1)} %get-tuple-element.18), channel_id=1, source_target_pairs={{0,8},{1,9},{2,10},{3,11},{4,12},{5,13},{6,14},{7,15},{8,0},{9,1},... | collective-permute-start | bytes 589832 | tf_op jit(solution)/shard_map/ppermute | solution.py:28

commit v2 on v1

v2 whole, which is shorter than its diff:
```python
import jax
import jax.numpy as jnp
from jax import lax
from jax.experimental import pallas as pl
from jax.experimental.pallas import tpu as pltpu
from jax.sharding import PartitionSpec as P

LANES = 128
VMEM = pl.BlockSpec(memory_space=pltpu.VMEM)
SMEM = pl.BlockSpec(memory_space=pltpu.SMEM)
HBM = pl.BlockSpec(memory_space=pltpu.HBM)


def team_size(count, rows, reach):
    for size in range(1, count + 1):
        if count % size == 0 and rows * size >= reach:
            return size
    return count


def shifted(value, team, by):
    count = lax.axis_size("span")
    return lax.ppermute(value, "span", [(i, (i + by * team) % count) for i in range(count)])


def crossed(value, team, x):
    count = lax.axis_size("span")
    return lax.ppermute(value, "span", [(i, (i // team ^ x) * team + i % team) for i in range(count)])


def crossing(pieces, team):
    return [pieces[0]] + [crossed(pieces[x], team, x) for x in range(1, len(pieces))]


def within(value, team):
    count = lax.axis_size("span")
    teams = [[first + i for i in range(team)] for first in range(0, count, team)]
    return lax.all_to_all(value, "span", 0, 0, axis_index_groups=teams, tiled=True)


def direct(pieces):
    count = lax.axis_size("span")
    order = sorted(range(1, len(pieces)), key=lambda x: -x)
    got = list(pieces)
    for x in order:
        got[x] = lax.ppermute(pieces[x], "span", [(i, i ^ x) for i in range(count)])
    return got


def kernel_call(body, inputs, outputs, in_specs=None, out_specs=None, scratch=(), flops=1e6, limit=16 << 20):
    moved = sum(a.size * a.dtype.itemsize for a in (*inputs, *outputs))
    return pl.pallas_call(
        body,
        in_specs=in_specs or [VMEM] * len(inputs),
        out_specs=out_specs or [VMEM] * len(outputs),
        out_shape=outputs,
        scratch_shapes=scratch,
        cost_estimate=pl.CostEstimate(flops=int(flops), bytes_accessed=moved, transcendentals=0),
        compiler_params=pltpu.CompilerParams(vmem_limit_bytes=limit),
    )(*inputs)


def band_kernel(taps_ref, band_ref):
    height, length = band_ref.shape
    spread = jnp.broadcast_to(taps_ref[...], (height, length))
    band_ref[...] = pltpu.roll(spread, 0, 1, stride=1, stride_axis=0).astype(jnp.bfloat16)


def band_of(taps, height, reach):
    lead = height - reach
    padded = jnp.pad(taps.astype(jnp.float32), (lead, 3 * height - lead - taps.shape[0]))
    shape = jax.ShapeDtypeStruct((height, 3 * height), jnp.bfloat16)
    return kernel_call(band_kernel, [padded[None]], [shape])[0]


def turned(slabs_ref, turned_ref, put):
    rows, parts, planes, width = slabs_ref.shape
    for part in range(parts):
        for column in range(width // LANES):
            at = slice(column * LANES, (column + 1) * LANES)
            held = turned_ref.at[(part * (width // LANES) + column) % turned_ref.shape[0]]
            for row in range(rows):
                held[pl.ds(row, planes, stride=rows), :] = slabs_ref[row, part, :, at].astype(jnp.float32)
            put(part, column, lambda plane: held[plane * rows : (plane + 1) * rows, :].astype(jnp.bfloat16))


def near_pack_kernel(early, place_ref, slabs_ref, *refs):
    strips_ref, turned_ref = refs[-2:]
    parts = slabs_ref.shape[1]
    strip = strips_ref.shape[3]

    def put(part, column, value):
        member, inner = divmod(column * LANES, strip)
        for plane in range(early):
            strips_ref[member, plane * parts + part, :, inner : inner + LANES] = value(plane)

    turned(slabs_ref, turned_ref, put)
    for x, ref in enumerate(refs[:-2]):
        ref[...] = strips_ref[place_ref[1] ^ x]


def far_pack_kernel(early, place_ref, slabs_ref, *refs):
    far_ref, turned_ref = refs[-2:]
    planes, width = slabs_ref.shape[2:]
    slots = width // far_ref.shape[0] // LANES

    def put(part, column, value):
        group, slot = divmod(column, slots)
        for plane in range(early, planes):
            member = (plane - early) * slots + slot
            far_ref[group, place_ref[1] ^ member, part] = value(plane)

    turned(slabs_ref, turned_ref, put)
    for k, ref in enumerate(refs[:-2]):
        ref[...] = far_ref[place_ref[0] ^ k]


def join_kernel(*refs):
    for x, ref in enumerate(refs[:-1]):
        refs[-1][x] = ref[...]


def swap_kernel(count, *refs):
    for k, ref in enumerate(refs[:count]):
        for x, out_ref in enumerate(refs[count:]):
            out_ref[k] = ref[x]


def banded(band_ref, blocks):
    height = band_ref.shape[0]
    total = None
    for i, block in enumerate(blocks):
        block = block.reshape(height, block.shape[-1])
        part = jnp.dot(band_ref[:, i * height : (i + 1) * height], block, preferred_element_type=jnp.float32)
        total = part if total is None else total + part
    return total


def near_rows(member, band_ref, before_ref, own_ref, after_ref, out_ref):
    team = own_ref.shape[0]
    for u in range(own_ref.shape[1]):
        blocks = [
            jnp.concatenate([ref[member ^ i, u] for i in range(team)], axis=0) for ref in (before_ref, own_ref, after_ref)
        ]
        out_ref[:, u] = banded(band_ref, blocks).astype(out_ref.dtype).reshape(out_ref[:, u].shape)


def near_kernel(band_ref, before_ref, after_ref, own_ref, out_ref):
    near_rows(0, band_ref, before_ref, own_ref, after_ref, out_ref)


def near_split_kernel(place_ref, band_ref, before_ref, after_ref, own_ref, *refs):
    near_rows(place_ref[1], band_ref, before_ref, own_ref, after_ref, refs[-1])
    for x, ref in enumerate(refs[:-1]):
        ref[...] = refs[-1][place_ref[1] ^ x]


def far_kernel(team, place_ref, band_ref, *refs):
    held_ref, out_ref = refs[2 * team :]
    groups, units = held_ref.shape[1:3]
    me, member = place_ref[0], place_ref[1]
    height = band_ref.shape[0]
    for x in range(team):
        held_ref[member ^ x] = refs[x][...]
    for q in range(groups):
        blocks = []
        for i in range(3):
            slot = me ^ ((q + i - 1) % groups)
            wide = [held_ref[:, slot, u].reshape(height, LANES) for u in range(units)]
            blocks.append(jnp.concatenate(wide, axis=1))
        total = banded(band_ref, blocks).astype(out_ref.dtype)
        for u in range(units):
            out_ref[:, me ^ q, u] = total[:, u * LANES : (u + 1) * LANES].reshape(team, -1, LANES)
    for x in range(team):
        refs[team + x][...] = out_ref[member ^ x]


def contract(rows, wall):
    return lax.dot_general(rows, wall, (((1,), (1,)), ((), ())), preferred_element_type=jnp.float32)


def advance(state, fresh, at, scale_ref, mean_ref, diag_ref, off_ref):
    def line(ref, i):
        return ref[i : i + 1, at]

    for i in range(len(state)):
        scale = line(scale_ref, i)
        decay = jnp.exp(-jnp.pi / (2.0 * scale))
        inject = jnp.sqrt(1.0 - jnp.exp(-jnp.pi / scale))
        state[i] = decay * state[i] + inject * fresh[i]
    along, normal, spanwise = state
    first = line(mean_ref, 0) + line(diag_ref, 0) * along
    second = line(off_ref, 0) * along + line(diag_ref, 1) * normal
    third = line(off_ref, 1) * along + line(off_ref, 2) * normal + line(diag_ref, 2) * spanwise
    return state, (first, second, third)


def stored(speeds, first, step, turned_ref, speed_ref, start):
    rows, parts = speed_ref.shape[:2]
    span = slice(first, first + len(speeds))
    for i in range(parts):
        for j in range(speeds[0][0].shape[1] // LANES):
            held = turned_ref.at[step, i, j]
            for plane, parted in enumerate(speeds):
                held[plane * rows : (plane + 1) * rows, :] = parted[i][:, j * LANES : (j + 1) * LANES]
            lanes = slice(start + j * LANES, start + (j + 1) * LANES)
            for row in range(rows):
                column = held[pl.ds(row, len(speeds), stride=rows), :]
                speed_ref[row, i, span, lanes] = column.astype(speed_ref.dtype)


def far_rows(member, ref, late, slot):
    slots = ref.shape[0] // late
    pair = [
        jnp.concatenate([ref[member ^ (p * slots + slot + i)].reshape(-1, LANES) for i in range(2)], axis=1) for p in range(late)
    ]
    return jnp.concatenate(pair, axis=0)


def far_sum(place_ref, refs, order, late, wall_ref, at, total):
    for k, ref in zip(order, refs):
        slots = ref.shape[0] // late
        for slot in range(0, slots, 2):
            where = pl.multiple_of((place_ref[0] ^ k) * (slots * LANES) + slot * LANES, 2 * LANES)
            part = contract(far_rows(place_ref[1], ref, late, slot), wall_ref[at, pl.ds(where, 2 * LANES)])
            total = part if total is None else total + part
    return total


def far_start_kernel(late, place_ref, own_ref, next_ref, wall_ref, sum_ref, held_ref, sems):
    width = wall_ref.shape[0]
    block = 2 * LANES
    copies = []
    for step, start in enumerate(range(0, width, block)):
        at = pl.ds(start, block)
        copies.append(pltpu.make_async_copy(wall_ref.at[at], held_ref.at[at], sems.at[step]))
        copies[-1].start()
    for step, start in enumerate(range(0, width, block)):
        at = slice(start, start + block)
        copies[step].wait()
        sum_ref[:, at] = far_sum(place_ref, [own_ref, next_ref], [0, 1], late, held_ref, at, None)


def near_wall_kernel(place_ref, *refs):
    near_refs = refs[:-9]
    wall_ref, state_ref, scale_ref, mean_ref, diag_ref, off_ref, speed_ref, next_ref, turned_ref = refs[-9:]
    units, rows, strip = near_refs[0].shape
    parts = state_ref.shape[0]
    width = wall_ref.shape[0]
    block = 2 * LANES
    for step, start in enumerate(range(0, width, block)):
        at = slice(start, start + block)
        total = None
        for x, ref in enumerate(near_refs):
            where = pl.multiple_of((place_ref[1] ^ x) * strip, strip)
            part = contract(ref[...].reshape(units * rows, strip), wall_ref[at, pl.ds(where, strip)])
            total = part if total is None else total + part
        state = [state_ref[i, :, at] for i in range(parts)]
        speeds = []
        for plane in range(units // parts):
            fresh = [total[(plane * parts + i) * rows :][:rows] for i in range(parts)]
            state, parted = advance(state, fresh, at, scale_ref, mean_ref, diag_ref, off_ref)
            speeds.append(parted)
        for i in range(parts):
            next_ref[i, :, at] = state[i]
        stored(speeds, 0, step, turned_ref, speed_ref, start)


def far_wall_kernel(late, count, place_ref, *refs):
    far_refs = refs[:count]
    sum_ref, wall_ref, state_ref, early_ref, scale_ref, mean_ref, diag_ref, off_ref = refs[count : count + 8]
    velocity_ref, last_ref, turned_ref, final_ref, sems = refs[count + 8 :]
    parts, rows, width = state_ref.shape
    early = velocity_ref.shape[2] - late
    block = 2 * LANES
    copies = []
    for step, start in enumerate(range(0, width, block)):
        at = slice(start, start + block)
        order = range(2, 2 + count)
        total = far_sum(place_ref, far_refs, order, late, wall_ref, at, sum_ref[:, at])
        state = [state_ref[i, :, at] for i in range(parts)]
        speeds = []
        for plane in range(late):
            fresh = [total[(plane * parts + i) * rows :][:rows] for i in range(parts)]
            state, parted = advance(state, fresh, at, scale_ref, mean_ref, diag_ref, off_ref)
            speeds.append(parted)
        for i in range(parts):
            final_ref[i, :, at] = state[i]
        stored(speeds, early, step, turned_ref, early_ref, start)
        here = pltpu.make_async_copy(early_ref.at[:, :, :, at], velocity_ref.at[:, :, :, at], sems.at[0, step])
        here.start()
        also = pltpu.make_async_copy(final_ref.at[:, :, at], last_ref.at[:, :, at], sems.at[1, step])
        also.start()
        copies += [here, also]
    for copy in copies:
        copy.wait()


def plain(slabs, band, wall_filter, prev_state, time_scale, mean_velocity, lund_diag, lund_off):
    rows, planes, parts, width = slabs.shape
    height = band.shape[0]
    team = height // rows
    strip = width // team
    near = slabs.reshape(rows, planes, parts, team, strip).transpose(3, 1, 2, 0, 4)
    near = within(near.reshape(team, planes * parts, rows, strip), team)
    after = shifted(near, team, -1)
    before = shifted(near, team, 1)
    shape = jax.ShapeDtypeStruct(near.shape, near.dtype)
    near = kernel_call(near_kernel, [band, before, after, near], [shape], limit=32 << 20)[0]
    near = within(near, team).reshape(team, planes, parts, rows, strip)
    near = near.transpose(1, 2, 3, 0, 4).reshape(planes, parts, rows, width)
    filtered = lax.dot_general(near, wall_filter, (((3,), (1,)), ((), ())), preferred_element_type=jnp.float32)
    decay = jnp.exp(-jnp.pi / (2.0 * time_scale))[:, None]
    inject = jnp.sqrt(1.0 - jnp.exp(-jnp.pi / time_scale))[:, None]
    state = prev_state.transpose(1, 0, 2)
    outputs = []
    for plane in range(planes):
        state = decay * state + inject * filtered[plane]
        first = mean_velocity + lund_diag[0] * state[0]
        second = lund_off[0] * state[0] + lund_diag[1] * state[1]
        third = lund_off[1] * state[0] + lund_off[2] * state[1] + lund_diag[2] * state[2]
        outputs.append(jnp.stack([first, second, third]).astype(jnp.bfloat16))
    return (jnp.stack(outputs).transpose(2, 0, 1, 3), state.transpose(1, 0, 2))


def body(
    random_slabs,
    span_weights,
    wall_filter,
    prev_state,
    time_scale,
    mean_velocity,
    lund_diag,
    lund_off,
):
    rows, planes, parts, width = random_slabs.shape
    reach = (span_weights.shape[0] - 1) // 2
    count = lax.axis_size("span")
    team = team_size(count, rows, reach)
    groups = count // team
    height = rows * team
    scaling = jnp.sqrt(jnp.sum(span_weights * span_weights))
    taps = (span_weights / scaling).astype(jnp.bfloat16)
    band = band_of(taps, height, reach)
    device = lax.axis_index("span")
    place = jnp.stack([device // team, device % team]).astype(jnp.int32)

    late = planes // 2
    if width != groups * (team // late) * LANES or groups > 4:
        return plain(random_slabs, band, wall_filter, prev_state, time_scale, mean_velocity, lund_diag, lund_off)
    early = planes - late
    strip = width // team
    units = early * parts
    slabs = random_slabs.transpose(0, 2, 1, 3)
    state = prev_state.transpose(1, 0, 2)
    lines = [time_scale, mean_velocity[None], lund_diag, lund_off]
    shape = jax.ShapeDtypeStruct

    turning = [pltpu.VMEM((4, planes * rows, LANES), jnp.float32)]
    far = kernel_call(
        lambda *refs: far_pack_kernel(early, *refs),
        [place, slabs],
        [shape((team, parts, rows, LANES), slabs.dtype)] * groups,
        in_specs=[SMEM, VMEM],
        scratch=[pltpu.VMEM((groups, team, parts, rows, LANES), slabs.dtype), *turning],
    )
    near = kernel_call(
        lambda *refs: near_pack_kernel(early, *refs),
        [place, slabs],
        [shape((units, rows, strip), slabs.dtype)] * team,
        in_specs=[SMEM, VMEM],
        scratch=[pltpu.VMEM((team, units, rows, strip), slabs.dtype), *turning],
    )
    far = crossing(far, team)
    near = direct(near)
    near = kernel_call(join_kernel, near, [shape((team, units, rows, strip), slabs.dtype)])[0]
    after = shifted(near, team, -1)
    before = shifted(near, team, 1)
    pieces = [shape((groups, parts, rows, LANES), slabs.dtype)] * team
    far = kernel_call(lambda *refs: swap_kernel(groups, *refs), far, pieces)
    far = direct(far)
    far = kernel_call(
        lambda *refs: far_kernel(team, *refs),
        [place, band, *far],
        pieces,
        in_specs=[SMEM] + [VMEM] * (1 + team),
        scratch=[pltpu.VMEM((team, *pieces[0].shape), slabs.dtype)] * 2,
        flops=2 * band.size * groups * team * parts * rows * LANES // rows,
    )
    far = direct(far)
    far = kernel_call(
        lambda *refs: swap_kernel(team, *refs), far, [shape((team, parts, rows, LANES), slabs.dtype)] * groups
    )
    near = kernel_call(
        near_split_kernel,
        [place, band, before, after, near],
        [shape(near.shape[1:], near.dtype)] * team,
        in_specs=[SMEM] + [VMEM] * 4,
        scratch=[pltpu.VMEM(near.shape, near.dtype)],
        flops=2 * band.size * near.size // height,
    )
    near = direct(near)
    far = crossing(far, team)
    steps = width // (2 * LANES)
    turning = pltpu.VMEM((steps, parts, 2, late * rows, LANES), jnp.float32)
    sums, wall = kernel_call(
        lambda *refs: far_start_kernel(late, *refs),
        [place, far[0], far[1], wall_filter],
        [shape((late * parts * rows, width), jnp.float32), shape(wall_filter.shape, wall_filter.dtype)],
        in_specs=[SMEM, VMEM, VMEM, HBM],
        scratch=[pltpu.SemaphoreType.DMA((steps,))],
        flops=wall_filter.size * late * parts * rows,
        limit=42 << 20,
    )
    speeds, state = kernel_call(
        near_wall_kernel,
        [place, *near, wall, state, *lines],
        [shape(slabs.shape, slabs.dtype), shape(state.shape, state.dtype)],
        in_specs=[SMEM] + [VMEM] * (team + 6),
        scratch=[turning],
        flops=2 * wall_filter.size * units * rows,
    )
    rest = far[2:]
    velocity, state = kernel_call(
        lambda *refs: far_wall_kernel(late, len(rest), *refs),
        [place, *rest, sums, wall, state, speeds, *lines],
        [shape(slabs.shape, slabs.dtype), shape(state.shape, state.dtype)],
        in_specs=[SMEM] + [VMEM] * (len(rest) + 8),
        out_specs=[HBM, HBM],
        scratch=[turning, pltpu.VMEM(state.shape, state.dtype), pltpu.SemaphoreType.DMA((2, steps))],
        flops=wall_filter.size * late * parts * rows,
    )
    return (velocity.transpose(0, 2, 1, 3), state.transpose(1, 0, 2))


def solution(mesh):
    placed = (P("span", None, None, None), P(), P(), P("span", None, None), P(), P(), P(), P())
    return jax.shard_map(
        body,
        mesh=mesh,
        in_specs=placed,
        out_specs=(P("span", None, None, None), P("span", None, None)),
        check_vma=False,
    )
```

time: 112 us -> 112 us (level); the launches traced: 111 us -> 110 us
  starting transfers between devices: 28.3 us -> 37.7 us
  waiting for transfers between devices: 54.8 us -> 46.2 us
    ppermute x0 -> x28, starting transfers between devices: none -> 25.7 us  [direct(): got[x] = lax.ppermute(pieces[x], 'span', [(i, i ^ x) for i in range(count)])]
    ppermute x0 -> x28, waiting for transfers between devices: none -> 17.3 us  [direct(): got[x] = lax.ppermute(pieces[x], 'span', [(i, i ^ x) for i in range(count)])]
    all_to_all x4 -> x0, starting transfers between devices: 17 us -> none  [within(): lax.all_to_all(value, 'span', 0, 0, axis_index_groups=teams, tiled=True)]
    all_to_all x4 -> x0, waiting for transfers between devices: 16 us -> none  [within(): lax.all_to_all(value, 'span', 0, 0, axis_index_groups=teams, tiled=True)]
    ppermute x2, waiting for transfers between devices: 19.8 us -> 14.5 us  [shifted(): lax.ppermute(value, 'span', [(i, (i + by * team) % count) for i in range(...]
    ppermute x6, waiting for transfers between devices: 19 us -> 14.4 us  [crossed(): lax.ppermute(value, 'span', [(i, (i // team ^ x) * team + i % team) for i...]
    pallas_call x7 -> x11, Pallas kernels: 22.8 us -> 22.6 us  [kernel_call(): pl.pallas_call(body, in_specs=in_specs or [VMEM] * len(inputs), out_specs...]
  transfers between devices with their start and end apart: 12 -> 36, of which waited for: 7 -> 15; matrix products, arithmetic and copies ran while one was open for 2% -> 1% of each run, Pallas kernels for 12% -> 14%
where the time goes in v2:
time: 112 us; the launch traced here: 110 us
  waiting for transfers between devices  46.2 us (41%)
  starting transfers between devices  37.7 us (34%)
  Pallas kernels  22.6 us (20%)
  between operations  1.73 us (2%)
  local copies, waits for them, and re-layouts  1.44 us (1%)
    ppermute x28, starting transfers between devices, direct(): got[x] = lax.ppermute(pieces[x], 'span', [(i, i ^ x) for i in range(count)])  25.7 us
    pallas_call x11, Pallas kernels, kernel_call(): pl.pallas_call(body, in_specs=in_specs or [VMEM] * len(inputs), out_specs...  22.6 us
    ppermute x28, waiting for transfers between devices, direct(): got[x] = lax.ppermute(pieces[x], 'span', [(i, i ^ x) for i in range(count)])  17.3 us
    ppermute x2, waiting for transfers between devices, shifted(): lax.ppermute(value, 'span', [(i, (i + by * team) % count) for i in range(...  14.5 us
    ppermute x6, waiting for transfers between devices, crossed(): lax.ppermute(value, 'span', [(i, (i // team ^ x) * team + i % team) for i...  14.4 us
    ppermute x6, starting transfers between devices, crossed(): lax.ppermute(value, 'span', [(i, (i // team ^ x) * team + i % team) for i...  9.02 us
    ppermute x2, starting transfers between devices, shifted(): lax.ppermute(value, 'span', [(i, (i + by * team) % count) for i in range(...  3.03 us
  transfers between devices with their start and end apart: 36, of which 15 were waited for; matrix products, arithmetic and copies ran while one was open for 1% of the time, Pallas kernels for 14%

profile of v2, /device:TPU:0, one launch (start us, length us, event | category | flops | bytes accessed | tf_op | source)
XLA Modules:
  0.0 110.3 jit_solution(18091617425655747649)
XLA Ops:
  2.1 2.0 %shard_map.96 = (bf16[8,3,32,128]{3,2,1,0:T(8,128)(2,1)S(1)}, bf16[8,3,32,128]{3,2,1,0:T(8,128)(2,1)S(1)}, bf16[8,3,32,128]{3,2,1,0:T(8,128)(2,1)S(1)}, bf16[8,3,32,128]{3,2,1,0:T(8,128)(2,1)S(1)}) custom-call(s32[2]{0:T(128)S(1)} %pad_add_fusion.refs_0_.place_ref, bf16[32,3,4,2048]{3,2,1,0:T(4,128)(2,1)S(1)} %bitcast.7), custom_call_target="tpu_custom_call" | custom-call | flops 1000000 | bytes 2359304 | tf_op jit(solution)/shard_map/pallas_call | solution.py:52
  4.2 3.1 %collective-permute-start = (bf16[8,3,32,128]{3,2,1,0:T(8,128)(2,1)S(1)}, bf16[8,3,32,128]{3,2,1,0:T(8,128)(2,1)S(1)}, u32[]{:S(2)}, u32[]{:S(2)}) collective-permute-start(bf16[8,3,32,128]{3,2,1,0:T(8,128)(2,1)S(1)} %get-tuple-element.49), channel_id=1, source_target_pairs={{0,8},{1,9},{2,10},{3,11},{4,12},{5,13},{6,14},{7,15},{8,0},{9,1},... | collective-permute-start | bytes 589832 | tf_op jit(solution)/shard_map/ppermute | solution.py:28
  7.3 2.6 %collective-permute-start.1 = (bf16[8,3,32,128]{3,2,1,0:T(8,128)(2,1)S(1)}, bf16[8,3,32,128]{3,2,1,0:T(8,128)(2,1)S(1)}, u32[]{:S(2)}, u32[]{:S(2)}) collective-permute-start(bf16[8,3,32,128]{3,2,1,0:T(8,128)(2,1)S(1)} %get-tuple-element.50), channel_id=1, source_target_pairs={{0,16},{1,17},{2,18},{3,19},{4,20},{5,21},{6,22},{7,23},{8,24},{9,... | collective-permute-start | bytes 589832 | tf_op jit(solution)/shard_map/ppermute | solution.py:28
  9.9 2.1 %shard_map.101 = (bf16[6,32,256]{2,1,0:T(8,128)(2,1)S(1)}, bf16[6,32,256]{2,1,0:T(8,128)(2,1)S(1)}, bf16[6,32,256]{2,1,0:T(8,128)(2,1)S(1)}, bf16[6,32,256]{2,1,...) custom-call(s32[2]{0:T(128)S(1)} %pad_add_fusion.refs_0_.place_ref, ...), custom_call_target="tpu_custom_call" | custom-call | flops 1000000 | bytes 2359304 | tf_op jit(solution)/shard_map/pallas_call | solution.py:52
  12.0 1.8 %collective-permute-start.21 = (bf16[6,32,256]{2,1,0:T(8,128)(2,1)S(1)}, bf16[6,32,256]{2,1,0:T(8,128)(2,1)S(1)}, u32[]{:S(2)}, u32[]{:S(2)}) collective-permute-start(bf16[6,32,256]{2,1,0:T(8,128)(2,1)S(1)} %get-tuple-element.76), channel_id=1, source_target_pairs={{0,2},{1,3},{2,0},{3,1},{4,6},{5,7},{6,4},{7,5},{8,10},{9,11},{10,... | collective-permute-start | bytes 294920 | tf_op jit(solution)/shard_map/ppermute | solution.py:46
  13.8 1.8 %collective-permute-done.refs_1_ = bf16[8,3,32,128]{3,2,1,0:T(8,128)(2,1)S(1)} collective-permute-done((bf16[8,3,32,128]{3,2,1,0:T(8,128)(2,1)S(1)}, bf16[8,3,32,128]{3,2,1,0:T(8,128)(2,1)S(1)}, u32[]{:S(2)}, u32[]{:S(2)}) %collective-permute-start) | collective-permute-done | bytes 196640 | tf_op jit(solution)/shard_map/ppermute | solution.py:28
  15.7 8.7 %collective-permute-done.1.refs_2_ = bf16[8,3,32,128]{3,2,1,0:T(8,128)(2,1)S(1)} collective-permute-done((bf16[8,3,32,128]{3,2,1,0:T(8,128)(2,1)S(1)}, bf16[8,3,32,128]{3,2,1,0:T(8,128)(2,1)S(1)}, u32[]{:S(2)}, u32[]{:S(2)}) %collective-permute-start.1) | collective-permute-done | bytes 196640 | tf_op jit(solution)/shard_map/ppermute | solution.py:28
  24.4 1.5 %collective-permute-start.23 = (bf16[6,32,256]{2,1,0:T(8,128)(2,1)S(1)}, bf16[6,32,256]{2,1,0:T(8,128)(2,1)S(1)}, u32[]{:S(2)}, u32[]{:S(2)}) collective-permute-start(bf16[6,32,256]{2,1,0:T(8,128)(2,1)S(1)} %get-tuple-element.78), channel_id=1, source_target_pairs={{0,4},{1,5},{2,6},{3,7},{4,0},{5,1},{6,2},{7,3},{8,12},{9,13},{10,... | collective-permute-start | bytes 294920 | tf_op jit(solution)/shard_map/ppermute | solution.py:46
  27.4 1.5 %collective-permute-start.25 = (bf16[6,32,256]{2,1,0:T(8,128)(2,1)S(1)}, bf16[6,32,256]{2,1,0:T(8,128)(2,1)S(1)}, u32[]{:S(2)}, u32[]{:S(2)}) collective-permute-start(bf16[6,32,256]{2,1,0:T(8,128)(2,1)S(1)} %get-tuple-element.80), channel_id=1, source_target_pairs={{0,6},{1,7},{2,4},{3,5},{4,2},{5,3},{6,0},{7,1},{8,14},{9,15},{10,... | collective-permute-start | bytes 294920 | tf_op jit(solution)/shard_map/ppermute | solution.py:46
  28.9 1.4 %collective-permute-start.26 = (bf16[6,32,256]{2,1,0:T(8,128)(2,1)S(1)}, bf16[6,32,256]{2,1,0:T(8,128)(2,1)S(1)}, u32[]{:S(2)}, u32[]{:S(2)}) collective-permute-start(bf16[6,32,256]{2,1,0:T(8,128)(2,1)S(1)} %get-tuple-element.81), channel_id=1, source_target_pairs={{0,7},{1,6},{2,5},{3,4},{4,3},{5,2},{6,1},{7,0},{8,15},{9,14},{10,... | collective-permute-start | bytes 294920 | tf_op jit(solution)/shard_map/ppermute | solution.py:46
  30.5 1.5 %collective-permute-start.4 = (bf16[4,3,32,128]{3,2,1,0:T(8,128)(2,1)S(1)}, bf16[4,3,32,128]{3,2,1,0:T(8,128)(2,1)S(1)}, u32[]{:S(2)}, u32[]{:S(2)}) collective-permute-start(bf16[4,3,32,128]{3,2,1,0:T(8,128)(2,1)S(1)} %get-tuple-element.54), channel_id=1, source_target_pairs={{0,2},{1,3},{2,0},{3,1},{4,6},{5,7},{6,4},{7,5},{8,10},{9,11},{10,... | collective-permute-start | bytes 294920 | tf_op jit(solution)/shard_map/ppermute | solution.py:46
  32.0 2.7 %collective-permute-done.24.refs_5_ = bf16[6,32,256]{2,1,0:T(8,128)(2,1)S(1)} collective-permute-done((bf16[6,32,256]{2,1,0:T(8,128)(2,1)S(1)}, bf16[6,32,256]{2,1,0:T(8,128)(2,1)S(1)}, u32[]{:S(2)}, u32[]{:S(2)}) %collective-permute-start.24) | collective-permute-done | bytes 98336 | tf_op jit(solution)/shard_map/ppermute | solution.py:46
  34.7 3.4 %collective-permute-start.6 = (bf16[4,3,32,128]{3,2,1,0:T(8,128)(2,1)S(1)}, bf16[4,3,32,128]{3,2,1,0:T(8,128)(2,1)S(1)}, u32[]{:S(2)}, u32[]{:S(2)}) collective-permute-start(bf16[4,3,32,128]{3,2,1,0:T(8,128)(2,1)S(1)} %get-tuple-element.56), channel_id=1, source_target_pairs={{0,4},{1,5},{2,6},{3,7},{4,0},{5,1},{6,2},{7,3},{8,12},{9,13},{10,... | collective-permute-start | bytes 294920 | tf_op jit(solution)/shard_map/ppermute | solution.py:46
  38.1 1.9 %collective-permute-start.8 = (bf16[4,3,32,128]{3,2,1,0:T(8,128)(2,1)S(1)}, bf16[4,3,32,128]{3,2,1,0:T(8,128)(2,1)S(1)}, u32[]{:S(2)}, u32[]{:S(2)}) collective-permute-start(bf16[4,3,32,128]{3,2,1,0:T(8,128)(2,1)S(1)} %get-tuple-element.58), channel_id=1, source_target_pairs={{0,6},{1,7},{2,4},{3,5},{4,2},{5,3},{6,0},{7,1},{8,14},{9,15},{10,... | collective-permute-start | bytes 294920 | tf_op jit(solution)/shard_map/ppermute | solution.py:46
  40.8 2.5 %collective-permute-start.28 = (bf16[8,6,32,256]{3,2,1,0:T(8,128)(2,1)S(1)}, bf16[8,6,32,256]{3,2,1,0:T(8,128)(2,1)S(1)}, u32[]{:S(2)}, u32[]{:S(2)}) collective-permute-start(bf16[8,6,32,256]{3,2,1,0:T(8,128)(2,1)S(1)} %shard_map.102.own_ref), channel_id=1, source_target_pairs={{0,24},{1,25},{2,26},{3,27},{4,28},{5,29},{6,30},{7,31},{8,0},{9,1... | collective-permute-start | bytes 2359304 | tf_op jit(solution)/shard_map/ppermute | solution.py:23
  43.8 3.6 %collective-permute-done.7.refs_7_ = bf16[4,3,32,128]{3,2,1,0:T(8,128)(2,1)S(1)} collective-permute-done((bf16[4,3,32,128]{3,2,1,0:T(8,128)(2,1)S(1)}, bf16[4,3,32,128]{3,2,1,0:T(8,128)(2,1)S(1)}, u32[]{:S(2)}, u32[]{:S(2)}) %collective-permute-start.7) | collective-permute-done | bytes 98336 | tf_op jit(solution)/shard_map/ppermute | solution.py:46
  47.4 1.6 %shard_map.98 = (bf16[4,3,32,128]{3,2,1,0:T(8,128)(2,1)S(1)}, bf16[4,3,32,128]{3,2,1,0:T(8,128)(2,1)S(1)}, bf16[4,3,32,128]{3,2,1,0:T(8,128)(2,1)S(1)}, bf16[4,3...) custom-call(s32[2]{0:T(128)S(1)} %pad_add_fusion.refs_0_.place_ref, ...), custom_call_target="tpu_custom_call" | custom-call | flops 4831838208 | bytes 1966088 | tf_op jit(solution)/shard_map/pallas_call | solution.py:52
  51.0 1.6 %collective-permute-start.13 = (bf16[4,3,32,128]{3,2,1,0:T(8,128)(2,1)S(1)}, bf16[4,3,32,128]{3,2,1,0:T(8,128)(2,1)S(1)}, u32[]{:S(2)}, u32[]{:S(2)}) collective-permute-start(bf16[4,3,32,128]{3,2,1,0:T(8,128)(2,1)S(1)} %get-tuple-element.64), channel_id=1, source_target_pairs={{0,4},{1,5},{2,6},{3,7},{4,0},{5,1},{6,2},{7,3},{8,12},{9,13},{10,... | collective-permute-start | bytes 294920 | tf_op jit(solution)/shard_map/ppermute | solution.py:46
  52.6 2.5 %collective-permute-done.11.refs_2_ = bf16[4,3,32,128]{3,2,1,0:T(8,128)(2,1)S(1)} collective-permute-done((bf16[4,3,32,128]{3,2,1,0:T(8,128)(2,1)S(1)}, bf16[4,3,32,128]{3,2,1,0:T(8,128)(2,1)S(1)}, u32[]{:S(2)}, u32[]{:S(2)}) %collective-permute-start.11) | collective-permute-done | bytes 98336 | tf_op jit(solution)/shard_map/ppermute | solution.py:46
  55.6 2.1 %collective-permute-start.15 = (bf16[4,3,32,128]{3,2,1,0:T(8,128)(2,1)S(1)}, bf16[4,3,32,128]{3,2,1,0:T(8,128)(2,1)S(1)}, u32[]{:S(2)}, u32[]{:S(2)}) collective-permute-start(bf16[4,3,32,128]{3,2,1,0:T(8,128)(2,1)S(1)} %get-tuple-element.66), channel_id=1, source_target_pairs={{0,6},{1,7},{2,4},{3,5},{4,2},{5,3},{6,0},{7,1},{8,14},{9,15},{10,... | collective-permute-start | bytes 294920 | tf_op jit(solution)/shard_map/ppermute | solution.py:46
  57.7 1.5 %collective-permute-start.16 = (bf16[4,3,32,128]{3,2,1,0:T(8,128)(2,1)S(1)}, bf16[4,3,32,128]{3,2,1,0:T(8,128)(2,1)S(1)}, u32[]{:S(2)}, u32[]{:S(2)}) collective-permute-start(bf16[4,3,32,128]{3,2,1,0:T(8,128)(2,1)S(1)} %get-tuple-element.67), channel_id=1, source_target_pairs={{0,7},{1,6},{2,5},{3,4},{4,3},{5,2},{6,1},{7,0},{8,15},{9,14},{10,... | collective-permute-start | bytes 294920 | tf_op jit(solution)/shard_map/ppermute | solution.py:46
  59.9 2.1 %collective-permute-done.15.refs_6_ = bf16[4,3,32,128]{3,2,1,0:T(8,128)(2,1)S(1)} collective-permute-done((bf16[4,3,32,128]{3,2,1,0:T(8,128)(2,1)S(1)}, bf16[4,3,32,128]{3,2,1,0:T(8,128)(2,1)S(1)}, u32[]{:S(2)}, u32[]{:S(2)}) %collective-permute-start.15) | collective-permute-done | bytes 98336 | tf_op jit(solution)/shard_map/ppermute | solution.py:46
  62.0 2.5 %collective-permute-done.16.refs_7_ = bf16[4,3,32,128]{3,2,1,0:T(8,128)(2,1)S(1)} collective-permute-done((bf16[4,3,32,128]{3,2,1,0:T(8,128)(2,1)S(1)}, bf16[4,3,32,128]{3,2,1,0:T(8,128)(2,1)S(1)}, u32[]{:S(2)}, u32[]{:S(2)}) %collective-permute-start.16) | collective-permute-done | bytes 98336 | tf_op jit(solution)/shard_map/ppermute | solution.py:46
  64.5 1.5 %collective-permute-start.19 = (bf16[8,3,32,128]{3,2,1,0:T(8,128)(2,1)S(1)}, bf16[8,3,32,128]{3,2,1,0:T(8,128)(2,1)S(1)}, u32[]{:S(2)}, u32[]{:S(2)}) collective-permute-start(bf16[8,3,32,128]{3,2,1,0:T(8,128)(2,1)S(1)} %get-tuple-element.71), channel_id=1, source_target_pairs={{0,8},{1,9},{2,10},{3,11},{4,12},{5,13},{6,14},{7,15},{8,0},{9,1},... | collective-permute-start | bytes 589832 | tf_op jit(solution)/shard_map/ppermute | solution.py:28
  66.0 14.5 %collective-permute-done.27.before_ref = bf16[8,6,32,256]{3,2,1,0:T(8,128)(2,1)S(1)} collective-permute-done((bf16[8,6,32,256]{3,2,1,0:T(8,128)(2,1)S(1)}, bf16[8,6,32,256]{3,2,1,0:T(8,128)(2,1)S(1)}, u32[]{:S(2)}, u32[]{:S(2)}) %collective-permute-start.27) | collective-permute-done | bytes 786464 | tf_op jit(solution)/shard_map/ppermute | solution.py:23
  84.0 1.5 %collective-permute-start.33 = (bf16[6,32,256]{2,1,0:T(8,128)(2,1)S(1)}, bf16[6,32,256]{2,1,0:T(8,128)(2,1)S(1)}, u32[]{:S(2)}, u32[]{:S(2)}) collective-permute-start(bf16[6,32,256]{2,1,0:T(8,128)(2,1)S(1)} %get-tuple-element.87), channel_id=1, source_target_pairs={{0,5},{1,4},{2,7},{3,6},{4,1},{5,0},{6,3},{7,2},{8,13},{9,12},{10,... | collective-permute-start | bytes 294920 | tf_op jit(solution)/shard_map/ppermute | solution.py:46
  86.1 1.6 %collective-permute-done.30.refs_2_ = bf16[6,32,256]{2,1,0:T(8,128)(2,1)S(1)} collective-permute-done((bf16[6,32,256]{2,1,0:T(8,128)(2,1)S(1)}, bf16[6,32,256]{2,1,0:T(8,128)(2,1)S(1)}, u32[]{:S(2)}, u32[]{:S(2)}) %collective-permute-start.30) | collective-permute-done | bytes 98336 | tf_op jit(solution)/shard_map/ppermute | solution.py:46
  89.5 1.7 %collective-permute-start.18 = (bf16[8,3,32,128]{3,2,1,0:T(8,128)(2,1)S(1)}, bf16[8,3,32,128]{3,2,1,0:T(8,128)(2,1)S(1)}, u32[]{:S(2)}, u32[]{:S(2)}) collective-permute-start(bf16[8,3,32,128]{3,2,1,0:T(8,128)(2,1)S(1)} %get-tuple-element.69), channel_id=1, source_target_pairs={{0,24},{1,25},{2,26},{3,27},{4,28},{5,29},{6,30},{7,31},{8,16},{9,... | collective-permute-start | bytes 589832 | tf_op jit(solution)/shard_map/ppermute | solution.py:28
  91.2 5.4 %shard_map.100 = (f32[192,2048]{1,0:T(8,128)S(1)}, bf16[2048,2048]{1,0:T(8,128)(2,1)S(1)}) custom-call(s32[2]{0:T(128)S(1)} %pad_add_fusion.refs_0_.place_ref, bf16[8,3,32,128]{3,2,1,0:T(8,128)(2,1)S(1)} %get-tuple-element.70.refs_1_, bf16[8,3,32,128]{3,2,1,0:T(8,128)(2,1)S(1)} %collective-permute-done.19.refs_2_, bf16[2048,2048]{1,0:T(8,128)(2,1)} %refs_3_.1), custom_call_target="tpu_custom_call" | custom-call | flops 805306368 | bytes 18743304 | tf_op jit(solution)/shard_map/pallas_call | solution.py:52
  96.7 4.9 %shard_map.104 = (bf16[32,3,4,2048]{3,2,1,0:T(4,128)(2,1)S(1)}, f32[3,32,2048]{2,1,0:T(8,128)S(1)}) custom-call(s32[2]{0:T(128)S(1)} %pad_add_fusion.refs_0_.place_ref, bf16[6,32,256]{2,1,0:T(8,128)(2,1)S(1)} %get-tuple-element.82.refs_0_, bf16[6,32,256]{2,1,0:T(8,128)(2,1)S(1)} %collective-permute-done.29.refs_1_, ...), custom_call_target="tpu_custom_call" | custom-call | flops 1610612736 | bytes 12402696 | tf_op jit(solution)/shard_map/pallas_call | solution.py:52
  101.6 3.7 %collective-permute-done.17.refs_1_ = bf16[8,3,32,128]{3,2,1,0:T(8,128)(2,1)S(1)} collective-permute-done((bf16[8,3,32,128]{3,2,1,0:T(8,128)(2,1)S(1)}, bf16[8,3,32,128]{3,2,1,0:T(8,128)(2,1)S(1)}, u32[]{:S(2)}, u32[]{:S(2)}) %collective-permute-start.17) | collective-permute-done | bytes 196640 | tf_op jit(solution)/shard_map/ppermute | solution.py:28
  105.3 4.8 %shard_map.105 = (bf16[32,3,4,2048]{3,2,1,0:T(4,128)(2,1)}, f32[3,32,2048]{2,1,0:T(8,128)}) custom-call(s32[2]{0:T(128)S(1)} %pad_add_fusion.refs_0_.place_ref, bf16[8,3,32,128]{3,2,1,0:T(8,128)(2,1)S(1)} %collective-permute-done.17.refs_1_, bf16[8,3,32,128]{3,2,1,0:T(8,128)(2,1)S(1)} %collective-permute-done.18.refs_2_, ...), custom_call_target="tpu_custom_call" | custom-call | flops 805306368 | bytes 15155208 | tf_op jit(solution)/shard_map/pallas_call | solution.py:52
  (70 shorter events, 12.9 us)
Async XLA Ops:
  4.2 11.5 %collective-permute-start = (bf16[8,3,32,128]{3,2,1,0:T(8,128)(2,1)S(1)}, bf16[8,3,32,128]{3,2,1,0:T(8,128)(2,1)S(1)}, u32[]{:S(2)}, u32[]{:S(2)}) collective-permute-start(bf16[8,3,32,128]{3,2,1,0:T(8,128)(2,1)S(1)} %get-tuple-element.49), channel_id=1, source_target_pairs={{0,8},{1,9},{2,10},{3,11},{4,12},{5,13},{6,14},{7,15},{8,0},{9,1},... | collective-permute-start | bytes 589832 | tf_op jit(solution)/shard_map/ppermute | solution.py:28
  7.3 17.1 %collective-permute-start.1 = (bf16[8,3,32,128]{3,2,1,0:T(8,128)(2,1)S(1)}, bf16[8,3,32,128]{3,2,1,0:T(8,128)(2,1)S(1)}, u32[]{:S(2)}, u32[]{:S(2)}) collective-permute-start(bf16[8,3,32,128]{3,2,1,0:T(8,128)(2,1)S(1)} %get-tuple-element.50), channel_id=1, source_target_pairs={{0,16},{1,17},{2,18},{3,19},{4,20},{5,21},{6,22},{7,23},{8,24},{9,... | collective-permute-start | bytes 589832 | tf_op jit(solution)/shard_map/ppermute | solution.py:28
  9.9 17.3 %collective-permute-start.2 = (bf16[8,3,32,128]{3,2,1,0:T(8,128)(2,1)S(1)}, bf16[8,3,32,128]{3,2,1,0:T(8,128)(2,1)S(1)}, u32[]{:S(2)}, u32[]{:S(2)}) collective-permute-start(bf16[8,3,32,128]{3,2,1,0:T(8,128)(2,1)S(1)} %get-tuple-element.51), channel_id=1, source_target_pairs={{0,24},{1,25},{2,26},{3,27},{4,28},{5,29},{6,30},{7,31},{8,16},{9,... | collective-permute-start | bytes 589832 | tf_op jit(solution)/shard_map/ppermute | solution.py:28
  12.0 15.4 %collective-permute-start.20 = (bf16[6,32,256]{2,1,0:T(8,128)(2,1)S(1)}, bf16[6,32,256]{2,1,0:T(8,128)(2,1)S(1)}, u32[]{:S(2)}, u32[]{:S(2)}) collective-permute-start(bf16[6,32,256]{2,1,0:T(8,128)(2,1)S(1)} %get-tuple-element.75), channel_id=1, source_target_pairs={{0,1},{1,0},{2,3},{3,2},{4,5},{5,4},{6,7},{7,6},{8,9},{9,8},{10,11... | collective-permute-start | bytes 294920 | tf_op jit(solution)/shard_map/ppermute | solution.py:46
  12.0 16.8 %collective-permute-start.21 = (bf16[6,32,256]{2,1,0:T(8,128)(2,1)S(1)}, bf16[6,32,256]{2,1,0:T(8,128)(2,1)S(1)}, u32[]{:S(2)}, u32[]{:S(2)}) collective-permute-start(bf16[6,32,256]{2,1,0:T(8,128)(2,1)S(1)} %get-tuple-element.76), channel_id=1, source_target_pairs={{0,2},{1,3},{2,0},{3,1},{4,6},{5,7},{6,4},{7,5},{8,10},{9,11},{10,... | collective-permute-start | bytes 294920 | tf_op jit(solution)/shard_map/ppermute | solution.py:46
  15.7 14.6 %collective-permute-start.22 = (bf16[6,32,256]{2,1,0:T(8,128)(2,1)S(1)}, bf16[6,32,256]{2,1,0:T(8,128)(2,1)S(1)}, u32[]{:S(2)}, u32[]{:S(2)}) collective-permute-start(bf16[6,32,256]{2,1,0:T(8,128)(2,1)S(1)} %get-tuple-element.77), channel_id=1, source_target_pairs={{0,3},{1,2},{2,1},{3,0},{4,7},{5,6},{6,5},{7,4},{8,11},{9,10},{10,... | collective-permute-start | bytes 294920 | tf_op jit(solution)/shard_map/ppermute | solution.py:46
  24.4 6.1 %collective-permute-start.23 = (bf16[6,32,256]{2,1,0:T(8,128)(2,1)S(1)}, bf16[6,32,256]{2,1,0:T(8,128)(2,1)S(1)}, u32[]{:S(2)}, u32[]{:S(2)}) collective-permute-start(bf16[6,32,256]{2,1,0:T(8,128)(2,1)S(1)} %get-tuple-element.78), channel_id=1, source_target_pairs={{0,4},{1,5},{2,6},{3,7},{4,0},{5,1},{6,2},{7,3},{8,12},{9,13},{10,... | collective-permute-start | bytes 294920 | tf_op jit(solution)/shard_map/ppermute | solution.py:46
  27.2 7.4 %collective-permute-start.24 = (bf16[6,32,256]{2,1,0:T(8,128)(2,1)S(1)}, bf16[6,32,256]{2,1,0:T(8,128)(2,1)S(1)}, u32[]{:S(2)}, u32[]{:S(2)}) collective-permute-start(bf16[6,32,256]{2,1,0:T(8,128)(2,1)S(1)} %get-tuple-element.79), channel_id=1, source_target_pairs={{0,5},{1,4},{2,7},{3,6},{4,1},{5,0},{6,3},{7,2},{8,13},{9,12},{10,... | collective-permute-start | bytes 294920 | tf_op jit(solution)/shard_map/ppermute | solution.py:46
  27.4 7.3 %collective-permute-start.25 = (bf16[6,32,256]{2,1,0:T(8,128)(2,1)S(1)}, bf16[6,32,256]{2,1,0:T(8,128)(2,1)S(1)}, u32[]{:S(2)}, u32[]{:S(2)}) collective-permute-start(bf16[6,32,256]{2,1,0:T(8,128)(2,1)S(1)} %get-tuple-element.80), channel_id=1, source_target_pairs={{0,6},{1,7},{2,4},{3,5},{4,2},{5,3},{6,0},{7,1},{8,14},{9,15},{10,... | collective-permute-start | bytes 294920 | tf_op jit(solution)/shard_map/ppermute | solution.py:46
  28.9 9.2 %collective-permute-start.26 = (bf16[6,32,256]{2,1,0:T(8,128)(2,1)S(1)}, bf16[6,32,256]{2,1,0:T(8,128)(2,1)S(1)}, u32[]{:S(2)}, u32[]{:S(2)}) collective-permute-start(bf16[6,32,256]{2,1,0:T(8,128)(2,1)S(1)} %get-tuple-element.81), channel_id=1, source_target_pairs={{0,7},{1,6},{2,5},{3,4},{4,3},{5,2},{6,1},{7,0},{8,15},{9,14},{10,... | collective-permute-start | bytes 294920 | tf_op jit(solution)/shard_map/ppermute | solution.py:46
  30.3 7.8 %collective-permute-start.3 = (bf16[4,3,32,128]{3,2,1,0:T(8,128)(2,1)S(1)}, bf16[4,3,32,128]{3,2,1,0:T(8,128)(2,1)S(1)}, u32[]{:S(2)}, u32[]{:S(2)}) collective-permute-start(bf16[4,3,32,128]{3,2,1,0:T(8,128)(2,1)S(1)} %get-tuple-element.53), channel_id=1, source_target_pairs={{0,1},{1,0},{2,3},{3,2},{4,5},{5,4},{6,7},{7,6},{8,9},{9,8},{10,11... | collective-permute-start | bytes 294920 | tf_op jit(solution)/shard_map/ppermute | solution.py:46
  30.5 9.5 %collective-permute-start.4 = (bf16[4,3,32,128]{3,2,1,0:T(8,128)(2,1)S(1)}, bf16[4,3,32,128]{3,2,1,0:T(8,128)(2,1)S(1)}, u32[]{:S(2)}, u32[]{:S(2)}) collective-permute-start(bf16[4,3,32,128]{3,2,1,0:T(8,128)(2,1)S(1)} %get-tuple-element.54), channel_id=1, source_target_pairs={{0,2},{1,3},{2,0},{3,1},{4,6},{5,7},{6,4},{7,5},{8,10},{9,11},{10,... | collective-permute-start | bytes 294920 | tf_op jit(solution)/shard_map/ppermute | solution.py:46
  34.6 6.1 %collective-permute-start.5 = (bf16[4,3,32,128]{3,2,1,0:T(8,128)(2,1)S(1)}, bf16[4,3,32,128]{3,2,1,0:T(8,128)(2,1)S(1)}, u32[]{:S(2)}, u32[]{:S(2)}) collective-permute-start(bf16[4,3,32,128]{3,2,1,0:T(8,128)(2,1)S(1)} %get-tuple-element.55), channel_id=1, source_target_pairs={{0,3},{1,2},{2,1},{3,0},{4,7},{5,6},{6,5},{7,4},{8,11},{9,10},{10,... | collective-permute-start | bytes 294920 | tf_op jit(solution)/shard_map/ppermute | solution.py:46
  34.7 8.6 %collective-permute-start.6 = (bf16[4,3,32,128]{3,2,1,0:T(8,128)(2,1)S(1)}, bf16[4,3,32,128]{3,2,1,0:T(8,128)(2,1)S(1)}, u32[]{:S(2)}, u32[]{:S(2)}) collective-permute-start(bf16[4,3,32,128]{3,2,1,0:T(8,128)(2,1)S(1)} %get-tuple-element.56), channel_id=1, source_target_pairs={{0,4},{1,5},{2,6},{3,7},{4,0},{5,1},{6,2},{7,3},{8,12},{9,13},{10,... | collective-permute-start | bytes 294920 | tf_op jit(solution)/shard_map/ppermute | solution.py:46
  38.1 9.3 %collective-permute-start.7 = (bf16[4,3,32,128]{3,2,1,0:T(8,128)(2,1)S(1)}, bf16[4,3,32,128]{3,2,1,0:T(8,128)(2,1)S(1)}, u32[]{:S(2)}, u32[]{:S(2)}) collective-permute-start(bf16[4,3,32,128]{3,2,1,0:T(8,128)(2,1)S(1)} %get-tuple-element.57), channel_id=1, source_target_pairs={{0,5},{1,4},{2,7},{3,6},{4,1},{5,0},{6,3},{7,2},{8,13},{9,12},{10,... | collective-permute-start | bytes 294920 | tf_op jit(solution)/shard_map/ppermute | solution.py:46
  38.1 9.3 %collective-permute-start.8 = (bf16[4,3,32,128]{3,2,1,0:T(8,128)(2,1)S(1)}, bf16[4,3,32,128]{3,2,1,0:T(8,128)(2,1)S(1)}, u32[]{:S(2)}, u32[]{:S(2)}) collective-permute-start(bf16[4,3,32,128]{3,2,1,0:T(8,128)(2,1)S(1)} %get-tuple-element.58), channel_id=1, source_target_pairs={{0,6},{1,7},{2,4},{3,5},{4,2},{5,3},{6,0},{7,1},{8,14},{9,15},{10,... | collective-permute-start | bytes 294920 | tf_op jit(solution)/shard_map/ppermute | solution.py:46
  40.0 7.5 %collective-permute-start.9 = (bf16[4,3,32,128]{3,2,1,0:T(8,128)(2,1)S(1)}, bf16[4,3,32,128]{3,2,1,0:T(8,128)(2,1)S(1)}, u32[]{:S(2)}, u32[]{:S(2)}) collective-permute-start(bf16[4,3,32,128]{3,2,1,0:T(8,128)(2,1)S(1)} %get-tuple-element.59), channel_id=1, source_target_pairs={{0,7},{1,6},{2,5},{3,4},{4,3},{5,2},{6,1},{7,0},{8,15},{9,14},{10,... | collective-permute-start | bytes 294920 | tf_op jit(solution)/shard_map/ppermute | solution.py:46
  40.8 25.2 %collective-permute-start.28 = (bf16[8,6,32,256]{3,2,1,0:T(8,128)(2,1)S(1)}, bf16[8,6,32,256]{3,2,1,0:T(8,128)(2,1)S(1)}, u32[]{:S(2)}, u32[]{:S(2)}) collective-permute-start(bf16[8,6,32,256]{3,2,1,0:T(8,128)(2,1)S(1)} %shard_map.102.own_ref), channel_id=1, source_target_pairs={{0,24},{1,25},{2,26},{3,27},{4,28},{5,29},{6,30},{7,31},{8,0},{9,1... | collective-permute-start | bytes 2359304 | tf_op jit(solution)/shard_map/ppermute | solution.py:23
  43.3 37.2 %collective-permute-start.27 = (bf16[8,6,32,256]{3,2,1,0:T(8,128)(2,1)S(1)}, bf16[8,6,32,256]{3,2,1,0:T(8,128)(2,1)S(1)}, u32[]{:S(2)}, u32[]{:S(2)}) collective-permute-start(bf16[8,6,32,256]{3,2,1,0:T(8,128)(2,1)S(1)} %shard_map.102.own_ref), channel_id=1, source_target_pairs={{0,8},{1,9},{2,10},{3,11},{4,12},{5,13},{6,14},{7,15},{8,16},{9,17... | collective-permute-start | bytes 2359304 | tf_op jit(solution)/shard_map/ppermute | solution.py:23
  49.4 5.7 %collective-permute-start.11 = (bf16[4,3,32,128]{3,2,1,0:T(8,128)(2,1)S(1)}, bf16[4,3,32,128]{3,2,1,0:T(8,128)(2,1)S(1)}, u32[]{:S(2)}, u32[]{:S(2)}) collective-permute-start(bf16[4,3,32,128]{3,2,1,0:T(8,128)(2,1)S(1)} %get-tuple-element.62), channel_id=1, source_target_pairs={{0,2},{1,3},{2,0},{3,1},{4,6},{5,7},{6,4},{7,5},{8,10},{9,11},{10,... | collective-permute-start | bytes 294920 | tf_op jit(solution)/shard_map/ppermute | solution.py:46
  51.0 6.8 %collective-permute-start.13 = (bf16[4,3,32,128]{3,2,1,0:T(8,128)(2,1)S(1)}, bf16[4,3,32,128]{3,2,1,0:T(8,128)(2,1)S(1)}, u32[]{:S(2)}, u32[]{:S(2)}) collective-permute-start(bf16[4,3,32,128]{3,2,1,0:T(8,128)(2,1)S(1)} %get-tuple-element.64), channel_id=1, source_target_pairs={{0,4},{1,5},{2,6},{3,7},{4,0},{5,1},{6,2},{7,3},{8,12},{9,13},{10,... | collective-permute-start | bytes 294920 | tf_op jit(solution)/shard_map/ppermute | solution.py:46
  55.6 6.3 %collective-permute-start.15 = (bf16[4,3,32,128]{3,2,1,0:T(8,128)(2,1)S(1)}, bf16[4,3,32,128]{3,2,1,0:T(8,128)(2,1)S(1)}, u32[]{:S(2)}, u32[]{:S(2)}) collective-permute-start(bf16[4,3,32,128]{3,2,1,0:T(8,128)(2,1)S(1)} %get-tuple-element.66), channel_id=1, source_target_pairs={{0,6},{1,7},{2,4},{3,5},{4,2},{5,3},{6,0},{7,1},{8,14},{9,15},{10,... | collective-permute-start | bytes 294920 | tf_op jit(solution)/shard_map/ppermute | solution.py:46
  57.7 6.7 %collective-permute-start.16 = (bf16[4,3,32,128]{3,2,1,0:T(8,128)(2,1)S(1)}, bf16[4,3,32,128]{3,2,1,0:T(8,128)(2,1)S(1)}, u32[]{:S(2)}, u32[]{:S(2)}) collective-permute-start(bf16[4,3,32,128]{3,2,1,0:T(8,128)(2,1)S(1)} %get-tuple-element.67), channel_id=1, source_target_pairs={{0,7},{1,6},{2,5},{3,4},{4,3},{5,2},{6,1},{7,0},{8,15},{9,14},{10,... | collective-permute-start | bytes 294920 | tf_op jit(solution)/shard_map/ppermute | solution.py:46
  64.5 19.5 %collective-permute-start.19 = (bf16[8,3,32,128]{3,2,1,0:T(8,128)(2,1)S(1)}, bf16[8,3,32,128]{3,2,1,0:T(8,128)(2,1)S(1)}, u32[]{:S(2)}, u32[]{:S(2)}) collective-permute-start(bf16[8,3,32,128]{3,2,1,0:T(8,128)(2,1)S(1)} %get-tuple-element.71), channel_id=1, source_target_pairs={{0,8},{1,9},{2,10},{3,11},{4,12},{5,13},{6,14},{7,15},{8,0},{9,1},... | collective-permute-start | bytes 589832 | tf_op jit(solution)/shard_map/ppermute | solution.py:28
  82.0 5.7 %collective-permute-start.30 = (bf16[6,32,256]{2,1,0:T(8,128)(2,1)S(1)}, bf16[6,32,256]{2,1,0:T(8,128)(2,1)S(1)}, u32[]{:S(2)}, u32[]{:S(2)}) collective-permute-start(bf16[6,32,256]{2,1,0:T(8,128)(2,1)S(1)} %get-tuple-element.84), channel_id=1, source_target_pairs={{0,2},{1,3},{2,0},{3,1},{4,6},{5,7},{6,4},{7,5},{8,10},{9,11},{10,... | collective-permute-start | bytes 294920 | tf_op jit(solution)/shard_map/ppermute | solution.py:46
  82.8 5.9 %collective-permute-start.31 = (bf16[6,32,256]{2,1,0:T(8,128)(2,1)S(1)}, bf16[6,32,256]{2,1,0:T(8,128)(2,1)S(1)}, u32[]{:S(2)}, u32[]{:S(2)}) collective-permute-start(bf16[6,32,256]{2,1,0:T(8,128)(2,1)S(1)} %get-tuple-element.85), channel_id=1, source_target_pairs={{0,3},{1,2},{2,1},{3,0},{4,7},{5,6},{6,5},{7,4},{8,11},{9,10},{10,... | collective-permute-start | bytes 294920 | tf_op jit(solution)/shard_map/ppermute | solution.py:46
  83.8 5.7 %collective-permute-start.32 = (bf16[6,32,256]{2,1,0:T(8,128)(2,1)S(1)}, bf16[6,32,256]{2,1,0:T(8,128)(2,1)S(1)}, u32[]{:S(2)}, u32[]{:S(2)}) collective-permute-start(bf16[6,32,256]{2,1,0:T(8,128)(2,1)S(1)} %get-tuple-element.86), channel_id=1, source_target_pairs={{0,4},{1,5},{2,6},{3,7},{4,0},{5,1},{6,2},{7,3},{8,12},{9,13},{10,... | collective-permute-start | bytes 294920 | tf_op jit(solution)/shard_map/ppermute | solution.py:46
  84.0 12.6 %collective-permute-start.33 = (bf16[6,32,256]{2,1,0:T(8,128)(2,1)S(1)}, bf16[6,32,256]{2,1,0:T(8,128)(2,1)S(1)}, u32[]{:S(2)}, u32[]{:S(2)}) collective-permute-start(bf16[6,32,256]{2,1,0:T(8,128)(2,1)S(1)} %get-tuple-element.87), channel_id=1, source_target_pairs={{0,5},{1,4},{2,7},{3,6},{4,1},{5,0},{6,3},{7,2},{8,13},{9,12},{10,... | collective-permute-start | bytes 294920 | tf_op jit(solution)/shard_map/ppermute | solution.py:46
  85.5 11.1 %collective-permute-start.34 = (bf16[6,32,256]{2,1,0:T(8,128)(2,1)S(1)}, bf16[6,32,256]{2,1,0:T(8,128)(2,1)S(1)}, u32[]{:S(2)}, u32[]{:S(2)}) collective-permute-start(bf16[6,32,256]{2,1,0:T(8,128)(2,1)S(1)} %get-tuple-element.88), channel_id=1, source_target_pairs={{0,6},{1,7},{2,4},{3,5},{4,2},{5,3},{6,0},{7,1},{8,14},{9,15},{10,... | collective-permute-start | bytes 294920 | tf_op jit(solution)/shard_map/ppermute | solution.py:46
  87.7 9.0 %collective-permute-start.35 = (bf16[6,32,256]{2,1,0:T(8,128)(2,1)S(1)}, bf16[6,32,256]{2,1,0:T(8,128)(2,1)S(1)}, u32[]{:S(2)}, u32[]{:S(2)}) collective-permute-start(bf16[6,32,256]{2,1,0:T(8,128)(2,1)S(1)} %get-tuple-element.89), channel_id=1, source_target_pairs={{0,7},{1,6},{2,5},{3,4},{4,3},{5,2},{6,1},{7,0},{8,15},{9,14},{10,... | collective-permute-start | bytes 294920 | tf_op jit(solution)/shard_map/ppermute | solution.py:46
  88.7 16.6 %collective-permute-start.17 = (bf16[8,3,32,128]{3,2,1,0:T(8,128)(2,1)S(1)}, bf16[8,3,32,128]{3,2,1,0:T(8,128)(2,1)S(1)}, u32[]{:S(2)}, u32[]{:S(2)}) collective-permute-start(bf16[8,3,32,128]{3,2,1,0:T(8,128)(2,1)S(1)} %get-tuple-element.68), channel_id=1, source_target_pairs={{0,16},{1,17},{2,18},{3,19},{4,20},{5,21},{6,22},{7,23},{8,24},{9,... | collective-permute-start | bytes 589832 | tf_op jit(solution)/shard_map/ppermute | solution.py:28
  89.5 15.9 %collective-permute-start.18 = (bf16[8,3,32,128]{3,2,1,0:T(8,128)(2,1)S(1)}, bf16[8,3,32,128]{3,2,1,0:T(8,128)(2,1)S(1)}, u32[]{:S(2)}, u32[]{:S(2)}) collective-permute-start(bf16[8,3,32,128]{3,2,1,0:T(8,128)(2,1)S(1)} %get-tuple-element.69), channel_id=1, source_target_pairs={{0,24},{1,25},{2,26},{3,27},{4,28},{5,29},{6,30},{7,31},{8,16},{9,... | collective-permute-start | bytes 589832 | tf_op jit(solution)/shard_map/ppermute | solution.py:28
  (11 other events, 68.4 us)

commit v3 on v2

v3 whole, which is shorter than its diff:
```python
import functools

import jax
import jax.numpy as jnp
from jax import lax
from jax.experimental import pallas as pl
from jax.experimental.pallas import tpu as pltpu
from jax.sharding import PartitionSpec as P

LANES = 128
BLOCK = 512
VMEM = pl.BlockSpec(memory_space=pltpu.VMEM)
SMEM = pl.BlockSpec(memory_space=pltpu.SMEM)
HBM = pl.BlockSpec(memory_space=pltpu.HBM)


def team_size(count, rows, reach):
    for size in range(1, count + 1):
        if count % size == 0 and rows * size >= reach:
            return size
    return count


def shifted(value, team, by):
    count = lax.axis_size("span")
    return lax.ppermute(value, "span", [(i, (i + by * team) % count) for i in range(count)])


def crossed(value, team, x):
    count = lax.axis_size("span")
    return lax.ppermute(value, "span", [(i, (i // team ^ x) * team + i % team) for i in range(count)])


def crossing(pieces, team):
    return [pieces[0]] + [crossed(pieces[x], team, x) for x in range(1, len(pieces))]


def within(value, team):
    count = lax.axis_size("span")
    teams = [[first + i for i in range(team)] for first in range(0, count, team)]
    return lax.all_to_all(value, "span", 0, 0, axis_index_groups=teams, tiled=True)


def direct(pieces):
    count = lax.axis_size("span")
    order = sorted(range(1, len(pieces)), key=lambda x: -x)
    got = list(pieces)
    for x in order:
        got[x] = lax.ppermute(pieces[x], "span", [(i, i ^ x) for i in range(count)])
    return got


def placed(body, team):
    def wrapped(index_ref, *refs):
        body((lax.div(index_ref[0], jnp.int32(team)), lax.rem(index_ref[0], jnp.int32(team))), *refs)

    return wrapped


def kernel_call(body, inputs, outputs, in_specs=None, out_specs=None, scratch=(), flops=1e6, limit=16 << 20):
    moved = sum(a.size * a.dtype.itemsize for a in (*inputs, *outputs))
    return pl.pallas_call(
        body,
        in_specs=in_specs or [VMEM] * len(inputs),
        out_specs=out_specs or [VMEM] * len(outputs),
        out_shape=outputs,
        scratch_shapes=scratch,
        cost_estimate=pl.CostEstimate(flops=int(flops), bytes_accessed=moved, transcendentals=0),
        compiler_params=pltpu.CompilerParams(vmem_limit_bytes=limit),
    )(*inputs)


def band_kernel(taps_ref, band_ref):
    height, length = band_ref.shape
    spread = jnp.broadcast_to(taps_ref[...], (height, length))
    band_ref[...] = pltpu.roll(spread, 0, 1, stride=1, stride_axis=0).astype(jnp.bfloat16)


def band_of(taps, height, reach):
    lead = height - reach
    padded = jnp.pad(taps.astype(jnp.float32), (lead, 3 * height - lead - taps.shape[0]))
    shape = jax.ShapeDtypeStruct((height, 3 * height), jnp.bfloat16)
    return kernel_call(band_kernel, [padded[None]], [shape])[0]


def pack_kernel(early, groups, place, slabs_ref, *refs):
    far_ref, near_ref, turned_ref = refs[-3:]
    rows, parts, planes, width = slabs_ref.shape
    strip = near_ref.shape[3]
    slots = width // groups // LANES

    @pl.loop(0, parts)
    def _(part):
        for column in range(width // LANES):
            at = slice(column * LANES, (column + 1) * LANES)
            held = turned_ref.at[column]
            for row in range(rows):
                held[pl.ds(row, planes, stride=rows), :] = slabs_ref[row, part, :, at].astype(jnp.float32)
            member, inner = divmod(column * LANES, strip)
            group, slot = divmod(column, slots)
            for plane in range(planes):
                value = held[plane * rows : (plane + 1) * rows, :].astype(jnp.bfloat16)
                if plane < early:
                    near_ref[member, plane * parts + part, :, inner : inner + LANES] = value
                else:
                    far_ref[group, place[1] ^ ((plane - early) * slots + slot), part] = value

    for k in range(groups):
        refs[k][...] = far_ref[place[0] ^ k]
    for x, ref in enumerate(refs[groups:-3]):
        ref[...] = near_ref[place[1] ^ x]


def fetch_kernel(wall_ref, held_ref, sems):
    rows = wall_ref.shape[0] // sems.shape[0]
    copies = []
    for i in range(sems.shape[0]):
        at = pl.ds(i * rows, rows)
        copies.append(pltpu.make_async_copy(wall_ref.at[at], held_ref.at[at], sems.at[i]))
        copies[-1].start()
    for copy in copies:
        copy.wait()


def join_kernel(*refs):
    for x, ref in enumerate(refs[:-1]):
        refs[-1][x] = ref[...]


def swap_kernel(count, *refs):
    for k, ref in enumerate(refs[:count]):
        for x, out_ref in enumerate(refs[count:]):
            out_ref[k] = ref[x]


def banded(band_ref, blocks):
    height = band_ref.shape[0]
    total = None
    for i, block in enumerate(blocks):
        block = block.reshape(height, block.shape[-1])
        part = jnp.dot(band_ref[:, i * height : (i + 1) * height], block, preferred_element_type=jnp.float32)
        total = part if total is None else total + part
    return total


def near_rows(member, band_ref, before_ref, own_ref, after_ref, out_ref):
    team = own_ref.shape[0]
    for u in range(own_ref.shape[1]):
        blocks = [
            jnp.concatenate([ref[member ^ i, u] for i in range(team)], axis=0) for ref in (before_ref, own_ref, after_ref)
        ]
        out_ref[:, u] = banded(band_ref, blocks).astype(out_ref.dtype).reshape(out_ref[:, u].shape)


def near_kernel(band_ref, before_ref, after_ref, own_ref, out_ref):
    near_rows(0, band_ref, before_ref, own_ref, after_ref, out_ref)


def near_split_kernel(place, band_ref, before_ref, after_ref, own_ref, *refs):
    near_rows(place[1], band_ref, before_ref, own_ref, after_ref, refs[-1])
    for x, ref in enumerate(refs[:-1]):
        ref[...] = refs[-1][place[1] ^ x]


def far_kernel(team, place, band_ref, *refs):
    held_ref, out_ref = refs[2 * team :]
    groups, units = held_ref.shape[1:3]
    me, member = place[0], place[1]
    height = band_ref.shape[0]
    for x in range(team):
        held_ref[member ^ x] = refs[x][...]
    for q in range(groups):
        blocks = []
        for i in range(3):
            slot = me ^ ((q + i - 1) % groups)
            wide = [held_ref[:, slot, u].reshape(height, LANES) for u in range(units)]
            blocks.append(jnp.concatenate(wide, axis=1))
        total = banded(band_ref, blocks).astype(out_ref.dtype)
        for u in range(units):
            out_ref[:, me ^ q, u] = total[:, u * LANES : (u + 1) * LANES].reshape(team, -1, LANES)
    for x in range(team):
        refs[team + x][...] = out_ref[member ^ x]


def contract(rows, wall):
    return lax.dot_general(rows, wall, (((1,), (1,)), ((), ())), preferred_element_type=jnp.float32)


def advance(state, fresh, at, scale_ref, mean_ref, diag_ref, off_ref):
    def line(ref, i):
        return ref[i : i + 1, at]

    for i in range(len(state)):
        scale = line(scale_ref, i)
        decay = jnp.exp(-jnp.pi / (2.0 * scale))
        inject = jnp.sqrt(1.0 - jnp.exp(-jnp.pi / scale))
        state[i] = decay * state[i] + inject * fresh[i]
    along, normal, spanwise = state
    first = line(mean_ref, 0) + line(diag_ref, 0) * along
    second = line(off_ref, 0) * along + line(diag_ref, 1) * normal
    third = line(off_ref, 1) * along + line(off_ref, 2) * normal + line(diag_ref, 2) * spanwise
    return state, (first, second, third)


def far_rows(member, ref, late, slot):
    slots = ref.shape[0] // late
    pair = [
        jnp.concatenate([ref[member ^ (p * slots + slot + i)].reshape(-1, LANES) for i in range(2)], axis=1) for p in range(late)
    ]
    return jnp.concatenate(pair, axis=0)


def far_sum(place, refs, order, late, wall_ref, at, total):
    for k, ref in zip(order, refs):
        slots = ref.shape[0] // late
        for slot in range(0, slots, 2):
            where = pl.multiple_of((place[0] ^ k) * (slots * LANES) + slot * LANES, 2 * LANES)
            part = contract(far_rows(place[1], ref, late, slot), wall_ref[at, pl.ds(where, 2 * LANES)])
            total = part if total is None else total + part
    return total


def far_start_kernel(late, place, own_ref, next_ref, wall_ref, sum_ref):
    width = wall_ref.shape[0]
    block = 2 * LANES
    for start in range(0, width, block):
        at = slice(start, start + block)
        sum_ref[:, at] = far_sum(place, [own_ref, next_ref], [0, 1], late, wall_ref, at, None)


def wall_kernel(late, team, place, *refs):
    near_refs, far_refs = refs[:team], refs[team:-15]
    sum_ref, wall_ref, state_ref, scale_ref, mean_ref, diag_ref, off_ref, velocity_ref, last_ref = refs[-15:-6]
    rows_ref, sums_ref, turned_ref, speed_ref, final_ref, sems = refs[-6:]
    units, rows, strip = near_refs[0].shape
    parts, _, width = state_ref.shape
    planes = velocity_ref.shape[2]
    block = sums_ref.shape[1]
    tiles = block // LANES
    slots = far_refs[0].shape[0] // late
    quarter = slots * LANES
    first = units * rows

    for x, ref in enumerate(near_refs):
        where = pl.multiple_of((place[1] ^ x) * strip, strip)
        rows_ref[:first, pl.ds(where, strip)] = ref[...].reshape(first, strip)
    done = width // quarter - len(far_refs)
    for k, ref in enumerate(far_refs):
        for slot in range(0, slots, 2):
            where = pl.multiple_of((place[0] ^ (done + k)) * quarter + slot * LANES, 2 * LANES)
            rows_ref[first:, pl.ds(where, 2 * LANES)] = far_rows(place[1], ref, late, slot)

    copies = []
    for step, start in enumerate(range(0, width, block)):
        at = slice(start, start + block)
        both = near = None
        for k in range(width // quarter):
            where = pl.ds(pl.multiple_of((place[0] ^ k) * quarter, quarter), quarter)
            if k < done:
                part = contract(rows_ref[:first, where], wall_ref[at, where])
                near = part if near is None else near + part
            else:
                part = contract(rows_ref[:, where], wall_ref[at, where])
                both = part if both is None else both + part
        sums_ref[:first] = both[:first] + near
        sums_ref[first:] = both[first:] + sum_ref[:, at]
        state = [state_ref[i, :, at] for i in range(parts)]
        for plane in range(planes):
            fresh = [sums_ref[(plane * parts + i) * rows :][:rows] for i in range(parts)]
            state, speeds = advance(state, fresh, at, scale_ref, mean_ref, diag_ref, off_ref)
            for i in range(parts):
                for j in range(tiles):
                    value = speeds[i][:, j * LANES : (j + 1) * LANES]
                    turned_ref[i, j, pl.ds(plane, rows, stride=planes), :] = value
        for i in range(parts):
            final_ref[i, :, at] = state[i]
            for j in range(tiles):
                lanes = slice(start + j * LANES, start + (j + 1) * LANES)
                for row in range(rows):
                    column = turned_ref[i, j, row * planes : (row + 1) * planes, :]
                    speed_ref[row, i, :, lanes] = column.astype(speed_ref.dtype)
        here = pltpu.make_async_copy(speed_ref.at[:, :, :, at], velocity_ref.at[:, :, :, at], sems.at[0, step])
        here.start()
        also = pltpu.make_async_copy(final_ref.at[:, :, at], last_ref.at[:, :, at], sems.at[1, step])
        also.start()
        copies += [here, also]
    for copy in copies:
        copy.wait()


def plain(slabs, band, wall_filter, prev_state, time_scale, mean_velocity, lund_diag, lund_off):
    rows, planes, parts, width = slabs.shape
    height = band.shape[0]
    team = height // rows
    strip = width // team
    near = slabs.reshape(rows, planes, parts, team, strip).transpose(3, 1, 2, 0, 4)
    near = within(near.reshape(team, planes * parts, rows, strip), team)
    after = shifted(near, team, -1)
    before = shifted(near, team, 1)
    shape = jax.ShapeDtypeStruct(near.shape, near.dtype)
    near = kernel_call(near_kernel, [band, before, after, near], [shape], limit=32 << 20)[0]
    near = within(near, team).reshape(team, planes, parts, rows, strip)
    near = near.transpose(1, 2, 3, 0, 4).reshape(planes, parts, rows, width)
    filtered = lax.dot_general(near, wall_filter, (((3,), (1,)), ((), ())), preferred_element_type=jnp.float32)
    decay = jnp.exp(-jnp.pi / (2.0 * time_scale))[:, None]
    inject = jnp.sqrt(1.0 - jnp.exp(-jnp.pi / time_scale))[:, None]
    state = prev_state.transpose(1, 0, 2)
    outputs = []
    for plane in range(planes):
        state = decay * state + inject * filtered[plane]
        first = mean_velocity + lund_diag[0] * state[0]
        second = lund_off[0] * state[0] + lund_diag[1] * state[1]
        third = lund_off[1] * state[0] + lund_off[2] * state[1] + lund_diag[2] * state[2]
        outputs.append(jnp.stack([first, second, third]).astype(jnp.bfloat16))
    return (jnp.stack(outputs).transpose(2, 0, 1, 3), state.transpose(1, 0, 2))


def body(
    random_slabs,
    span_weights,
    wall_filter,
    prev_state,
    time_scale,
    mean_velocity,
    lund_diag,
    lund_off,
):
    rows, planes, parts, width = random_slabs.shape
    reach = (span_weights.shape[0] - 1) // 2
    count = lax.axis_size("span")
    team = team_size(count, rows, reach)
    groups = count // team
    height = rows * team
    scaling = jnp.sqrt(jnp.sum(span_weights * span_weights))
    taps = (span_weights / scaling).astype(jnp.bfloat16)
    band = band_of(taps, height, reach)
    place = lax.axis_index("span").astype(jnp.int32)[None]

    late = planes // 2
    if width != groups * (team // late) * LANES or groups > 4:
        return plain(random_slabs, band, wall_filter, prev_state, time_scale, mean_velocity, lund_diag, lund_off)
    early = planes - late
    strip = width // team
    units = early * parts
    slabs = random_slabs.transpose(0, 2, 1, 3)
    state = prev_state.transpose(1, 0, 2)
    lines = [time_scale, mean_velocity[None], lund_diag, lund_off]
    shape = jax.ShapeDtypeStruct

    packed = kernel_call(
        placed(functools.partial(pack_kernel, early, groups), team),
        [place, slabs],
        [shape((team, parts, rows, LANES), slabs.dtype)] * groups + [shape((units, rows, strip), slabs.dtype)] * team,
        in_specs=[SMEM, VMEM],
        scratch=[
            pltpu.VMEM((groups, team, parts, rows, LANES), slabs.dtype),
            pltpu.VMEM((team, units, rows, strip), slabs.dtype),
            pltpu.VMEM((width // LANES, planes * rows, LANES), jnp.float32),
        ],
    )
    far, near = packed[:groups], packed[groups:]
    far = crossing(far, team)
    near = direct(near)
    near = kernel_call(join_kernel, near, [shape((team, units, rows, strip), slabs.dtype)])[0]
    after = shifted(near, team, -1)
    before = shifted(near, team, 1)
    pieces = [shape((groups, parts, rows, LANES), slabs.dtype)] * team
    far = kernel_call(lambda *refs: swap_kernel(groups, *refs), far, pieces)
    far = direct(far)
    wall = kernel_call(
        fetch_kernel,
        [wall_filter],
        [shape(wall_filter.shape, wall_filter.dtype)],
        in_specs=[HBM],
        scratch=[pltpu.SemaphoreType.DMA((4,))],
        limit=42 << 20,
    )[0]
    far = kernel_call(
        placed(functools.partial(far_kernel, team), team),
        [place, band, *far],
        pieces,
        in_specs=[SMEM] + [VMEM] * (1 + team),
        scratch=[pltpu.VMEM((team, *pieces[0].shape), slabs.dtype)] * 2,
        flops=2 * band.size * groups * team * parts * rows * LANES // rows,
    )
    far = direct(far)
    far = kernel_call(
        lambda *refs: swap_kernel(team, *refs), far, [shape((team, parts, rows, LANES), slabs.dtype)] * groups
    )
    near = kernel_call(
        placed(near_split_kernel, team),
        [place, band, before, after, near],
        [shape(near.shape[1:], near.dtype)] * team,
        in_specs=[SMEM] + [VMEM] * 4,
        scratch=[pltpu.VMEM(near.shape, near.dtype)],
        flops=2 * band.size * near.size // height,
    )
    near = direct(near)
    far = crossing(far, team)
    sums = kernel_call(
        placed(functools.partial(far_start_kernel, late), team),
        [place, far[0], far[1], wall],
        [shape((late * parts * rows, width), jnp.float32)],
        in_specs=[SMEM, VMEM, VMEM, VMEM],
        flops=wall_filter.size * late * parts * rows,
    )[0]
    block = BLOCK
    velocity, state = kernel_call(
        placed(functools.partial(wall_kernel, late, team), team),
        [place, *near, *far[2:], sums, wall, state, *lines],
        [shape(slabs.shape, slabs.dtype), shape(state.shape, state.dtype)],
        in_specs=[SMEM] + [VMEM] * (team + groups - 2 + 7),
        out_specs=[HBM, HBM],
        scratch=[
            pltpu.VMEM((planes * parts * rows, width), slabs.dtype),
            pltpu.VMEM((planes * parts * rows, block), jnp.float32),
            pltpu.VMEM((parts, block // LANES, planes * rows, LANES), jnp.float32),
            pltpu.VMEM(slabs.shape, slabs.dtype),
            pltpu.VMEM(state.shape, state.dtype),
            pltpu.SemaphoreType.DMA((2, width // block)),
        ],
        flops=2 * wall_filter.size * planes * parts * rows,
    )
    return (velocity.transpose(0, 2, 1, 3), state.transpose(1, 0, 2))


def solution(mesh):
    placed = (P("span", None, None, None), P(), P(), P("span", None, None), P(), P(), P(), P())
    return jax.shard_map(
        body,
        mesh=mesh,
        in_specs=placed,
        out_specs=(P("span", None, None, None), P("span", None, None)),
        check_vma=False,
    )
```

time: 112 us -> 111 us (level)
  Pallas kernels: 22.6 us -> 15 us
  waiting for transfers between devices: 46.2 us -> 51.9 us
  starting transfers between devices: 37.7 us -> 39.2 us
    ppermute x6, waiting for transfers between devices: 14.4 us -> 23 us  [crossed(): lax.ppermute(value, 'span', [(i, (i // team ^ x) * team + i % team) for i...]
    pallas_call x11 -> x10, Pallas kernels: 22.6 us -> 15 us  [kernel_call(): pl.pallas_call(body, in_specs=in_specs or [VMEM] * len(inputs), out_specs...]
    ppermute x2, waiting for transfers between devices: 14.5 us -> 12.8 us  [shifted(): lax.ppermute(value, 'span', [(i, (i + by * team) % count) for i in range(...]
    ppermute x28, waiting for transfers between devices: 17.3 us -> 16.1 us  [direct(): got[x] = lax.ppermute(pieces[x], 'span', [(i, i ^ x) for i in range(count)])]
  transfers between devices with their start and end apart: 36 -> 36, of which waited for: 15 -> 12; matrix products, arithmetic and copies ran while one was open for 1% -> 1% of each run, Pallas kernels for 14% -> 7%
where the time goes in v3:
time: 111 us; the launch traced here: 110 us
  waiting for transfers between devices  51.9 us (47%)
  starting transfers between devices  39.2 us (35%)
  Pallas kernels  15 us (14%)
  between operations  1.57 us (1%)
  local copies, waits for them, and re-layouts  1.45 us (1%)
    ppermute x28, starting transfers between devices, direct(): got[x] = lax.ppermute(pieces[x], 'span', [(i, i ^ x) for i in range(count)])  26.6 us
    ppermute x6, waiting for transfers between devices, crossed(): lax.ppermute(value, 'span', [(i, (i // team ^ x) * team + i % team) for i...  23 us
    ppermute x28, waiting for transfers between devices, direct(): got[x] = lax.ppermute(pieces[x], 'span', [(i, i ^ x) for i in range(count)])  16.1 us
    pallas_call x10, Pallas kernels, kernel_call(): pl.pallas_call(body, in_specs=in_specs or [VMEM] * len(inputs), out_specs...  15 us
    ppermute x2, waiting for transfers between devices, shifted(): lax.ppermute(value, 'span', [(i, (i + by * team) % count) for i in range(...  12.8 us
    ppermute x6, starting transfers between devices, crossed(): lax.ppermute(value, 'span', [(i, (i // team ^ x) * team + i % team) for i...  9.58 us
    ppermute x2, starting transfers between devices, shifted(): lax.ppermute(value, 'span', [(i, (i + by * team) % count) for i in range(...  3.03 us
  transfers between devices with their start and end apart: 36, of which 12 were waited for; matrix products, arithmetic and copies ran while one was open for 1% of the time, Pallas kernels for 7%

profile of v3, /device:TPU:0, one launch (start us, length us, event | category | flops | bytes accessed | tf_op | source)
XLA Modules:
  0.0 109.7 jit_solution(18358273004140570262)
XLA Ops:
  0.7 1.4 %copy-done = bf16[32,4,3,2048]{3,1,2,0:T(4,128)(2,1)S(1)} copy-done((bf16[32,4,3,2048]{3,1,2,0:T(4,128)(2,1)S(1)}, bf16[32,4,3,2048]{3,1,2,0:T(4,128)(2,1)}, u32[]{:S(2)}) %copy-start) | copy-done | bytes 1572888
  2.1 2.4 %shard_map.96 = (bf16[8,3,32,128]{3,2,1,0:T(8,128)(2,1)S(1)}, bf16[8,3,32,128]{3,2,1,0:T(8,128)(2,1)S(1)}, bf16[8,3,32,128]{3,2,1,0:T(8,128)(2,1)S(1)}, bf16[8,3...) custom-call(s32[1]{0:T(128)} %bitcast.index_ref, ...), custom_call_target="tpu_custom_call" | custom-call | flops 1000000 | bytes 3145732 | tf_op jit(solution)/shard_map/pallas_call | solution.py:62
  4.4 3.1 %collective-permute-start.16 = (bf16[8,3,32,128]{3,2,1,0:T(8,128)(2,1)S(1)}, bf16[8,3,32,128]{3,2,1,0:T(8,128)(2,1)S(1)}, u32[]{:S(2)}, u32[]{:S(2)}) collective-permute-start(bf16[8,3,32,128]{3,2,1,0:T(8,128)(2,1)S(1)} %get-tuple-element.61), channel_id=1, source_target_pairs={{0,8},{1,9},{2,10},{3,11},{4,12},{5,13},{6,14},{7,15},{8,0},{9,1},... | collective-permute-start | bytes 589832 | tf_op jit(solution)/shard_map/ppermute | solution.py:31
  7.6 2.6 %collective-permute-start.17 = (bf16[8,3,32,128]{3,2,1,0:T(8,128)(2,1)S(1)}, bf16[8,3,32,128]{3,2,1,0:T(8,128)(2,1)S(1)}, u32[]{:S(2)}, u32[]{:S(2)}) collective-permute-start(bf16[8,3,32,128]{3,2,1,0:T(8,128)(2,1)S(1)} %get-tuple-element.62), channel_id=1, source_target_pairs={{0,16},{1,17},{2,18},{3,19},{4,20},{5,21},{6,22},{7,23},{8,24},{9,... | collective-permute-start | bytes 589832 | tf_op jit(solution)/shard_map/ppermute | solution.py:31
  10.2 1.7 %collective-permute-start.1 = (bf16[6,32,256]{2,1,0:T(8,128)(2,1)S(1)}, bf16[6,32,256]{2,1,0:T(8,128)(2,1)S(1)}, u32[]{:S(2)}, u32[]{:S(2)}) collective-permute-start(bf16[6,32,256]{2,1,0:T(8,128)(2,1)S(1)} %get-tuple-element.46), channel_id=1, source_target_pairs={{0,2},{1,3},{2,0},{3,1},{4,6},{5,7},{6,4},{7,5},{8,10},{9,11},{10,... | collective-permute-start | bytes 294920 | tf_op jit(solution)/shard_map/ppermute | solution.py:49
  11.9 4.1 %collective-permute-done.16.refs_1_ = bf16[8,3,32,128]{3,2,1,0:T(8,128)(2,1)S(1)} collective-permute-done((bf16[8,3,32,128]{3,2,1,0:T(8,128)(2,1)S(1)}, bf16[8,3,32,128]{3,2,1,0:T(8,128)(2,1)S(1)}, u32[]{:S(2)}, u32[]{:S(2)}) %collective-permute-start.16) | collective-permute-done | bytes 196640 | tf_op jit(solution)/shard_map/ppermute | solution.py:31
  15.9 8.7 %collective-permute-done.17.refs_2_ = bf16[8,3,32,128]{3,2,1,0:T(8,128)(2,1)S(1)} collective-permute-done((bf16[8,3,32,128]{3,2,1,0:T(8,128)(2,1)S(1)}, bf16[8,3,32,128]{3,2,1,0:T(8,128)(2,1)S(1)}, u32[]{:S(2)}, u32[]{:S(2)}) %collective-permute-start.17) | collective-permute-done | bytes 196640 | tf_op jit(solution)/shard_map/ppermute | solution.py:31
  24.7 1.5 %collective-permute-start.3 = (bf16[6,32,256]{2,1,0:T(8,128)(2,1)S(1)}, bf16[6,32,256]{2,1,0:T(8,128)(2,1)S(1)}, u32[]{:S(2)}, u32[]{:S(2)}) collective-permute-start(bf16[6,32,256]{2,1,0:T(8,128)(2,1)S(1)} %get-tuple-element.48), channel_id=1, source_target_pairs={{0,4},{1,5},{2,6},{3,7},{4,0},{5,1},{6,2},{7,3},{8,12},{9,13},{10,... | collective-permute-start | bytes 294920 | tf_op jit(solution)/shard_map/ppermute | solution.py:49
  27.6 1.5 %collective-permute-start.5 = (bf16[6,32,256]{2,1,0:T(8,128)(2,1)S(1)}, bf16[6,32,256]{2,1,0:T(8,128)(2,1)S(1)}, u32[]{:S(2)}, u32[]{:S(2)}) collective-permute-start(bf16[6,32,256]{2,1,0:T(8,128)(2,1)S(1)} %get-tuple-element.50), channel_id=1, source_target_pairs={{0,6},{1,7},{2,4},{3,5},{4,2},{5,3},{6,0},{7,1},{8,14},{9,15},{10,... | collective-permute-start | bytes 294920 | tf_op jit(solution)/shard_map/ppermute | solution.py:49
  29.1 1.4 %collective-permute-start.6 = (bf16[6,32,256]{2,1,0:T(8,128)(2,1)S(1)}, bf16[6,32,256]{2,1,0:T(8,128)(2,1)S(1)}, u32[]{:S(2)}, u32[]{:S(2)}) collective-permute-start(bf16[6,32,256]{2,1,0:T(8,128)(2,1)S(1)} %get-tuple-element.51), channel_id=1, source_target_pairs={{0,7},{1,6},{2,5},{3,4},{4,3},{5,2},{6,1},{7,0},{8,15},{9,14},{10,... | collective-permute-start | bytes 294920 | tf_op jit(solution)/shard_map/ppermute | solution.py:49
  30.8 1.5 %collective-permute-start.20 = (bf16[4,3,32,128]{3,2,1,0:T(8,128)(2,1)S(1)}, bf16[4,3,32,128]{3,2,1,0:T(8,128)(2,1)S(1)}, u32[]{:S(2)}, u32[]{:S(2)}) collective-permute-start(bf16[4,3,32,128]{3,2,1,0:T(8,128)(2,1)S(1)} %get-tuple-element.66), channel_id=1, source_target_pairs={{0,2},{1,3},{2,0},{3,1},{4,6},{5,7},{6,4},{7,5},{8,10},{9,11},{10,... | collective-permute-start | bytes 294920 | tf_op jit(solution)/shard_map/ppermute | solution.py:49
  32.3 2.7 %collective-permute-done.4.refs_5_ = bf16[6,32,256]{2,1,0:T(8,128)(2,1)S(1)} collective-permute-done((bf16[6,32,256]{2,1,0:T(8,128)(2,1)S(1)}, bf16[6,32,256]{2,1,0:T(8,128)(2,1)S(1)}, u32[]{:S(2)}, u32[]{:S(2)}) %collective-permute-start.4) | collective-permute-done | bytes 98336 | tf_op jit(solution)/shard_map/ppermute | solution.py:49
  34.9 3.4 %collective-permute-start.22 = (bf16[4,3,32,128]{3,2,1,0:T(8,128)(2,1)S(1)}, bf16[4,3,32,128]{3,2,1,0:T(8,128)(2,1)S(1)}, u32[]{:S(2)}, u32[]{:S(2)}) collective-permute-start(bf16[4,3,32,128]{3,2,1,0:T(8,128)(2,1)S(1)} %get-tuple-element.68), channel_id=1, source_target_pairs={{0,4},{1,5},{2,6},{3,7},{4,0},{5,1},{6,2},{7,3},{8,12},{9,13},{10,... | collective-permute-start | bytes 294920 | tf_op jit(solution)/shard_map/ppermute | solution.py:49
  38.4 1.9 %collective-permute-start.24 = (bf16[4,3,32,128]{3,2,1,0:T(8,128)(2,1)S(1)}, bf16[4,3,32,128]{3,2,1,0:T(8,128)(2,1)S(1)}, u32[]{:S(2)}, u32[]{:S(2)}) collective-permute-start(bf16[4,3,32,128]{3,2,1,0:T(8,128)(2,1)S(1)} %get-tuple-element.70), channel_id=1, source_target_pairs={{0,6},{1,7},{2,4},{3,5},{4,2},{5,3},{6,0},{7,1},{8,14},{9,15},{10,... | collective-permute-start | bytes 294920 | tf_op jit(solution)/shard_map/ppermute | solution.py:49
  41.0 2.5 %collective-permute-start.8 = (bf16[8,6,32,256]{3,2,1,0:T(8,128)(2,1)S(1)}, bf16[8,6,32,256]{3,2,1,0:T(8,128)(2,1)S(1)}, u32[]{:S(2)}, u32[]{:S(2)}) collective-permute-start(bf16[8,6,32,256]{3,2,1,0:T(8,128)(2,1)S(1)} %shard_map.97.refs_3_), channel_id=1, source_target_pairs={{0,24},{1,25},{2,26},{3,27},{4,28},{5,29},{6,30},{7,31},{8,0},{9,1... | collective-permute-start | bytes 2359304 | tf_op jit(solution)/shard_map/ppermute | solution.py:26
  44.1 3.6 %collective-permute-done.23.refs_6_ = bf16[4,3,32,128]{3,2,1,0:T(8,128)(2,1)S(1)} collective-permute-done((bf16[4,3,32,128]{3,2,1,0:T(8,128)(2,1)S(1)}, bf16[4,3,32,128]{3,2,1,0:T(8,128)(2,1)S(1)}, u32[]{:S(2)}, u32[]{:S(2)}) %collective-permute-start.23) | collective-permute-done | bytes 98336 | tf_op jit(solution)/shard_map/ppermute | solution.py:49
  50.7 1.6 %collective-permute-start.29 = (bf16[4,3,32,128]{3,2,1,0:T(8,128)(2,1)S(1)}, bf16[4,3,32,128]{3,2,1,0:T(8,128)(2,1)S(1)}, u32[]{:S(2)}, u32[]{:S(2)}) collective-permute-start(bf16[4,3,32,128]{3,2,1,0:T(8,128)(2,1)S(1)} %get-tuple-element.76), channel_id=1, source_target_pairs={{0,4},{1,5},{2,6},{3,7},{4,0},{5,1},{6,2},{7,3},{8,12},{9,13},{10,... | collective-permute-start | bytes 294920 | tf_op jit(solution)/shard_map/ppermute | solution.py:49
  52.3 2.5 %collective-permute-done.27.refs_2_ = bf16[4,3,32,128]{3,2,1,0:T(8,128)(2,1)S(1)} collective-permute-done((bf16[4,3,32,128]{3,2,1,0:T(8,128)(2,1)S(1)}, bf16[4,3,32,128]{3,2,1,0:T(8,128)(2,1)S(1)}, u32[]{:S(2)}, u32[]{:S(2)}) %collective-permute-start.27) | collective-permute-done | bytes 98336 | tf_op jit(solution)/shard_map/ppermute | solution.py:49
  55.4 2.1 %collective-permute-start.31 = (bf16[4,3,32,128]{3,2,1,0:T(8,128)(2,1)S(1)}, bf16[4,3,32,128]{3,2,1,0:T(8,128)(2,1)S(1)}, u32[]{:S(2)}, u32[]{:S(2)}) collective-permute-start(bf16[4,3,32,128]{3,2,1,0:T(8,128)(2,1)S(1)} %get-tuple-element.78), channel_id=1, source_target_pairs={{0,6},{1,7},{2,4},{3,5},{4,2},{5,3},{6,0},{7,1},{8,14},{9,15},{10,... | collective-permute-start | bytes 294920 | tf_op jit(solution)/shard_map/ppermute | solution.py:49
  57.5 1.5 %collective-permute-start.32 = (bf16[4,3,32,128]{3,2,1,0:T(8,128)(2,1)S(1)}, bf16[4,3,32,128]{3,2,1,0:T(8,128)(2,1)S(1)}, u32[]{:S(2)}, u32[]{:S(2)}) collective-permute-start(bf16[4,3,32,128]{3,2,1,0:T(8,128)(2,1)S(1)} %get-tuple-element.79), channel_id=1, source_target_pairs={{0,7},{1,6},{2,5},{3,4},{4,3},{5,2},{6,1},{7,0},{8,15},{9,14},{10,... | collective-permute-start | bytes 294920 | tf_op jit(solution)/shard_map/ppermute | solution.py:49
  59.6 2.1 %collective-permute-done.31.refs_6_ = bf16[4,3,32,128]{3,2,1,0:T(8,128)(2,1)S(1)} collective-permute-done((bf16[4,3,32,128]{3,2,1,0:T(8,128)(2,1)S(1)}, bf16[4,3,32,128]{3,2,1,0:T(8,128)(2,1)S(1)}, u32[]{:S(2)}, u32[]{:S(2)}) %collective-permute-start.31) | collective-permute-done | bytes 98336 | tf_op jit(solution)/shard_map/ppermute | solution.py:49
  61.7 2.5 %collective-permute-done.32.refs_7_ = bf16[4,3,32,128]{3,2,1,0:T(8,128)(2,1)S(1)} collective-permute-done((bf16[4,3,32,128]{3,2,1,0:T(8,128)(2,1)S(1)}, bf16[4,3,32,128]{3,2,1,0:T(8,128)(2,1)S(1)}, u32[]{:S(2)}, u32[]{:S(2)}) %collective-permute-start.32) | collective-permute-done | bytes 98336 | tf_op jit(solution)/shard_map/ppermute | solution.py:49
  64.2 2.5 %collective-permute-start.33 = (bf16[8,3,32,128]{3,2,1,0:T(8,128)(2,1)S(1)}, bf16[8,3,32,128]{3,2,1,0:T(8,128)(2,1)S(1)}, u32[]{:S(2)}, u32[]{:S(2)}) collective-permute-start(bf16[8,3,32,128]{3,2,1,0:T(8,128)(2,1)S(1)} %get-tuple-element.80), channel_id=1, source_target_pairs={{0,16},{1,17},{2,18},{3,19},{4,20},{5,21},{6,22},{7,23},{8,24},{9,... | collective-permute-start | bytes 589832 | tf_op jit(solution)/shard_map/ppermute | solution.py:31
  66.7 1.3 %collective-permute-start.34 = (bf16[8,3,32,128]{3,2,1,0:T(8,128)(2,1)S(1)}, bf16[8,3,32,128]{3,2,1,0:T(8,128)(2,1)S(1)}, u32[]{:S(2)}, u32[]{:S(2)}) collective-permute-start(bf16[8,3,32,128]{3,2,1,0:T(8,128)(2,1)S(1)} %get-tuple-element.81), channel_id=1, source_target_pairs={{0,24},{1,25},{2,26},{3,27},{4,28},{5,29},{6,30},{7,31},{8,16},{9,... | collective-permute-start | bytes 589832 | tf_op jit(solution)/shard_map/ppermute | solution.py:31
  68.1 12.8 %collective-permute-done.7.refs_1_ = bf16[8,6,32,256]{3,2,1,0:T(8,128)(2,1)S(1)} collective-permute-done((bf16[8,6,32,256]{3,2,1,0:T(8,128)(2,1)S(1)}, bf16[8,6,32,256]{3,2,1,0:T(8,128)(2,1)S(1)}, u32[]{:S(2)}, u32[]{:S(2)}) %collective-permute-start.7) | collective-permute-done | bytes 786464 | tf_op jit(solution)/shard_map/ppermute | solution.py:26
  82.6 10.2 %collective-permute-done.33.refs_8_ = bf16[8,3,32,128]{3,2,1,0:T(8,128)(2,1)S(1)} collective-permute-done((bf16[8,3,32,128]{3,2,1,0:T(8,128)(2,1)S(1)}, bf16[8,3,32,128]{3,2,1,0:T(8,128)(2,1)S(1)}, u32[]{:S(2)}, u32[]{:S(2)}) %collective-permute-start.33) | collective-permute-done | bytes 196640 | tf_op jit(solution)/shard_map/ppermute | solution.py:31
  93.6 1.4 %collective-permute-start.13 = (bf16[6,32,256]{2,1,0:T(8,128)(2,1)S(1)}, bf16[6,32,256]{2,1,0:T(8,128)(2,1)S(1)}, u32[]{:S(2)}, u32[]{:S(2)}) collective-permute-start(bf16[6,32,256]{2,1,0:T(8,128)(2,1)S(1)} %get-tuple-element.57), channel_id=1, source_target_pairs={{0,5},{1,4},{2,7},{3,6},{4,1},{5,0},{6,3},{7,2},{8,13},{9,12},{10,... | collective-permute-start | bytes 294920 | tf_op jit(solution)/shard_map/ppermute | solution.py:49
  96.3 1.4 %collective-permute-start.15 = (bf16[6,32,256]{2,1,0:T(8,128)(2,1)S(1)}, bf16[6,32,256]{2,1,0:T(8,128)(2,1)S(1)}, u32[]{:S(2)}, u32[]{:S(2)}) collective-permute-start(bf16[6,32,256]{2,1,0:T(8,128)(2,1)S(1)} %get-tuple-element.59), channel_id=1, source_target_pairs={{0,7},{1,6},{2,5},{3,4},{4,3},{5,2},{6,1},{7,0},{8,15},{9,14},{10,... | collective-permute-start | bytes 294920 | tf_op jit(solution)/shard_map/ppermute | solution.py:49
  97.6 3.5 %shard_map.102.refs_2_.refs_11_ = bf16[2048,2048]{1,0:T(8,128)(2,1)S(1)} custom-call(bf16[2048,2048]{1,0:T(8,128)(2,1)} %wall_ref.1), custom_call_target="tpu_custom_call" | custom-call | flops 1000000 | bytes 16777216 | tf_op jit(solution)/shard_map/pallas_call | solution.py:62
  101.2 1.5 %shard_map.103.refs_10_ = f32[192,2048]{1,0:T(8,128)S(1)} custom-call(s32[1]{0:T(128)} %bitcast.index_ref, bf16[8,3,32,128]{3,2,1,0:T(8,128)(2,1)S(1)} %get-tuple-element.82.refs_0_, bf16[8,3,32,128]{3,2,1,0:T(8,128)(2,1)S(1)} %collective-permute-done.35.refs_1_, bf16[2048,2048]{1,0:T(8,128)(2,1)S(1)} %shard_map.102.refs_2_.refs_11_), custom_call_target="tpu_custom_call" | custom-call | flops 805306368 | bytes 10354692 | tf_op jit(solution)/shard_map/pallas_call | solution.py:62
  102.7 1.5 %collective-permute-done.13.refs_5_ = bf16[6,32,256]{2,1,0:T(8,128)(2,1)S(1)} collective-permute-done((bf16[6,32,256]{2,1,0:T(8,128)(2,1)S(1)}, bf16[6,32,256]{2,1,0:T(8,128)(2,1)S(1)}, u32[]{:S(2)}, u32[]{:S(2)}) %collective-permute-start.13) | collective-permute-done | bytes 98336 | tf_op jit(solution)/shard_map/ppermute | solution.py:49
  104.3 5.4 %shard_map.104 = (bf16[32,3,4,2048]{3,2,1,0:T(4,128)(2,1)}, f32[3,32,2048]{2,1,0:T(8,128)}) custom-call(s32[1]{0:T(128)} %bitcast.index_ref, bf16[6,32,256]{2,1,0:T(8,128)(2,1)S(1)} %get-tuple-element.52.refs_0_, bf16[6,32,256]{2,1,0:T(8,128)(2,1)S(1)} %collective-permute-done.9.refs_1_, bf16[6,32,256]{2,1,0:T(8,128)(2,1)S(1)} %collective-permute-done.10.refs_2_, ...), custom_call_target="tpu_custom_call" | custom-call | flops 3221225472 | bytes 14368772 | tf_op jit(solution)/shard_map/pallas_call | solution.py:62
  (68 shorter events, 10.3 us)
Async XLA Ops:
  4.4 11.5 %collective-permute-start.16 = (bf16[8,3,32,128]{3,2,1,0:T(8,128)(2,1)S(1)}, bf16[8,3,32,128]{3,2,1,0:T(8,128)(2,1)S(1)}, u32[]{:S(2)}, u32[]{:S(2)}) collective-permute-start(bf16[8,3,32,128]{3,2,1,0:T(8,128)(2,1)S(1)} %get-tuple-element.61), channel_id=1, source_target_pairs={{0,8},{1,9},{2,10},{3,11},{4,12},{5,13},{6,14},{7,15},{8,0},{9,1},... | collective-permute-start | bytes 589832 | tf_op jit(solution)/shard_map/ppermute | solution.py:31
  7.6 17.1 %collective-permute-start.17 = (bf16[8,3,32,128]{3,2,1,0:T(8,128)(2,1)S(1)}, bf16[8,3,32,128]{3,2,1,0:T(8,128)(2,1)S(1)}, u32[]{:S(2)}, u32[]{:S(2)}) collective-permute-start(bf16[8,3,32,128]{3,2,1,0:T(8,128)(2,1)S(1)} %get-tuple-element.62), channel_id=1, source_target_pairs={{0,16},{1,17},{2,18},{3,19},{4,20},{5,21},{6,22},{7,23},{8,24},{9,... | collective-permute-start | bytes 589832 | tf_op jit(solution)/shard_map/ppermute | solution.py:31
  10.1 17.3 %collective-permute-start.18 = (bf16[8,3,32,128]{3,2,1,0:T(8,128)(2,1)S(1)}, bf16[8,3,32,128]{3,2,1,0:T(8,128)(2,1)S(1)}, u32[]{:S(2)}, u32[]{:S(2)}) collective-permute-start(bf16[8,3,32,128]{3,2,1,0:T(8,128)(2,1)S(1)} %get-tuple-element.63), channel_id=1, source_target_pairs={{0,24},{1,25},{2,26},{3,27},{4,28},{5,29},{6,30},{7,31},{8,16},{9,... | collective-permute-start | bytes 589832 | tf_op jit(solution)/shard_map/ppermute | solution.py:31
  10.2 17.5 %collective-permute-start = (bf16[6,32,256]{2,1,0:T(8,128)(2,1)S(1)}, bf16[6,32,256]{2,1,0:T(8,128)(2,1)S(1)}, u32[]{:S(2)}, u32[]{:S(2)}) collective-permute-start(bf16[6,32,256]{2,1,0:T(8,128)(2,1)S(1)} %get-tuple-element.45), channel_id=1, source_target_pairs={{0,1},{1,0},{2,3},{3,2},{4,5},{5,4},{6,7},{7,6},{8,9},{9,8},{10,11... | collective-permute-start | bytes 294920 | tf_op jit(solution)/shard_map/ppermute | solution.py:49
  10.2 19.0 %collective-permute-start.1 = (bf16[6,32,256]{2,1,0:T(8,128)(2,1)S(1)}, bf16[6,32,256]{2,1,0:T(8,128)(2,1)S(1)}, u32[]{:S(2)}, u32[]{:S(2)}) collective-permute-start(bf16[6,32,256]{2,1,0:T(8,128)(2,1)S(1)} %get-tuple-element.46), channel_id=1, source_target_pairs={{0,2},{1,3},{2,0},{3,1},{4,6},{5,7},{6,4},{7,5},{8,10},{9,11},{10,... | collective-permute-start | bytes 294920 | tf_op jit(solution)/shard_map/ppermute | solution.py:49
  15.9 14.6 %collective-permute-start.2 = (bf16[6,32,256]{2,1,0:T(8,128)(2,1)S(1)}, bf16[6,32,256]{2,1,0:T(8,128)(2,1)S(1)}, u32[]{:S(2)}, u32[]{:S(2)}) collective-permute-start(bf16[6,32,256]{2,1,0:T(8,128)(2,1)S(1)} %get-tuple-element.47), channel_id=1, source_target_pairs={{0,3},{1,2},{2,1},{3,0},{4,7},{5,6},{6,5},{7,4},{8,11},{9,10},{10,... | collective-permute-start | bytes 294920 | tf_op jit(solution)/shard_map/ppermute | solution.py:49
  24.7 6.1 %collective-permute-start.3 = (bf16[6,32,256]{2,1,0:T(8,128)(2,1)S(1)}, bf16[6,32,256]{2,1,0:T(8,128)(2,1)S(1)}, u32[]{:S(2)}, u32[]{:S(2)}) collective-permute-start(bf16[6,32,256]{2,1,0:T(8,128)(2,1)S(1)} %get-tuple-element.48), channel_id=1, source_target_pairs={{0,4},{1,5},{2,6},{3,7},{4,0},{5,1},{6,2},{7,3},{8,12},{9,13},{10,... | collective-permute-start | bytes 294920 | tf_op jit(solution)/shard_map/ppermute | solution.py:49
  27.5 7.4 %collective-permute-start.4 = (bf16[6,32,256]{2,1,0:T(8,128)(2,1)S(1)}, bf16[6,32,256]{2,1,0:T(8,128)(2,1)S(1)}, u32[]{:S(2)}, u32[]{:S(2)}) collective-permute-start(bf16[6,32,256]{2,1,0:T(8,128)(2,1)S(1)} %get-tuple-element.49), channel_id=1, source_target_pairs={{0,5},{1,4},{2,7},{3,6},{4,1},{5,0},{6,3},{7,2},{8,13},{9,12},{10,... | collective-permute-start | bytes 294920 | tf_op jit(solution)/shard_map/ppermute | solution.py:49
  27.6 7.3 %collective-permute-start.5 = (bf16[6,32,256]{2,1,0:T(8,128)(2,1)S(1)}, bf16[6,32,256]{2,1,0:T(8,128)(2,1)S(1)}, u32[]{:S(2)}, u32[]{:S(2)}) collective-permute-start(bf16[6,32,256]{2,1,0:T(8,128)(2,1)S(1)} %get-tuple-element.50), channel_id=1, source_target_pairs={{0,6},{1,7},{2,4},{3,5},{4,2},{5,3},{6,0},{7,1},{8,14},{9,15},{10,... | collective-permute-start | bytes 294920 | tf_op jit(solution)/shard_map/ppermute | solution.py:49
  29.1 9.2 %collective-permute-start.6 = (bf16[6,32,256]{2,1,0:T(8,128)(2,1)S(1)}, bf16[6,32,256]{2,1,0:T(8,128)(2,1)S(1)}, u32[]{:S(2)}, u32[]{:S(2)}) collective-permute-start(bf16[6,32,256]{2,1,0:T(8,128)(2,1)S(1)} %get-tuple-element.51), channel_id=1, source_target_pairs={{0,7},{1,6},{2,5},{3,4},{4,3},{5,2},{6,1},{7,0},{8,15},{9,14},{10,... | collective-permute-start | bytes 294920 | tf_op jit(solution)/shard_map/ppermute | solution.py:49
  30.6 7.8 %collective-permute-start.19 = (bf16[4,3,32,128]{3,2,1,0:T(8,128)(2,1)S(1)}, bf16[4,3,32,128]{3,2,1,0:T(8,128)(2,1)S(1)}, u32[]{:S(2)}, u32[]{:S(2)}) collective-permute-start(bf16[4,3,32,128]{3,2,1,0:T(8,128)(2,1)S(1)} %get-tuple-element.65), channel_id=1, source_target_pairs={{0,1},{1,0},{2,3},{3,2},{4,5},{5,4},{6,7},{7,6},{8,9},{9,8},{10,11... | collective-permute-start | bytes 294920 | tf_op jit(solution)/shard_map/ppermute | solution.py:49
  30.8 9.5 %collective-permute-start.20 = (bf16[4,3,32,128]{3,2,1,0:T(8,128)(2,1)S(1)}, bf16[4,3,32,128]{3,2,1,0:T(8,128)(2,1)S(1)}, u32[]{:S(2)}, u32[]{:S(2)}) collective-permute-start(bf16[4,3,32,128]{3,2,1,0:T(8,128)(2,1)S(1)} %get-tuple-element.66), channel_id=1, source_target_pairs={{0,2},{1,3},{2,0},{3,1},{4,6},{5,7},{6,4},{7,5},{8,10},{9,11},{10,... | collective-permute-start | bytes 294920 | tf_op jit(solution)/shard_map/ppermute | solution.py:49
  34.9 6.1 %collective-permute-start.21 = (bf16[4,3,32,128]{3,2,1,0:T(8,128)(2,1)S(1)}, bf16[4,3,32,128]{3,2,1,0:T(8,128)(2,1)S(1)}, u32[]{:S(2)}, u32[]{:S(2)}) collective-permute-start(bf16[4,3,32,128]{3,2,1,0:T(8,128)(2,1)S(1)} %get-tuple-element.67), channel_id=1, source_target_pairs={{0,3},{1,2},{2,1},{3,0},{4,7},{5,6},{6,5},{7,4},{8,11},{9,10},{10,... | collective-permute-start | bytes 294920 | tf_op jit(solution)/shard_map/ppermute | solution.py:49
  34.9 8.6 %collective-permute-start.22 = (bf16[4,3,32,128]{3,2,1,0:T(8,128)(2,1)S(1)}, bf16[4,3,32,128]{3,2,1,0:T(8,128)(2,1)S(1)}, u32[]{:S(2)}, u32[]{:S(2)}) collective-permute-start(bf16[4,3,32,128]{3,2,1,0:T(8,128)(2,1)S(1)} %get-tuple-element.68), channel_id=1, source_target_pairs={{0,4},{1,5},{2,6},{3,7},{4,0},{5,1},{6,2},{7,3},{8,12},{9,13},{10,... | collective-permute-start | bytes 294920 | tf_op jit(solution)/shard_map/ppermute | solution.py:49
  38.4 9.3 %collective-permute-start.23 = (bf16[4,3,32,128]{3,2,1,0:T(8,128)(2,1)S(1)}, bf16[4,3,32,128]{3,2,1,0:T(8,128)(2,1)S(1)}, u32[]{:S(2)}, u32[]{:S(2)}) collective-permute-start(bf16[4,3,32,128]{3,2,1,0:T(8,128)(2,1)S(1)} %get-tuple-element.69), channel_id=1, source_target_pairs={{0,5},{1,4},{2,7},{3,6},{4,1},{5,0},{6,3},{7,2},{8,13},{9,12},{10,... | collective-permute-start | bytes 294920 | tf_op jit(solution)/shard_map/ppermute | solution.py:49
  38.4 9.3 %collective-permute-start.24 = (bf16[4,3,32,128]{3,2,1,0:T(8,128)(2,1)S(1)}, bf16[4,3,32,128]{3,2,1,0:T(8,128)(2,1)S(1)}, u32[]{:S(2)}, u32[]{:S(2)}) collective-permute-start(bf16[4,3,32,128]{3,2,1,0:T(8,128)(2,1)S(1)} %get-tuple-element.70), channel_id=1, source_target_pairs={{0,6},{1,7},{2,4},{3,5},{4,2},{5,3},{6,0},{7,1},{8,14},{9,15},{10,... | collective-permute-start | bytes 294920 | tf_op jit(solution)/shard_map/ppermute | solution.py:49
  40.2 7.5 %collective-permute-start.25 = (bf16[4,3,32,128]{3,2,1,0:T(8,128)(2,1)S(1)}, bf16[4,3,32,128]{3,2,1,0:T(8,128)(2,1)S(1)}, u32[]{:S(2)}, u32[]{:S(2)}) collective-permute-start(bf16[4,3,32,128]{3,2,1,0:T(8,128)(2,1)S(1)} %get-tuple-element.71), channel_id=1, source_target_pairs={{0,7},{1,6},{2,5},{3,4},{4,3},{5,2},{6,1},{7,0},{8,15},{9,14},{10,... | collective-permute-start | bytes 294920 | tf_op jit(solution)/shard_map/ppermute | solution.py:49
  41.0 27.1 %collective-permute-start.8 = (bf16[8,6,32,256]{3,2,1,0:T(8,128)(2,1)S(1)}, bf16[8,6,32,256]{3,2,1,0:T(8,128)(2,1)S(1)}, u32[]{:S(2)}, u32[]{:S(2)}) collective-permute-start(bf16[8,6,32,256]{3,2,1,0:T(8,128)(2,1)S(1)} %shard_map.97.refs_3_), channel_id=1, source_target_pairs={{0,24},{1,25},{2,26},{3,27},{4,28},{5,29},{6,30},{7,31},{8,0},{9,1... | collective-permute-start | bytes 2359304 | tf_op jit(solution)/shard_map/ppermute | solution.py:26
  43.6 37.3 %collective-permute-start.7 = (bf16[8,6,32,256]{3,2,1,0:T(8,128)(2,1)S(1)}, bf16[8,6,32,256]{3,2,1,0:T(8,128)(2,1)S(1)}, u32[]{:S(2)}, u32[]{:S(2)}) collective-permute-start(bf16[8,6,32,256]{3,2,1,0:T(8,128)(2,1)S(1)} %shard_map.97.refs_3_), channel_id=1, source_target_pairs={{0,8},{1,9},{2,10},{3,11},{4,12},{5,13},{6,14},{7,15},{8,16},{9,17... | collective-permute-start | bytes 2359304 | tf_op jit(solution)/shard_map/ppermute | solution.py:26
  50.7 6.8 %collective-permute-start.29 = (bf16[4,3,32,128]{3,2,1,0:T(8,128)(2,1)S(1)}, bf16[4,3,32,128]{3,2,1,0:T(8,128)(2,1)S(1)}, u32[]{:S(2)}, u32[]{:S(2)}) collective-permute-start(bf16[4,3,32,128]{3,2,1,0:T(8,128)(2,1)S(1)} %get-tuple-element.76), channel_id=1, source_target_pairs={{0,4},{1,5},{2,6},{3,7},{4,0},{5,1},{6,2},{7,3},{8,12},{9,13},{10,... | collective-permute-start | bytes 294920 | tf_op jit(solution)/shard_map/ppermute | solution.py:49
  55.4 6.3 %collective-permute-start.31 = (bf16[4,3,32,128]{3,2,1,0:T(8,128)(2,1)S(1)}, bf16[4,3,32,128]{3,2,1,0:T(8,128)(2,1)S(1)}, u32[]{:S(2)}, u32[]{:S(2)}) collective-permute-start(bf16[4,3,32,128]{3,2,1,0:T(8,128)(2,1)S(1)} %get-tuple-element.78), channel_id=1, source_target_pairs={{0,6},{1,7},{2,4},{3,5},{4,2},{5,3},{6,0},{7,1},{8,14},{9,15},{10,... | collective-permute-start | bytes 294920 | tf_op jit(solution)/shard_map/ppermute | solution.py:49
  57.5 6.7 %collective-permute-start.32 = (bf16[4,3,32,128]{3,2,1,0:T(8,128)(2,1)S(1)}, bf16[4,3,32,128]{3,2,1,0:T(8,128)(2,1)S(1)}, u32[]{:S(2)}, u32[]{:S(2)}) collective-permute-start(bf16[4,3,32,128]{3,2,1,0:T(8,128)(2,1)S(1)} %get-tuple-element.79), channel_id=1, source_target_pairs={{0,7},{1,6},{2,5},{3,4},{4,3},{5,2},{6,1},{7,0},{8,15},{9,14},{10,... | collective-permute-start | bytes 294920 | tf_op jit(solution)/shard_map/ppermute | solution.py:49
  64.2 28.6 %collective-permute-start.33 = (bf16[8,3,32,128]{3,2,1,0:T(8,128)(2,1)S(1)}, bf16[8,3,32,128]{3,2,1,0:T(8,128)(2,1)S(1)}, u32[]{:S(2)}, u32[]{:S(2)}) collective-permute-start(bf16[8,3,32,128]{3,2,1,0:T(8,128)(2,1)S(1)} %get-tuple-element.80), channel_id=1, source_target_pairs={{0,16},{1,17},{2,18},{3,19},{4,20},{5,21},{6,22},{7,23},{8,24},{9,... | collective-permute-start | bytes 589832 | tf_op jit(solution)/shard_map/ppermute | solution.py:31
  66.7 26.5 %collective-permute-start.34 = (bf16[8,3,32,128]{3,2,1,0:T(8,128)(2,1)S(1)}, bf16[8,3,32,128]{3,2,1,0:T(8,128)(2,1)S(1)}, u32[]{:S(2)}, u32[]{:S(2)}) collective-permute-start(bf16[8,3,32,128]{3,2,1,0:T(8,128)(2,1)S(1)} %get-tuple-element.81), channel_id=1, source_target_pairs={{0,24},{1,25},{2,26},{3,27},{4,28},{5,29},{6,30},{7,31},{8,16},{9,... | collective-permute-start | bytes 589832 | tf_op jit(solution)/shard_map/ppermute | solution.py:31
  68.1 25.6 %collective-permute-start.35 = (bf16[8,3,32,128]{3,2,1,0:T(8,128)(2,1)S(1)}, bf16[8,3,32,128]{3,2,1,0:T(8,128)(2,1)S(1)}, u32[]{:S(2)}, u32[]{:S(2)}) collective-permute-start(bf16[8,3,32,128]{3,2,1,0:T(8,128)(2,1)S(1)} %get-tuple-element.83), channel_id=1, source_target_pairs={{0,8},{1,9},{2,10},{3,11},{4,12},{5,13},{6,14},{7,15},{8,0},{9,1},... | collective-permute-start | bytes 589832 | tf_op jit(solution)/shard_map/ppermute | solution.py:31
  81.7 13.3 %collective-permute-start.9 = (bf16[6,32,256]{2,1,0:T(8,128)(2,1)S(1)}, bf16[6,32,256]{2,1,0:T(8,128)(2,1)S(1)}, u32[]{:S(2)}, u32[]{:S(2)}) collective-permute-start(bf16[6,32,256]{2,1,0:T(8,128)(2,1)S(1)} %get-tuple-element.53), channel_id=1, source_target_pairs={{0,1},{1,0},{2,3},{3,2},{4,5},{5,4},{6,7},{7,6},{8,9},{9,8},{10,11... | collective-permute-start | bytes 294920 | tf_op jit(solution)/shard_map/ppermute | solution.py:49
  81.8 14.4 %collective-permute-start.10 = (bf16[6,32,256]{2,1,0:T(8,128)(2,1)S(1)}, bf16[6,32,256]{2,1,0:T(8,128)(2,1)S(1)}, u32[]{:S(2)}, u32[]{:S(2)}) collective-permute-start(bf16[6,32,256]{2,1,0:T(8,128)(2,1)S(1)} %get-tuple-element.54), channel_id=1, source_target_pairs={{0,2},{1,3},{2,0},{3,1},{4,6},{5,7},{6,4},{7,5},{8,10},{9,11},{10,... | collective-permute-start | bytes 294920 | tf_op jit(solution)/shard_map/ppermute | solution.py:49
  92.8 9.9 %collective-permute-start.11 = (bf16[6,32,256]{2,1,0:T(8,128)(2,1)S(1)}, bf16[6,32,256]{2,1,0:T(8,128)(2,1)S(1)}, u32[]{:S(2)}, u32[]{:S(2)}) collective-permute-start(bf16[6,32,256]{2,1,0:T(8,128)(2,1)S(1)} %get-tuple-element.55), channel_id=1, source_target_pairs={{0,3},{1,2},{2,1},{3,0},{4,7},{5,6},{6,5},{7,4},{8,11},{9,10},{10,... | collective-permute-start | bytes 294920 | tf_op jit(solution)/shard_map/ppermute | solution.py:49
  93.2 9.5 %collective-permute-start.12 = (bf16[6,32,256]{2,1,0:T(8,128)(2,1)S(1)}, bf16[6,32,256]{2,1,0:T(8,128)(2,1)S(1)}, u32[]{:S(2)}, u32[]{:S(2)}) collective-permute-start(bf16[6,32,256]{2,1,0:T(8,128)(2,1)S(1)} %get-tuple-element.56), channel_id=1, source_target_pairs={{0,4},{1,5},{2,6},{3,7},{4,0},{5,1},{6,2},{7,3},{8,12},{9,13},{10,... | collective-permute-start | bytes 294920 | tf_op jit(solution)/shard_map/ppermute | solution.py:49
  93.6 10.6 %collective-permute-start.13 = (bf16[6,32,256]{2,1,0:T(8,128)(2,1)S(1)}, bf16[6,32,256]{2,1,0:T(8,128)(2,1)S(1)}, u32[]{:S(2)}, u32[]{:S(2)}) collective-permute-start(bf16[6,32,256]{2,1,0:T(8,128)(2,1)S(1)} %get-tuple-element.57), channel_id=1, source_target_pairs={{0,5},{1,4},{2,7},{3,6},{4,1},{5,0},{6,3},{7,2},{8,13},{9,12},{10,... | collective-permute-start | bytes 294920 | tf_op jit(solution)/shard_map/ppermute | solution.py:49
  95.1 9.2 %collective-permute-start.14 = (bf16[6,32,256]{2,1,0:T(8,128)(2,1)S(1)}, bf16[6,32,256]{2,1,0:T(8,128)(2,1)S(1)}, u32[]{:S(2)}, u32[]{:S(2)}) collective-permute-start(bf16[6,32,256]{2,1,0:T(8,128)(2,1)S(1)} %get-tuple-element.58), channel_id=1, source_target_pairs={{0,6},{1,7},{2,4},{3,5},{4,2},{5,3},{6,0},{7,1},{8,14},{9,15},{10,... | collective-permute-start | bytes 294920 | tf_op jit(solution)/shard_map/ppermute | solution.py:49
  96.3 8.0 %collective-permute-start.15 = (bf16[6,32,256]{2,1,0:T(8,128)(2,1)S(1)}, bf16[6,32,256]{2,1,0:T(8,128)(2,1)S(1)}, u32[]{:S(2)}, u32[]{:S(2)}) collective-permute-start(bf16[6,32,256]{2,1,0:T(8,128)(2,1)S(1)} %get-tuple-element.59), channel_id=1, source_target_pairs={{0,7},{1,6},{2,5},{3,4},{4,3},{5,2},{6,1},{7,0},{8,15},{9,14},{10,... | collective-permute-start | bytes 294920 | tf_op jit(solution)/shard_map/ppermute | solution.py:49
  (11 other events, 60.3 us)

commit v4 on v3

--- a/solution.py
+++ b/solution.py
@@ -32,7 +32,10 @@
 
 
 def crossing(pieces, team):
-    return [pieces[0]] + [crossed(pieces[x], team, x) for x in range(1, len(pieces))]
+    got = [pieces[0]]
+    for x in range(1, len(pieces)):
+        got.append(crossed(pieces[x], team, x))
+    return got
 
 
 def within(value, team):
@@ -43,9 +46,8 @@
 
 def direct(pieces):
     count = lax.axis_size("span")
-    order = sorted(range(1, len(pieces)), key=lambda x: -x)
     got = list(pieces)
-    for x in order:
+    for x in range(1, len(pieces)):
         got[x] = lax.ppermute(pieces[x], "span", [(i, i ^ x) for i in range(count)])
     return got
 
@@ -84,18 +86,25 @@
 
 
 def pack_kernel(early, groups, place, slabs_ref, *refs):
-    far_ref, near_ref, turned_ref = refs[-3:]
+    slab_ref, far_ref, near_ref, turned_ref, sems = refs[-5:]
     rows, parts, planes, width = slabs_ref.shape
     strip = near_ref.shape[3]
     slots = width // groups // LANES
 
+    def fetch(part):
+        return pltpu.make_async_copy(slabs_ref.at[:, part], slab_ref.at[part], sems.at[part])
+
+    for part in range(parts):
+        fetch(part).start()
+
     @pl.loop(0, parts)
     def _(part):
+        fetch(part).wait()
         for column in range(width // LANES):
             at = slice(column * LANES, (column + 1) * LANES)
             held = turned_ref.at[column]
             for row in range(rows):
-                held[pl.ds(row, planes, stride=rows), :] = slabs_ref[row, part, :, at].astype(jnp.float32)
+                held[pl.ds(row, planes, stride=rows), :] = slab_ref[part, row, :, at].astype(jnp.float32)
             member, inner = divmod(column * LANES, strip)
             group, slot = divmod(column, slots)
             for plane in range(planes):
@@ -107,7 +116,7 @@
 
     for k in range(groups):
         refs[k][...] = far_ref[place[0] ^ k]
-    for x, ref in enumerate(refs[groups:-3]):
+    for x, ref in enumerate(refs[groups:-5]):
         ref[...] = near_ref[place[1] ^ x]
 
 
@@ -220,50 +229,45 @@
     return total
 
 
-def far_start_kernel(late, place, own_ref, next_ref, wall_ref, sum_ref):
+def near_sum(place, refs, order, wall_ref, at):
+    total = None
+    for x, ref in zip(order, refs):
+        units, rows, strip = ref.shape
+        where = pl.multiple_of((place[1] ^ x) * strip, strip)
+        part = contract(ref[...].reshape(units * rows, strip), wall_ref[at, pl.ds(where, strip)])
+        total = part if total is None else total + part
+    return total
+
+
+def wall_start_kernel(late, place, *refs):
+    near_refs, far_refs = refs[:-4], refs[-4:-2]
+    wall_ref, sum_ref = refs[-2:]
     width = wall_ref.shape[0]
-    block = 2 * LANES
+    first = near_refs[0].shape[0] * near_refs[0].shape[1]
+    block = 4 * LANES
     for start in range(0, width, block):
         at = slice(start, start + block)
-        sum_ref[:, at] = far_sum(place, [own_ref, next_ref], [0, 1], late, wall_ref, at, None)
+        sum_ref[:first, at] = near_sum(place, near_refs, range(len(near_refs)), wall_ref, at)
+        sum_ref[first:, at] = far_sum(place, far_refs, [0, 1], late, wall_ref, at, None)
 
 
 def wall_kernel(late, team, place, *refs):
-    near_refs, far_refs = refs[:team], refs[team:-15]
-    sum_ref, wall_ref, state_ref, scale_ref, mean_ref, diag_ref, off_ref, velocity_ref, last_ref = refs[-15:-6]
-    rows_ref, sums_ref, turned_ref, speed_ref, final_ref, sems = refs[-6:]
-    units, rows, strip = near_refs[0].shape
+    near_refs, far_refs = refs[: team // 2], refs[team // 2 : -14]
+    sum_ref, wall_ref, state_ref, scale_ref, mean_ref, diag_ref, off_ref, velocity_ref, last_ref = refs[-14:-5]
+    sums_ref, turned_ref, speed_ref, final_ref, sems = refs[-5:]
+    units, rows, _ = near_refs[0].shape
     parts, _, width = state_ref.shape
     planes = velocity_ref.shape[2]
     block = sums_ref.shape[1]
     tiles = block // LANES
-    slots = far_refs[0].shape[0] // late
-    quarter = slots * LANES
     first = units * rows
-
-    for x, ref in enumerate(near_refs):
-        where = pl.multiple_of((place[1] ^ x) * strip, strip)
-        rows_ref[:first, pl.ds(where, strip)] = ref[...].reshape(first, strip)
-    done = width // quarter - len(far_refs)
-    for k, ref in enumerate(far_refs):
-        for slot in range(0, slots, 2):
-            where = pl.multiple_of((place[0] ^ (done + k)) * quarter + slot * LANES, 2 * LANES)
-            rows_ref[first:, pl.ds(where, 2 * LANES)] = far_rows(place[1], ref, late, slot)
 
     copies = []
     for step, start in enumerate(range(0, width, block)):
         at = slice(start, start + block)
-        both = near = None
-        for k in range(width // quarter):
-            where = pl.ds(pl.multiple_of((place[0] ^ k) * quarter, quarter), quarter)
-            if k < done:
-                part = contract(rows_ref[:first, where], wall_ref[at, where])
-                near = part if near is None else near + part
-            else:
-                part = contract(rows_ref[:, where], wall_ref[at, where])
-                both = part if both is None else both + part
-        sums_ref[:first] = both[:first] + near
-        sums_ref[first:] = both[first:] + sum_ref[:, at]
+        order = range(team // 2, team)
+        sums_ref[:first] = sum_ref[:first, at] + near_sum(place, near_refs, order, wall_ref, at)
+        sums_ref[first:] = far_sum(place, far_refs, [2, 3], late, wall_ref, at, sum_ref[first:, at])
         state = [state_ref[i, :, at] for i in range(parts)]
         for plane in range(planes):
             fresh = [sums_ref[(plane * parts + i) * rows :][:rows] for i in range(parts)]
@@ -337,7 +341,7 @@
     place = lax.axis_index("span").astype(jnp.int32)[None]
 
     late = planes // 2
-    if width != groups * (team // late) * LANES or groups > 4:
+    if width != groups * (team // late) * LANES or groups != 4 or team & (team - 1) or width % (2 * team * LANES):
         return plain(random_slabs, band, wall_filter, prev_state, time_scale, mean_velocity, lund_diag, lund_off)
     early = planes - late
     strip = width // team
@@ -351,12 +355,15 @@
         placed(functools.partial(pack_kernel, early, groups), team),
         [place, slabs],
         [shape((team, parts, rows, LANES), slabs.dtype)] * groups + [shape((units, rows, strip), slabs.dtype)] * team,
-        in_specs=[SMEM, VMEM],
+        in_specs=[SMEM, HBM],
         scratch=[
+            pltpu.VMEM((parts, rows, planes, width), slabs.dtype),
             pltpu.VMEM((groups, team, parts, rows, LANES), slabs.dtype),
             pltpu.VMEM((team, units, rows, strip), slabs.dtype),
             pltpu.VMEM((width // LANES, planes * rows, LANES), jnp.float32),
+            pltpu.SemaphoreType.DMA((parts,)),
         ],
+        limit=52 << 20,
     )
     far, near = packed[:groups], packed[groups:]
     far = crossing(far, team)
@@ -398,21 +405,20 @@
     near = direct(near)
     far = crossing(far, team)
     sums = kernel_call(
-        placed(functools.partial(far_start_kernel, late), team),
-        [place, far[0], far[1], wall],
-        [shape((late * parts * rows, width), jnp.float32)],
-        in_specs=[SMEM, VMEM, VMEM, VMEM],
-        flops=wall_filter.size * late * parts * rows,
+        placed(functools.partial(wall_start_kernel, late), team),
+        [place, *near[: team // 2], far[0], far[1], wall],
+        [shape((planes * parts * rows, width), jnp.float32)],
+        in_specs=[SMEM] + [VMEM] * (team // 2 + 3),
+        flops=wall_filter.size * planes * parts * rows,
     )[0]
     block = BLOCK
     velocity, state = kernel_call(
         placed(functools.partial(wall_kernel, late, team), team),
-        [place, *near, *far[2:], sums, wall, state, *lines],
+        [place, *near[team // 2 :], *far[2:], sums, wall, state, *lines],
         [shape(slabs.shape, slabs.dtype), shape(state.shape, state.dtype)],
-        in_specs=[SMEM] + [VMEM] * (team + groups - 2 + 7),
+        in_specs=[SMEM] + [VMEM] * (team // 2 + groups - 2 + 7),
         out_specs=[HBM, HBM],
         scratch=[
-            pltpu.VMEM((planes * parts * rows, width), slabs.dtype),
             pltpu.VMEM((planes * parts * rows, block), jnp.float32),
             pltpu.VMEM((parts, block // LANES, planes * rows, LANES), jnp.float32),
             pltpu.VMEM(slabs.shape, slabs.dtype),

time: 111 us -> 109 us (0.982)
  waiting for transfers between devices: 51.9 us -> 47.8 us
  Pallas kernels: 15 us -> 17 us
  local copies, waits for them, and re-layouts: 1.45 us -> 0.03 us
  other arithmetic: 0.61 us -> 1.99 us
    ppermute x6, waiting for transfers between devices: 23 us -> 17.6 us  [crossed(): lax.ppermute(value, 'span', [(i, (i // team ^ x) * team + i % team) for i...]
    pallas_call x10, Pallas kernels: 15 us -> 17 us  [kernel_call(): pl.pallas_call(body, in_specs=in_specs or [VMEM] * len(inputs), out_specs...]
    unnamed x14 -> x10, local copies, waits for them, and re-layouts: 1.44 us -> 0.02 us
    ppermute x28, waiting for transfers between devices: 16.1 us -> 17.3 us  [direct(): got[x] = lax.ppermute(pieces[x], 'span', [(i, i ^ x) for i in range(count)])]
  transfers between devices with their start and end apart: 36 -> 36, of which waited for: 12 -> 12; matrix products, arithmetic and copies ran while one was open for 1% -> 2% of each run, Pallas kernels for 7% -> 8%
where the time goes in v4:
time: 109 us
  waiting for transfers between devices  47.8 us (44%)
  starting transfers between devices  40.3 us (37%)
  Pallas kernels  17 us (16%)
  other arithmetic  1.99 us (2%)
  between operations  1.54 us (1%)
    ppermute x28, starting transfers between devices, direct(): got[x] = lax.ppermute(pieces[x], 'span', [(i, i ^ x) for i in range(count)])  27.3 us
    ppermute x6, waiting for transfers between devices, crossed(): lax.ppermute(value, 'span', [(i, (i // team ^ x) * team + i % team) for i...  17.6 us
    ppermute x28, waiting for transfers between devices, direct(): got[x] = lax.ppermute(pieces[x], 'span', [(i, i ^ x) for i in range(count)])  17.3 us
    pallas_call x10, Pallas kernels, kernel_call(): pl.pallas_call(body, in_specs=in_specs or [VMEM] * len(inputs), out_specs...  17 us
    ppermute x2, waiting for transfers between devices, shifted(): lax.ppermute(value, 'span', [(i, (i + by * team) % count) for i in range(...  12.9 us
    ppermute x6, starting transfers between devices, crossed(): lax.ppermute(value, 'span', [(i, (i // team ^ x) * team + i % team) for i...  10.5 us
    ppermute x2, starting transfers between devices, shifted(): lax.ppermute(value, 'span', [(i, (i + by * team) % count) for i in range(...  2.53 us
  transfers between devices with their start and end apart: 36, of which 12 were waited for; matrix products, arithmetic and copies ran while one was open for 2% of the time, Pallas kernels for 8%

profile of v4, /device:TPU:0, one launch (start us, length us, event | category | flops | bytes accessed | tf_op | source)
XLA Modules:
  0.0 108.7 jit_solution(6084291676267777597)
XLA Ops:
  0.6 3.4 %shard_map.96 = (bf16[8,3,32,128]{3,2,1,0:T(8,128)(2,1)S(1)}, bf16[8,3,32,128]{3,2,1,0:T(8,128)(2,1)S(1)}, bf16[8,3,32,128]{3,2,1,0:T(8,128)(2,1)S(1)}, bf16[8,3...) custom-call(s32[1]{0:T(128)} %bitcast.index_ref, ...), custom_call_target="tpu_custom_call" | custom-call | flops 1000000 | bytes 3145732 | tf_op jit(solution)/shard_map/pallas_call | solution.py:64
  4.0 3.1 %collective-permute-start.13 = (bf16[8,3,32,128]{3,2,1,0:T(8,128)(2,1)S(1)}, bf16[8,3,32,128]{3,2,1,0:T(8,128)(2,1)S(1)}, u32[]{:S(2)}, u32[]{:S(2)}) collective-permute-start(bf16[8,3,32,128]{3,2,1,0:T(8,128)(2,1)S(1)} %get-tuple-element.57), channel_id=1, source_target_pairs={{0,8},{1,9},{2,10},{3,11},{4,12},{5,13},{6,14},{7,15},{8,0},{9,1},... | collective-permute-start | bytes 589832 | tf_op jit(solution)/shard_map/ppermute | solution.py:31
  7.2 2.6 %collective-permute-start.14 = (bf16[8,3,32,128]{3,2,1,0:T(8,128)(2,1)S(1)}, bf16[8,3,32,128]{3,2,1,0:T(8,128)(2,1)S(1)}, u32[]{:S(2)}, u32[]{:S(2)}) collective-permute-start(bf16[8,3,32,128]{3,2,1,0:T(8,128)(2,1)S(1)} %get-tuple-element.58), channel_id=1, source_target_pairs={{0,16},{1,17},{2,18},{3,19},{4,20},{5,21},{6,22},{7,23},{8,24},{9,... | collective-permute-start | bytes 589832 | tf_op jit(solution)/shard_map/ppermute | solution.py:31
  9.7 1.7 %collective-permute-start.1 = (bf16[6,32,256]{2,1,0:T(8,128)(2,1)S(1)}, bf16[6,32,256]{2,1,0:T(8,128)(2,1)S(1)}, u32[]{:S(2)}, u32[]{:S(2)}) collective-permute-start(bf16[6,32,256]{2,1,0:T(8,128)(2,1)S(1)} %get-tuple-element.46), channel_id=1, source_target_pairs={{0,2},{1,3},{2,0},{3,1},{4,6},{5,7},{6,4},{7,5},{8,10},{9,11},{10,... | collective-permute-start | bytes 294920 | tf_op jit(solution)/shard_map/ppermute | solution.py:51
  11.5 4.1 %collective-permute-done.13.refs_1_ = bf16[8,3,32,128]{3,2,1,0:T(8,128)(2,1)S(1)} collective-permute-done((bf16[8,3,32,128]{3,2,1,0:T(8,128)(2,1)S(1)}, bf16[8,3,32,128]{3,2,1,0:T(8,128)(2,1)S(1)}, u32[]{:S(2)}, u32[]{:S(2)}) %collective-permute-start.13) | collective-permute-done | bytes 196640 | tf_op jit(solution)/shard_map/ppermute | solution.py:31
  15.5 8.7 %collective-permute-done.14.refs_2_ = bf16[8,3,32,128]{3,2,1,0:T(8,128)(2,1)S(1)} collective-permute-done((bf16[8,3,32,128]{3,2,1,0:T(8,128)(2,1)S(1)}, bf16[8,3,32,128]{3,2,1,0:T(8,128)(2,1)S(1)}, u32[]{:S(2)}, u32[]{:S(2)}) %collective-permute-start.14) | collective-permute-done | bytes 196640 | tf_op jit(solution)/shard_map/ppermute | solution.py:31
  24.3 1.5 %collective-permute-start.3 = (bf16[6,32,256]{2,1,0:T(8,128)(2,1)S(1)}, bf16[6,32,256]{2,1,0:T(8,128)(2,1)S(1)}, u32[]{:S(2)}, u32[]{:S(2)}) collective-permute-start(bf16[6,32,256]{2,1,0:T(8,128)(2,1)S(1)} %get-tuple-element.48), channel_id=1, source_target_pairs={{0,4},{1,5},{2,6},{3,7},{4,0},{5,1},{6,2},{7,3},{8,12},{9,13},{10,... | collective-permute-start | bytes 294920 | tf_op jit(solution)/shard_map/ppermute | solution.py:51
  25.8 1.3 %multiply_reduce_fusion = f32[]{:T(128)} fusion(f32[513]{0:T(1024)} %param.9), kind=kLoop, calls=%fused_computation.1 | loop fusion | flops 1025 | bytes 2056 | tf_op jit(solution)/shard_map/reduce_sum | solution.py:338
  27.9 1.5 %collective-permute-start.5 = (bf16[6,32,256]{2,1,0:T(8,128)(2,1)S(1)}, bf16[6,32,256]{2,1,0:T(8,128)(2,1)S(1)}, u32[]{:S(2)}, u32[]{:S(2)}) collective-permute-start(bf16[6,32,256]{2,1,0:T(8,128)(2,1)S(1)} %get-tuple-element.50), channel_id=1, source_target_pairs={{0,6},{1,7},{2,4},{3,5},{4,2},{5,3},{6,0},{7,1},{8,14},{9,15},{10,... | collective-permute-start | bytes 294920 | tf_op jit(solution)/shard_map/ppermute | solution.py:51
  29.4 1.4 %collective-permute-start.6 = (bf16[6,32,256]{2,1,0:T(8,128)(2,1)S(1)}, bf16[6,32,256]{2,1,0:T(8,128)(2,1)S(1)}, u32[]{:S(2)}, u32[]{:S(2)}) collective-permute-start(bf16[6,32,256]{2,1,0:T(8,128)(2,1)S(1)} %get-tuple-element.51), channel_id=1, source_target_pairs={{0,7},{1,6},{2,5},{3,4},{4,3},{5,2},{6,1},{7,0},{8,15},{9,14},{10,... | collective-permute-start | bytes 294920 | tf_op jit(solution)/shard_map/ppermute | solution.py:51
  31.0 1.5 %collective-permute-start.17 = (bf16[4,3,32,128]{3,2,1,0:T(8,128)(2,1)S(1)}, bf16[4,3,32,128]{3,2,1,0:T(8,128)(2,1)S(1)}, u32[]{:S(2)}, u32[]{:S(2)}) collective-permute-start(bf16[4,3,32,128]{3,2,1,0:T(8,128)(2,1)S(1)} %get-tuple-element.62), channel_id=1, source_target_pairs={{0,2},{1,3},{2,0},{3,1},{4,6},{5,7},{6,4},{7,5},{8,10},{9,11},{10,... | collective-permute-start | bytes 294920 | tf_op jit(solution)/shard_map/ppermute | solution.py:51
  33.2 2.0 %collective-permute-done.4.refs_5_ = bf16[6,32,256]{2,1,0:T(8,128)(2,1)S(1)} collective-permute-done((bf16[6,32,256]{2,1,0:T(8,128)(2,1)S(1)}, bf16[6,32,256]{2,1,0:T(8,128)(2,1)S(1)}, u32[]{:S(2)}, u32[]{:S(2)}) %collective-permute-start.4) | collective-permute-done | bytes 98336 | tf_op jit(solution)/shard_map/ppermute | solution.py:51
  35.2 3.4 %collective-permute-start.19 = (bf16[4,3,32,128]{3,2,1,0:T(8,128)(2,1)S(1)}, bf16[4,3,32,128]{3,2,1,0:T(8,128)(2,1)S(1)}, u32[]{:S(2)}, u32[]{:S(2)}) collective-permute-start(bf16[4,3,32,128]{3,2,1,0:T(8,128)(2,1)S(1)} %get-tuple-element.64), channel_id=1, source_target_pairs={{0,4},{1,5},{2,6},{3,7},{4,0},{5,1},{6,2},{7,3},{8,12},{9,13},{10,... | collective-permute-start | bytes 294920 | tf_op jit(solution)/shard_map/ppermute | solution.py:51
  38.7 1.9 %collective-permute-start.21 = (bf16[4,3,32,128]{3,2,1,0:T(8,128)(2,1)S(1)}, bf16[4,3,32,128]{3,2,1,0:T(8,128)(2,1)S(1)}, u32[]{:S(2)}, u32[]{:S(2)}) collective-permute-start(bf16[4,3,32,128]{3,2,1,0:T(8,128)(2,1)S(1)} %get-tuple-element.66), channel_id=1, source_target_pairs={{0,6},{1,7},{2,4},{3,5},{4,2},{5,3},{6,0},{7,1},{8,14},{9,15},{10,... | collective-permute-start | bytes 294920 | tf_op jit(solution)/shard_map/ppermute | solution.py:51
  41.3 2.5 %collective-permute-start.8 = (bf16[8,6,32,256]{3,2,1,0:T(8,128)(2,1)S(1)}, bf16[8,6,32,256]{3,2,1,0:T(8,128)(2,1)S(1)}, u32[]{:S(2)}, u32[]{:S(2)}) collective-permute-start(bf16[8,6,32,256]{3,2,1,0:T(8,128)(2,1)S(1)} %shard_map.97.refs_3_), channel_id=1, source_target_pairs={{0,24},{1,25},{2,26},{3,27},{4,28},{5,29},{6,30},{7,31},{8,0},{9,1... | collective-permute-start | bytes 2359304 | tf_op jit(solution)/shard_map/ppermute | solution.py:26
  43.8 4.1 %collective-permute-done.20.refs_6_ = bf16[4,3,32,128]{3,2,1,0:T(8,128)(2,1)S(1)} collective-permute-done((bf16[4,3,32,128]{3,2,1,0:T(8,128)(2,1)S(1)}, bf16[4,3,32,128]{3,2,1,0:T(8,128)(2,1)S(1)}, u32[]{:S(2)}, u32[]{:S(2)}) %collective-permute-start.20) | collective-permute-done | bytes 98336 | tf_op jit(solution)/shard_map/ppermute | solution.py:51
  51.0 1.6 %collective-permute-start.26 = (bf16[4,3,32,128]{3,2,1,0:T(8,128)(2,1)S(1)}, bf16[4,3,32,128]{3,2,1,0:T(8,128)(2,1)S(1)}, u32[]{:S(2)}, u32[]{:S(2)}) collective-permute-start(bf16[4,3,32,128]{3,2,1,0:T(8,128)(2,1)S(1)} %get-tuple-element.72), channel_id=1, source_target_pairs={{0,4},{1,5},{2,6},{3,7},{4,0},{5,1},{6,2},{7,3},{8,12},{9,13},{10,... | collective-permute-start | bytes 294920 | tf_op jit(solution)/shard_map/ppermute | solution.py:51
  52.6 2.5 %collective-permute-done.24.refs_2_ = bf16[4,3,32,128]{3,2,1,0:T(8,128)(2,1)S(1)} collective-permute-done((bf16[4,3,32,128]{3,2,1,0:T(8,128)(2,1)S(1)}, bf16[4,3,32,128]{3,2,1,0:T(8,128)(2,1)S(1)}, u32[]{:S(2)}, u32[]{:S(2)}) %collective-permute-start.24) | collective-permute-done | bytes 98336 | tf_op jit(solution)/shard_map/ppermute | solution.py:51
  55.7 2.1 %collective-permute-start.28 = (bf16[4,3,32,128]{3,2,1,0:T(8,128)(2,1)S(1)}, bf16[4,3,32,128]{3,2,1,0:T(8,128)(2,1)S(1)}, u32[]{:S(2)}, u32[]{:S(2)}) collective-permute-start(bf16[4,3,32,128]{3,2,1,0:T(8,128)(2,1)S(1)} %get-tuple-element.74), channel_id=1, source_target_pairs={{0,6},{1,7},{2,4},{3,5},{4,2},{5,3},{6,0},{7,1},{8,14},{9,15},{10,... | collective-permute-start | bytes 294920 | tf_op jit(solution)/shard_map/ppermute | solution.py:51
  57.8 1.5 %collective-permute-start.29 = (bf16[4,3,32,128]{3,2,1,0:T(8,128)(2,1)S(1)}, bf16[4,3,32,128]{3,2,1,0:T(8,128)(2,1)S(1)}, u32[]{:S(2)}, u32[]{:S(2)}) collective-permute-start(bf16[4,3,32,128]{3,2,1,0:T(8,128)(2,1)S(1)} %get-tuple-element.75), channel_id=1, source_target_pairs={{0,7},{1,6},{2,5},{3,4},{4,3},{5,2},{6,1},{7,0},{8,15},{9,14},{10,... | collective-permute-start | bytes 294920 | tf_op jit(solution)/shard_map/ppermute | solution.py:51
  59.9 2.0 %collective-permute-done.28.refs_6_ = bf16[4,3,32,128]{3,2,1,0:T(8,128)(2,1)S(1)} collective-permute-done((bf16[4,3,32,128]{3,2,1,0:T(8,128)(2,1)S(1)}, bf16[4,3,32,128]{3,2,1,0:T(8,128)(2,1)S(1)}, u32[]{:S(2)}, u32[]{:S(2)}) %collective-permute-start.28) | collective-permute-done | bytes 98336 | tf_op jit(solution)/shard_map/ppermute | solution.py:51
  62.0 2.5 %collective-permute-done.29.refs_7_ = bf16[4,3,32,128]{3,2,1,0:T(8,128)(2,1)S(1)} collective-permute-done((bf16[4,3,32,128]{3,2,1,0:T(8,128)(2,1)S(1)}, bf16[4,3,32,128]{3,2,1,0:T(8,128)(2,1)S(1)}, u32[]{:S(2)}, u32[]{:S(2)}) %collective-permute-start.29) | collective-permute-done | bytes 98336 | tf_op jit(solution)/shard_map/ppermute | solution.py:51
  64.5 1.8 %collective-permute-start.30 = (bf16[8,3,32,128]{3,2,1,0:T(8,128)(2,1)S(1)}, bf16[8,3,32,128]{3,2,1,0:T(8,128)(2,1)S(1)}, u32[]{:S(2)}, u32[]{:S(2)}) collective-permute-start(bf16[8,3,32,128]{3,2,1,0:T(8,128)(2,1)S(1)} %get-tuple-element.76), channel_id=1, source_target_pairs={{0,16},{1,17},{2,18},{3,19},{4,20},{5,21},{6,22},{7,23},{8,24},{9,... | collective-permute-start | bytes 589832 | tf_op jit(solution)/shard_map/ppermute | solution.py:31
  67.6 12.9 %collective-permute-done.7.refs_1_ = bf16[8,6,32,256]{3,2,1,0:T(8,128)(2,1)S(1)} collective-permute-done((bf16[8,6,32,256]{3,2,1,0:T(8,128)(2,1)S(1)}, bf16[8,6,32,256]{3,2,1,0:T(8,128)(2,1)S(1)}, u32[]{:S(2)}, u32[]{:S(2)}) %collective-permute-start.7) | collective-permute-done | bytes 786464 | tf_op jit(solution)/shard_map/ppermute | solution.py:26
  83.3 4.8 %collective-permute-done.30.refs_4_ = bf16[8,3,32,128]{3,2,1,0:T(8,128)(2,1)S(1)} collective-permute-done((bf16[8,3,32,128]{3,2,1,0:T(8,128)(2,1)S(1)}, bf16[8,3,32,128]{3,2,1,0:T(8,128)(2,1)S(1)}, u32[]{:S(2)}, u32[]{:S(2)}) %collective-permute-start.30) | collective-permute-done | bytes 196640 | tf_op jit(solution)/shard_map/ppermute | solution.py:31
  88.1 1.7 %collective-permute-start.31 = (bf16[8,3,32,128]{3,2,1,0:T(8,128)(2,1)S(1)}, bf16[8,3,32,128]{3,2,1,0:T(8,128)(2,1)S(1)}, u32[]{:S(2)}, u32[]{:S(2)}) collective-permute-start(bf16[8,3,32,128]{3,2,1,0:T(8,128)(2,1)S(1)} %get-tuple-element.77), channel_id=1, source_target_pairs={{0,24},{1,25},{2,26},{3,27},{4,28},{5,29},{6,30},{7,31},{8,16},{9,... | collective-permute-start | bytes 589832 | tf_op jit(solution)/shard_map/ppermute | solution.py:31
  89.8 3.5 %shard_map.102.refs_6_.refs_7_ = bf16[2048,2048]{1,0:T(8,128)(2,1)S(1)} custom-call(bf16[2048,2048]{1,0:T(8,128)(2,1)} %wall_ref.1), custom_call_target="tpu_custom_call" | custom-call | flops 1000000 | bytes 16777216 | tf_op jit(solution)/shard_map/pallas_call | solution.py:64
  94.4 1.4 %collective-permute-start.11 = (bf16[6,32,256]{2,1,0:T(8,128)(2,1)S(1)}, bf16[6,32,256]{2,1,0:T(8,128)(2,1)S(1)}, u32[]{:S(2)}, u32[]{:S(2)}) collective-permute-start(bf16[6,32,256]{2,1,0:T(8,128)(2,1)S(1)} %get-tuple-element.54), channel_id=1, source_target_pairs={{0,6},{1,7},{2,4},{3,5},{4,2},{5,3},{6,0},{7,1},{8,14},{9,15},{10,... | collective-permute-start | bytes 294920 | tf_op jit(solution)/shard_map/ppermute | solution.py:51
  95.8 2.0 %collective-permute-start.12 = (bf16[6,32,256]{2,1,0:T(8,128)(2,1)S(1)}, bf16[6,32,256]{2,1,0:T(8,128)(2,1)S(1)}, u32[]{:S(2)}, u32[]{:S(2)}) collective-permute-start(bf16[6,32,256]{2,1,0:T(8,128)(2,1)S(1)} %get-tuple-element.55), channel_id=1, source_target_pairs={{0,7},{1,6},{2,5},{3,4},{4,3},{5,2},{6,1},{7,0},{8,15},{9,14},{10,... | collective-permute-start | bytes 294920 | tf_op jit(solution)/shard_map/ppermute | solution.py:51
  97.8 2.9 %shard_map.103.refs_6_ = f32[384,2048]{1,0:T(8,128)S(1)} custom-call(s32[1]{0:T(128)} %bitcast.index_ref, bf16[6,32,256]{2,1,0:T(8,128)(2,1)S(1)} %get-tuple-element.78.refs_0_, bf16[6,32,256]{2,1,0:T(8,128)(2,1)S(1)} %collective-permute-done.32.refs_1_, bf16[6,32,256]{2,1,0:T(8,128)(2,1)S(1)} %collective-permute-done.33.refs_2_, ...), custom_call_target="tpu_custom_call" | custom-call | flops 1610612736 | bytes 12320772 | tf_op jit(solution)/shard_map/pallas_call | solution.py:64
  100.8 2.9 %collective-permute-done.10.refs_1_ = bf16[6,32,256]{2,1,0:T(8,128)(2,1)S(1)} collective-permute-done((bf16[6,32,256]{2,1,0:T(8,128)(2,1)S(1)}, bf16[6,32,256]{2,1,0:T(8,128)(2,1)S(1)}, u32[]{:S(2)}, u32[]{:S(2)}) %collective-permute-start.10) | collective-permute-done | bytes 98336 | tf_op jit(solution)/shard_map/ppermute | solution.py:51
  103.7 5.0 %shard_map.104 = (bf16[32,3,4,2048]{3,2,1,0:T(4,128)(2,1)}, f32[3,32,2048]{2,1,0:T(8,128)}) custom-call(s32[1]{0:T(128)} %bitcast.index_ref, bf16[6,32,256]{2,1,0:T(8,128)(2,1)S(1)} %collective-permute-done.9.refs_0_, bf16[6,32,256]{2,1,0:T(8,128)(2,1)S(1)} %collective-permute-done.10.refs_1_, bf16[6,32,256]{2,1,0:T(8,128)(2,1)S(1)} %collective-permute-done.11.refs_2_, ...), custom_call_target="tpu_custom_call" | custom-call | flops 3221225472 | bytes 15548420 | tf_op jit(solution)/shard_map/pallas_call | solution.py:64
  (64 shorter events, 11.2 us)
Async XLA Ops:
  4.0 11.5 %collective-permute-start.13 = (bf16[8,3,32,128]{3,2,1,0:T(8,128)(2,1)S(1)}, bf16[8,3,32,128]{3,2,1,0:T(8,128)(2,1)S(1)}, u32[]{:S(2)}, u32[]{:S(2)}) collective-permute-start(bf16[8,3,32,128]{3,2,1,0:T(8,128)(2,1)S(1)} %get-tuple-element.57), channel_id=1, source_target_pairs={{0,8},{1,9},{2,10},{3,11},{4,12},{5,13},{6,14},{7,15},{8,0},{9,1},... | collective-permute-start | bytes 589832 | tf_op jit(solution)/shard_map/ppermute | solution.py:31
  7.2 17.1 %collective-permute-start.14 = (bf16[8,3,32,128]{3,2,1,0:T(8,128)(2,1)S(1)}, bf16[8,3,32,128]{3,2,1,0:T(8,128)(2,1)S(1)}, u32[]{:S(2)}, u32[]{:S(2)}) collective-permute-start(bf16[8,3,32,128]{3,2,1,0:T(8,128)(2,1)S(1)} %get-tuple-element.58), channel_id=1, source_target_pairs={{0,16},{1,17},{2,18},{3,19},{4,20},{5,21},{6,22},{7,23},{8,24},{9,... | collective-permute-start | bytes 589832 | tf_op jit(solution)/shard_map/ppermute | solution.py:31
  9.7 18.0 %collective-permute-start.15 = (bf16[8,3,32,128]{3,2,1,0:T(8,128)(2,1)S(1)}, bf16[8,3,32,128]{3,2,1,0:T(8,128)(2,1)S(1)}, u32[]{:S(2)}, u32[]{:S(2)}) collective-permute-start(bf16[8,3,32,128]{3,2,1,0:T(8,128)(2,1)S(1)} %get-tuple-element.59), channel_id=1, source_target_pairs={{0,24},{1,25},{2,26},{3,27},{4,28},{5,29},{6,30},{7,31},{8,16},{9,... | collective-permute-start | bytes 589832 | tf_op jit(solution)/shard_map/ppermute | solution.py:31
  9.7 18.2 %collective-permute-start = (bf16[6,32,256]{2,1,0:T(8,128)(2,1)S(1)}, bf16[6,32,256]{2,1,0:T(8,128)(2,1)S(1)}, u32[]{:S(2)}, u32[]{:S(2)}) collective-permute-start(bf16[6,32,256]{2,1,0:T(8,128)(2,1)S(1)} %get-tuple-element.45), channel_id=1, source_target_pairs={{0,1},{1,0},{2,3},{3,2},{4,5},{5,4},{6,7},{7,6},{8,9},{9,8},{10,11... | collective-permute-start | bytes 294920 | tf_op jit(solution)/shard_map/ppermute | solution.py:51
  9.7 19.7 %collective-permute-start.1 = (bf16[6,32,256]{2,1,0:T(8,128)(2,1)S(1)}, bf16[6,32,256]{2,1,0:T(8,128)(2,1)S(1)}, u32[]{:S(2)}, u32[]{:S(2)}) collective-permute-start(bf16[6,32,256]{2,1,0:T(8,128)(2,1)S(1)} %get-tuple-element.46), channel_id=1, source_target_pairs={{0,2},{1,3},{2,0},{3,1},{4,6},{5,7},{6,4},{7,5},{8,10},{9,11},{10,... | collective-permute-start | bytes 294920 | tf_op jit(solution)/shard_map/ppermute | solution.py:51
  15.5 15.3 %collective-permute-start.2 = (bf16[6,32,256]{2,1,0:T(8,128)(2,1)S(1)}, bf16[6,32,256]{2,1,0:T(8,128)(2,1)S(1)}, u32[]{:S(2)}, u32[]{:S(2)}) collective-permute-start(bf16[6,32,256]{2,1,0:T(8,128)(2,1)S(1)} %get-tuple-element.47), channel_id=1, source_target_pairs={{0,3},{1,2},{2,1},{3,0},{4,7},{5,6},{6,5},{7,4},{8,11},{9,10},{10,... | collective-permute-start | bytes 294920 | tf_op jit(solution)/shard_map/ppermute | solution.py:51
  24.3 6.8 %collective-permute-start.3 = (bf16[6,32,256]{2,1,0:T(8,128)(2,1)S(1)}, bf16[6,32,256]{2,1,0:T(8,128)(2,1)S(1)}, u32[]{:S(2)}, u32[]{:S(2)}) collective-permute-start(bf16[6,32,256]{2,1,0:T(8,128)(2,1)S(1)} %get-tuple-element.48), channel_id=1, source_target_pairs={{0,4},{1,5},{2,6},{3,7},{4,0},{5,1},{6,2},{7,3},{8,12},{9,13},{10,... | collective-permute-start | bytes 294920 | tf_op jit(solution)/shard_map/ppermute | solution.py:51
  27.8 7.4 %collective-permute-start.4 = (bf16[6,32,256]{2,1,0:T(8,128)(2,1)S(1)}, bf16[6,32,256]{2,1,0:T(8,128)(2,1)S(1)}, u32[]{:S(2)}, u32[]{:S(2)}) collective-permute-start(bf16[6,32,256]{2,1,0:T(8,128)(2,1)S(1)} %get-tuple-element.49), channel_id=1, source_target_pairs={{0,5},{1,4},{2,7},{3,6},{4,1},{5,0},{6,3},{7,2},{8,13},{9,12},{10,... | collective-permute-start | bytes 294920 | tf_op jit(solution)/shard_map/ppermute | solution.py:51
  27.9 7.3 %collective-permute-start.5 = (bf16[6,32,256]{2,1,0:T(8,128)(2,1)S(1)}, bf16[6,32,256]{2,1,0:T(8,128)(2,1)S(1)}, u32[]{:S(2)}, u32[]{:S(2)}) collective-permute-start(bf16[6,32,256]{2,1,0:T(8,128)(2,1)S(1)} %get-tuple-element.50), channel_id=1, source_target_pairs={{0,6},{1,7},{2,4},{3,5},{4,2},{5,3},{6,0},{7,1},{8,14},{9,15},{10,... | collective-permute-start | bytes 294920 | tf_op jit(solution)/shard_map/ppermute | solution.py:51
  29.4 9.2 %collective-permute-start.6 = (bf16[6,32,256]{2,1,0:T(8,128)(2,1)S(1)}, bf16[6,32,256]{2,1,0:T(8,128)(2,1)S(1)}, u32[]{:S(2)}, u32[]{:S(2)}) collective-permute-start(bf16[6,32,256]{2,1,0:T(8,128)(2,1)S(1)} %get-tuple-element.51), channel_id=1, source_target_pairs={{0,7},{1,6},{2,5},{3,4},{4,3},{5,2},{6,1},{7,0},{8,15},{9,14},{10,... | collective-permute-start | bytes 294920 | tf_op jit(solution)/shard_map/ppermute | solution.py:51
  30.8 7.8 %collective-permute-start.16 = (bf16[4,3,32,128]{3,2,1,0:T(8,128)(2,1)S(1)}, bf16[4,3,32,128]{3,2,1,0:T(8,128)(2,1)S(1)}, u32[]{:S(2)}, u32[]{:S(2)}) collective-permute-start(bf16[4,3,32,128]{3,2,1,0:T(8,128)(2,1)S(1)} %get-tuple-element.61), channel_id=1, source_target_pairs={{0,1},{1,0},{2,3},{3,2},{4,5},{5,4},{6,7},{7,6},{8,9},{9,8},{10,11... | collective-permute-start | bytes 294920 | tf_op jit(solution)/shard_map/ppermute | solution.py:51
  31.0 9.5 %collective-permute-start.17 = (bf16[4,3,32,128]{3,2,1,0:T(8,128)(2,1)S(1)}, bf16[4,3,32,128]{3,2,1,0:T(8,128)(2,1)S(1)}, u32[]{:S(2)}, u32[]{:S(2)}) collective-permute-start(bf16[4,3,32,128]{3,2,1,0:T(8,128)(2,1)S(1)} %get-tuple-element.62), channel_id=1, source_target_pairs={{0,2},{1,3},{2,0},{3,1},{4,6},{5,7},{6,4},{7,5},{8,10},{9,11},{10,... | collective-permute-start | bytes 294920 | tf_op jit(solution)/shard_map/ppermute | solution.py:51
  35.2 6.1 %collective-permute-start.18 = (bf16[4,3,32,128]{3,2,1,0:T(8,128)(2,1)S(1)}, bf16[4,3,32,128]{3,2,1,0:T(8,128)(2,1)S(1)}, u32[]{:S(2)}, u32[]{:S(2)}) collective-permute-start(bf16[4,3,32,128]{3,2,1,0:T(8,128)(2,1)S(1)} %get-tuple-element.63), channel_id=1, source_target_pairs={{0,3},{1,2},{2,1},{3,0},{4,7},{5,6},{6,5},{7,4},{8,11},{9,10},{10,... | collective-permute-start | bytes 294920 | tf_op jit(solution)/shard_map/ppermute | solution.py:51
  35.2 8.6 %collective-permute-start.19 = (bf16[4,3,32,128]{3,2,1,0:T(8,128)(2,1)S(1)}, bf16[4,3,32,128]{3,2,1,0:T(8,128)(2,1)S(1)}, u32[]{:S(2)}, u32[]{:S(2)}) collective-permute-start(bf16[4,3,32,128]{3,2,1,0:T(8,128)(2,1)S(1)} %get-tuple-element.64), channel_id=1, source_target_pairs={{0,4},{1,5},{2,6},{3,7},{4,0},{5,1},{6,2},{7,3},{8,12},{9,13},{10,... | collective-permute-start | bytes 294920 | tf_op jit(solution)/shard_map/ppermute | solution.py:51
  38.7 9.3 %collective-permute-start.20 = (bf16[4,3,32,128]{3,2,1,0:T(8,128)(2,1)S(1)}, bf16[4,3,32,128]{3,2,1,0:T(8,128)(2,1)S(1)}, u32[]{:S(2)}, u32[]{:S(2)}) collective-permute-start(bf16[4,3,32,128]{3,2,1,0:T(8,128)(2,1)S(1)} %get-tuple-element.65), channel_id=1, source_target_pairs={{0,5},{1,4},{2,7},{3,6},{4,1},{5,0},{6,3},{7,2},{8,13},{9,12},{10,... | collective-permute-start | bytes 294920 | tf_op jit(solution)/shard_map/ppermute | solution.py:51
  38.7 9.3 %collective-permute-start.21 = (bf16[4,3,32,128]{3,2,1,0:T(8,128)(2,1)S(1)}, bf16[4,3,32,128]{3,2,1,0:T(8,128)(2,1)S(1)}, u32[]{:S(2)}, u32[]{:S(2)}) collective-permute-start(bf16[4,3,32,128]{3,2,1,0:T(8,128)(2,1)S(1)} %get-tuple-element.66), channel_id=1, source_target_pairs={{0,6},{1,7},{2,4},{3,5},{4,2},{5,3},{6,0},{7,1},{8,14},{9,15},{10,... | collective-permute-start | bytes 294920 | tf_op jit(solution)/shard_map/ppermute | solution.py:51
  40.5 7.5 %collective-permute-start.22 = (bf16[4,3,32,128]{3,2,1,0:T(8,128)(2,1)S(1)}, bf16[4,3,32,128]{3,2,1,0:T(8,128)(2,1)S(1)}, u32[]{:S(2)}, u32[]{:S(2)}) collective-permute-start(bf16[4,3,32,128]{3,2,1,0:T(8,128)(2,1)S(1)} %get-tuple-element.67), channel_id=1, source_target_pairs={{0,7},{1,6},{2,5},{3,4},{4,3},{5,2},{6,1},{7,0},{8,15},{9,14},{10,... | collective-permute-start | bytes 294920 | tf_op jit(solution)/shard_map/ppermute | solution.py:51
  41.3 26.3 %collective-permute-start.8 = (bf16[8,6,32,256]{3,2,1,0:T(8,128)(2,1)S(1)}, bf16[8,6,32,256]{3,2,1,0:T(8,128)(2,1)S(1)}, u32[]{:S(2)}, u32[]{:S(2)}) collective-permute-start(bf16[8,6,32,256]{3,2,1,0:T(8,128)(2,1)S(1)} %shard_map.97.refs_3_), channel_id=1, source_target_pairs={{0,24},{1,25},{2,26},{3,27},{4,28},{5,29},{6,30},{7,31},{8,0},{9,1... | collective-permute-start | bytes 2359304 | tf_op jit(solution)/shard_map/ppermute | solution.py:26
  43.8 36.7 %collective-permute-start.7 = (bf16[8,6,32,256]{3,2,1,0:T(8,128)(2,1)S(1)}, bf16[8,6,32,256]{3,2,1,0:T(8,128)(2,1)S(1)}, u32[]{:S(2)}, u32[]{:S(2)}) collective-permute-start(bf16[8,6,32,256]{3,2,1,0:T(8,128)(2,1)S(1)} %shard_map.97.refs_3_), channel_id=1, source_target_pairs={{0,8},{1,9},{2,10},{3,11},{4,12},{5,13},{6,14},{7,15},{8,16},{9,17... | collective-permute-start | bytes 2359304 | tf_op jit(solution)/shard_map/ppermute | solution.py:26
  51.0 6.8 %collective-permute-start.26 = (bf16[4,3,32,128]{3,2,1,0:T(8,128)(2,1)S(1)}, bf16[4,3,32,128]{3,2,1,0:T(8,128)(2,1)S(1)}, u32[]{:S(2)}, u32[]{:S(2)}) collective-permute-start(bf16[4,3,32,128]{3,2,1,0:T(8,128)(2,1)S(1)} %get-tuple-element.72), channel_id=1, source_target_pairs={{0,4},{1,5},{2,6},{3,7},{4,0},{5,1},{6,2},{7,3},{8,12},{9,13},{10,... | collective-permute-start | bytes 294920 | tf_op jit(solution)/shard_map/ppermute | solution.py:51
  55.7 6.3 %collective-permute-start.28 = (bf16[4,3,32,128]{3,2,1,0:T(8,128)(2,1)S(1)}, bf16[4,3,32,128]{3,2,1,0:T(8,128)(2,1)S(1)}, u32[]{:S(2)}, u32[]{:S(2)}) collective-permute-start(bf16[4,3,32,128]{3,2,1,0:T(8,128)(2,1)S(1)} %get-tuple-element.74), channel_id=1, source_target_pairs={{0,6},{1,7},{2,4},{3,5},{4,2},{5,3},{6,0},{7,1},{8,14},{9,15},{10,... | collective-permute-start | bytes 294920 | tf_op jit(solution)/shard_map/ppermute | solution.py:51
  57.8 6.7 %collective-permute-start.29 = (bf16[4,3,32,128]{3,2,1,0:T(8,128)(2,1)S(1)}, bf16[4,3,32,128]{3,2,1,0:T(8,128)(2,1)S(1)}, u32[]{:S(2)}, u32[]{:S(2)}) collective-permute-start(bf16[4,3,32,128]{3,2,1,0:T(8,128)(2,1)S(1)} %get-tuple-element.75), channel_id=1, source_target_pairs={{0,7},{1,6},{2,5},{3,4},{4,3},{5,2},{6,1},{7,0},{8,15},{9,14},{10,... | collective-permute-start | bytes 294920 | tf_op jit(solution)/shard_map/ppermute | solution.py:51
  64.5 23.6 %collective-permute-start.30 = (bf16[8,3,32,128]{3,2,1,0:T(8,128)(2,1)S(1)}, bf16[8,3,32,128]{3,2,1,0:T(8,128)(2,1)S(1)}, u32[]{:S(2)}, u32[]{:S(2)}) collective-permute-start(bf16[8,3,32,128]{3,2,1,0:T(8,128)(2,1)S(1)} %get-tuple-element.76), channel_id=1, source_target_pairs={{0,16},{1,17},{2,18},{3,19},{4,20},{5,21},{6,22},{7,23},{8,24},{9,... | collective-permute-start | bytes 589832 | tf_op jit(solution)/shard_map/ppermute | solution.py:31
  66.3 27.0 %collective-permute-start.35 = (bf16[8,3,32,128]{3,2,1,0:T(8,128)(2,1)S(1)}, bf16[8,3,32,128]{3,2,1,0:T(8,128)(2,1)S(1)}, u32[]{:S(2)}, u32[]{:S(2)}) collective-permute-start(bf16[8,3,32,128]{3,2,1,0:T(8,128)(2,1)S(1)} %get-tuple-element.83), channel_id=1, source_target_pairs={{0,8},{1,9},{2,10},{3,11},{4,12},{5,13},{6,14},{7,15},{8,0},{9,1},... | collective-permute-start | bytes 589832 | tf_op jit(solution)/shard_map/ppermute | solution.py:31
  81.3 13.0 %collective-permute-start.32 = (bf16[6,32,256]{2,1,0:T(8,128)(2,1)S(1)}, bf16[6,32,256]{2,1,0:T(8,128)(2,1)S(1)}, u32[]{:S(2)}, u32[]{:S(2)}) collective-permute-start(bf16[6,32,256]{2,1,0:T(8,128)(2,1)S(1)} %get-tuple-element.79), channel_id=1, source_target_pairs={{0,1},{1,0},{2,3},{3,2},{4,5},{5,4},{6,7},{7,6},{8,9},{9,8},{10,11... | collective-permute-start | bytes 294920 | tf_op jit(solution)/shard_map/ppermute | solution.py:51
  81.4 12.9 %collective-permute-start.33 = (bf16[6,32,256]{2,1,0:T(8,128)(2,1)S(1)}, bf16[6,32,256]{2,1,0:T(8,128)(2,1)S(1)}, u32[]{:S(2)}, u32[]{:S(2)}) collective-permute-start(bf16[6,32,256]{2,1,0:T(8,128)(2,1)S(1)} %get-tuple-element.80), channel_id=1, source_target_pairs={{0,2},{1,3},{2,0},{3,1},{4,6},{5,7},{6,4},{7,5},{8,10},{9,11},{10,... | collective-permute-start | bytes 294920 | tf_op jit(solution)/shard_map/ppermute | solution.py:51
  82.2 13.5 %collective-permute-start.34 = (bf16[6,32,256]{2,1,0:T(8,128)(2,1)S(1)}, bf16[6,32,256]{2,1,0:T(8,128)(2,1)S(1)}, u32[]{:S(2)}, u32[]{:S(2)}) collective-permute-start(bf16[6,32,256]{2,1,0:T(8,128)(2,1)S(1)} %get-tuple-element.81), channel_id=1, source_target_pairs={{0,3},{1,2},{2,1},{3,0},{4,7},{5,6},{6,5},{7,4},{8,11},{9,10},{10,... | collective-permute-start | bytes 294920 | tf_op jit(solution)/shard_map/ppermute | solution.py:51
  88.1 12.6 %collective-permute-start.31 = (bf16[8,3,32,128]{3,2,1,0:T(8,128)(2,1)S(1)}, bf16[8,3,32,128]{3,2,1,0:T(8,128)(2,1)S(1)}, u32[]{:S(2)}, u32[]{:S(2)}) collective-permute-start(bf16[8,3,32,128]{3,2,1,0:T(8,128)(2,1)S(1)} %get-tuple-element.77), channel_id=1, source_target_pairs={{0,24},{1,25},{2,26},{3,27},{4,28},{5,29},{6,30},{7,31},{8,16},{9,... | collective-permute-start | bytes 589832 | tf_op jit(solution)/shard_map/ppermute | solution.py:31
  93.3 7.4 %collective-permute-start.9 = (bf16[6,32,256]{2,1,0:T(8,128)(2,1)S(1)}, bf16[6,32,256]{2,1,0:T(8,128)(2,1)S(1)}, u32[]{:S(2)}, u32[]{:S(2)}) collective-permute-start(bf16[6,32,256]{2,1,0:T(8,128)(2,1)S(1)} %get-tuple-element.52), channel_id=1, source_target_pairs={{0,4},{1,5},{2,6},{3,7},{4,0},{5,1},{6,2},{7,3},{8,12},{9,13},{10,... | collective-permute-start | bytes 294920 | tf_op jit(solution)/shard_map/ppermute | solution.py:51
  94.3 9.3 %collective-permute-start.10 = (bf16[6,32,256]{2,1,0:T(8,128)(2,1)S(1)}, bf16[6,32,256]{2,1,0:T(8,128)(2,1)S(1)}, u32[]{:S(2)}, u32[]{:S(2)}) collective-permute-start(bf16[6,32,256]{2,1,0:T(8,128)(2,1)S(1)} %get-tuple-element.53), channel_id=1, source_target_pairs={{0,5},{1,4},{2,7},{3,6},{4,1},{5,0},{6,3},{7,2},{8,13},{9,12},{10,... | collective-permute-start | bytes 294920 | tf_op jit(solution)/shard_map/ppermute | solution.py:51
  94.4 9.3 %collective-permute-start.11 = (bf16[6,32,256]{2,1,0:T(8,128)(2,1)S(1)}, bf16[6,32,256]{2,1,0:T(8,128)(2,1)S(1)}, u32[]{:S(2)}, u32[]{:S(2)}) collective-permute-start(bf16[6,32,256]{2,1,0:T(8,128)(2,1)S(1)} %get-tuple-element.54), channel_id=1, source_target_pairs={{0,6},{1,7},{2,4},{3,5},{4,2},{5,3},{6,0},{7,1},{8,14},{9,15},{10,... | collective-permute-start | bytes 294920 | tf_op jit(solution)/shard_map/ppermute | solution.py:51
  95.8 7.9 %collective-permute-start.12 = (bf16[6,32,256]{2,1,0:T(8,128)(2,1)S(1)}, bf16[6,32,256]{2,1,0:T(8,128)(2,1)S(1)}, u32[]{:S(2)}, u32[]{:S(2)}) collective-permute-start(bf16[6,32,256]{2,1,0:T(8,128)(2,1)S(1)} %get-tuple-element.55), channel_id=1, source_target_pairs={{0,7},{1,6},{2,5},{3,4},{4,3},{5,2},{6,1},{7,0},{8,15},{9,14},{10,... | collective-permute-start | bytes 294920 | tf_op jit(solution)/shard_map/ppermute | solution.py:51
  (9 other events, 47.2 us)

commit v5 on v4

--- a/solution.py
+++ b/solution.py
@@ -195,15 +195,20 @@
     return lax.dot_general(rows, wall, (((1,), (1,)), ((), ())), preferred_element_type=jnp.float32)
 
 
-def advance(state, fresh, at, scale_ref, mean_ref, diag_ref, off_ref):
+def rates_of(scale_ref, at):
+    rates = []
+    for i in range(scale_ref.shape[0]):
+        scale = scale_ref[i : i + 1, at]
+        rates.append((jnp.exp(-jnp.pi / (2.0 * scale)), jnp.sqrt(1.0 - jnp.exp(-jnp.pi / scale))))
+    return rates
+
+
+def advance(state, fresh, at, rates, mean_ref, diag_ref, off_ref):
     def line(ref, i):
         return ref[i : i + 1, at]
 
     for i in range(len(state)):
-        scale = line(scale_ref, i)
-        decay = jnp.exp(-jnp.pi / (2.0 * scale))
-        inject = jnp.sqrt(1.0 - jnp.exp(-jnp.pi / scale))
-        state[i] = decay * state[i] + inject * fresh[i]
+        state[i] = rates[i][0] * state[i] + rates[i][1] * fresh[i]
     along, normal, spanwise = state
     first = line(mean_ref, 0) + line(diag_ref, 0) * along
     second = line(off_ref, 0) * along + line(diag_ref, 1) * normal
@@ -269,9 +274,10 @@
         sums_ref[:first] = sum_ref[:first, at] + near_sum(place, near_refs, order, wall_ref, at)
         sums_ref[first:] = far_sum(place, far_refs, [2, 3], late, wall_ref, at, sum_ref[first:, at])
         state = [state_ref[i, :, at] for i in range(parts)]
+        rates = rates_of(scale_ref, at)
         for plane in range(planes):
             fresh = [sums_ref[(plane * parts + i) * rows :][:rows] for i in range(parts)]
-            state, speeds = advance(state, fresh, at, scale_ref, mean_ref, diag_ref, off_ref)
+            state, speeds = advance(state, fresh, at, rates, mean_ref, diag_ref, off_ref)
             for i in range(parts):
                 for j in range(tiles):
                     value = speeds[i][:, j * LANES : (j + 1) * LANES]
@@ -280,9 +286,9 @@
             final_ref[i, :, at] = state[i]
             for j in range(tiles):
                 lanes = slice(start + j * LANES, start + (j + 1) * LANES)
-                for row in range(rows):
-                    column = turned_ref[i, j, row * planes : (row + 1) * planes, :]
-                    speed_ref[row, i, :, lanes] = column.astype(speed_ref.dtype)
+                for row in range(0, rows, 2):
+                    column = turned_ref[i, j, row * planes : (row + 2) * planes, :].astype(speed_ref.dtype)
+                    speed_ref[row : row + 2, i, :, lanes] = column.reshape(2, planes, LANES)
         here = pltpu.make_async_copy(speed_ref.at[:, :, :, at], velocity_ref.at[:, :, :, at], sems.at[0, step])
         here.start()
         also = pltpu.make_async_copy(final_ref.at[:, :, at], last_ref.at[:, :, at], sems.at[1, step])

time: 109 us -> 109 us (level)
  no operation moved by 1% of the time
where the time goes in v5:
time: 109 us
  waiting for transfers between devices  47.8 us (44%)
  starting transfers between devices  40.3 us (37%)
  Pallas kernels  17 us (16%)
  other arithmetic  1.99 us (2%)
  between operations  1.54 us (1%)
    ppermute x28, starting transfers between devices, direct(): got[x] = lax.ppermute(pieces[x], 'span', [(i, i ^ x) for i in range(count)])  27.3 us
    ppermute x6, waiting for transfers between devices, crossed(): lax.ppermute(value, 'span', [(i, (i // team ^ x) * team + i % team) for i...  17.6 us
    ppermute x28, waiting for transfers between devices, direct(): got[x] = lax.ppermute(pieces[x], 'span', [(i, i ^ x) for i in range(count)])  17.3 us
    pallas_call x10, Pallas kernels, kernel_call(): pl.pallas_call(body, in_specs=in_specs or [VMEM] * len(inputs), out_specs...  17 us
    ppermute x2, waiting for transfers between devices, shifted(): lax.ppermute(value, 'span', [(i, (i + by * team) % count) for i in range(...  12.9 us
    ppermute x6, starting transfers between devices, crossed(): lax.ppermute(value, 'span', [(i, (i // team ^ x) * team + i % team) for i...  10.5 us
    ppermute x2, starting transfers between devices, shifted(): lax.ppermute(value, 'span', [(i, (i + by * team) % count) for i in range(...  2.53 us
  transfers between devices with their start and end apart: 36, of which 12 were waited for; matrix products, arithmetic and copies ran while one was open for 2% of the time, Pallas kernels for 8%

profile of v5, /device:TPU:0, one launch (start us, length us, event | category | flops | bytes accessed | tf_op | source)
XLA Modules:
  0.0 108.7 jit_solution(4618199113243605542)
XLA Ops:
  0.6 3.4 %shard_map.96 = (bf16[8,3,32,128]{3,2,1,0:T(8,128)(2,1)S(1)}, bf16[8,3,32,128]{3,2,1,0:T(8,128)(2,1)S(1)}, bf16[8,3,32,128]{3,2,1,0:T(8,128)(2,1)S(1)}, bf16[8,3...) custom-call(s32[1]{0:T(128)} %bitcast.index_ref, ...), custom_call_target="tpu_custom_call" | custom-call | flops 1000000 | bytes 3145732 | tf_op jit(solution)/shard_map/pallas_call | solution.py:64
  4.0 3.1 %collective-permute-start.13 = (bf16[8,3,32,128]{3,2,1,0:T(8,128)(2,1)S(1)}, bf16[8,3,32,128]{3,2,1,0:T(8,128)(2,1)S(1)}, u32[]{:S(2)}, u32[]{:S(2)}) collective-permute-start(bf16[8,3,32,128]{3,2,1,0:T(8,128)(2,1)S(1)} %get-tuple-element.57), channel_id=1, source_target_pairs={{0,8},{1,9},{2,10},{3,11},{4,12},{5,13},{6,14},{7,15},{8,0},{9,1},... | collective-permute-start | bytes 589832 | tf_op jit(solution)/shard_map/ppermute | solution.py:31
  7.2 2.6 %collective-permute-start.14 = (bf16[8,3,32,128]{3,2,1,0:T(8,128)(2,1)S(1)}, bf16[8,3,32,128]{3,2,1,0:T(8,128)(2,1)S(1)}, u32[]{:S(2)}, u32[]{:S(2)}) collective-permute-start(bf16[8,3,32,128]{3,2,1,0:T(8,128)(2,1)S(1)} %get-tuple-element.58), channel_id=1, source_target_pairs={{0,16},{1,17},{2,18},{3,19},{4,20},{5,21},{6,22},{7,23},{8,24},{9,... | collective-permute-start | bytes 589832 | tf_op jit(solution)/shard_map/ppermute | solution.py:31
  9.7 1.7 %collective-permute-start.1 = (bf16[6,32,256]{2,1,0:T(8,128)(2,1)S(1)}, bf16[6,32,256]{2,1,0:T(8,128)(2,1)S(1)}, u32[]{:S(2)}, u32[]{:S(2)}) collective-permute-start(bf16[6,32,256]{2,1,0:T(8,128)(2,1)S(1)} %get-tuple-element.46), channel_id=1, source_target_pairs={{0,2},{1,3},{2,0},{3,1},{4,6},{5,7},{6,4},{7,5},{8,10},{9,11},{10,... | collective-permute-start | bytes 294920 | tf_op jit(solution)/shard_map/ppermute | solution.py:51
  11.5 4.1 %collective-permute-done.13.refs_1_ = bf16[8,3,32,128]{3,2,1,0:T(8,128)(2,1)S(1)} collective-permute-done((bf16[8,3,32,128]{3,2,1,0:T(8,128)(2,1)S(1)}, bf16[8,3,32,128]{3,2,1,0:T(8,128)(2,1)S(1)}, u32[]{:S(2)}, u32[]{:S(2)}) %collective-permute-start.13) | collective-permute-done | bytes 196640 | tf_op jit(solution)/shard_map/ppermute | solution.py:31
  15.5 8.7 %collective-permute-done.14.refs_2_ = bf16[8,3,32,128]{3,2,1,0:T(8,128)(2,1)S(1)} collective-permute-done((bf16[8,3,32,128]{3,2,1,0:T(8,128)(2,1)S(1)}, bf16[8,3,32,128]{3,2,1,0:T(8,128)(2,1)S(1)}, u32[]{:S(2)}, u32[]{:S(2)}) %collective-permute-start.14) | collective-permute-done | bytes 196640 | tf_op jit(solution)/shard_map/ppermute | solution.py:31
  24.3 1.5 %collective-permute-start.3 = (bf16[6,32,256]{2,1,0:T(8,128)(2,1)S(1)}, bf16[6,32,256]{2,1,0:T(8,128)(2,1)S(1)}, u32[]{:S(2)}, u32[]{:S(2)}) collective-permute-start(bf16[6,32,256]{2,1,0:T(8,128)(2,1)S(1)} %get-tuple-element.48), channel_id=1, source_target_pairs={{0,4},{1,5},{2,6},{3,7},{4,0},{5,1},{6,2},{7,3},{8,12},{9,13},{10,... | collective-permute-start | bytes 294920 | tf_op jit(solution)/shard_map/ppermute | solution.py:51
  25.8 1.3 %multiply_reduce_fusion = f32[]{:T(128)} fusion(f32[513]{0:T(1024)} %param.9), kind=kLoop, calls=%fused_computation.1 | loop fusion | flops 1025 | bytes 2056 | tf_op jit(solution)/shard_map/reduce_sum | solution.py:344
  27.9 1.5 %collective-permute-start.5 = (bf16[6,32,256]{2,1,0:T(8,128)(2,1)S(1)}, bf16[6,32,256]{2,1,0:T(8,128)(2,1)S(1)}, u32[]{:S(2)}, u32[]{:S(2)}) collective-permute-start(bf16[6,32,256]{2,1,0:T(8,128)(2,1)S(1)} %get-tuple-element.50), channel_id=1, source_target_pairs={{0,6},{1,7},{2,4},{3,5},{4,2},{5,3},{6,0},{7,1},{8,14},{9,15},{10,... | collective-permute-start | bytes 294920 | tf_op jit(solution)/shard_map/ppermute | solution.py:51
  29.4 1.4 %collective-permute-start.6 = (bf16[6,32,256]{2,1,0:T(8,128)(2,1)S(1)}, bf16[6,32,256]{2,1,0:T(8,128)(2,1)S(1)}, u32[]{:S(2)}, u32[]{:S(2)}) collective-permute-start(bf16[6,32,256]{2,1,0:T(8,128)(2,1)S(1)} %get-tuple-element.51), channel_id=1, source_target_pairs={{0,7},{1,6},{2,5},{3,4},{4,3},{5,2},{6,1},{7,0},{8,15},{9,14},{10,... | collective-permute-start | bytes 294920 | tf_op jit(solution)/shard_map/ppermute | solution.py:51
  31.0 1.5 %collective-permute-start.17 = (bf16[4,3,32,128]{3,2,1,0:T(8,128)(2,1)S(1)}, bf16[4,3,32,128]{3,2,1,0:T(8,128)(2,1)S(1)}, u32[]{:S(2)}, u32[]{:S(2)}) collective-permute-start(bf16[4,3,32,128]{3,2,1,0:T(8,128)(2,1)S(1)} %get-tuple-element.62), channel_id=1, source_target_pairs={{0,2},{1,3},{2,0},{3,1},{4,6},{5,7},{6,4},{7,5},{8,10},{9,11},{10,... | collective-permute-start | bytes 294920 | tf_op jit(solution)/shard_map/ppermute | solution.py:51
  33.2 2.0 %collective-permute-done.4.refs_5_ = bf16[6,32,256]{2,1,0:T(8,128)(2,1)S(1)} collective-permute-done((bf16[6,32,256]{2,1,0:T(8,128)(2,1)S(1)}, bf16[6,32,256]{2,1,0:T(8,128)(2,1)S(1)}, u32[]{:S(2)}, u32[]{:S(2)}) %collective-permute-start.4) | collective-permute-done | bytes 98336 | tf_op jit(solution)/shard_map/ppermute | solution.py:51
  35.2 3.4 %collective-permute-start.19 = (bf16[4,3,32,128]{3,2,1,0:T(8,128)(2,1)S(1)}, bf16[4,3,32,128]{3,2,1,0:T(8,128)(2,1)S(1)}, u32[]{:S(2)}, u32[]{:S(2)}) collective-permute-start(bf16[4,3,32,128]{3,2,1,0:T(8,128)(2,1)S(1)} %get-tuple-element.64), channel_id=1, source_target_pairs={{0,4},{1,5},{2,6},{3,7},{4,0},{5,1},{6,2},{7,3},{8,12},{9,13},{10,... | collective-permute-start | bytes 294920 | tf_op jit(solution)/shard_map/ppermute | solution.py:51
  38.7 1.9 %collective-permute-start.21 = (bf16[4,3,32,128]{3,2,1,0:T(8,128)(2,1)S(1)}, bf16[4,3,32,128]{3,2,1,0:T(8,128)(2,1)S(1)}, u32[]{:S(2)}, u32[]{:S(2)}) collective-permute-start(bf16[4,3,32,128]{3,2,1,0:T(8,128)(2,1)S(1)} %get-tuple-element.66), channel_id=1, source_target_pairs={{0,6},{1,7},{2,4},{3,5},{4,2},{5,3},{6,0},{7,1},{8,14},{9,15},{10,... | collective-permute-start | bytes 294920 | tf_op jit(solution)/shard_map/ppermute | solution.py:51
  41.3 2.5 %collective-permute-start.8 = (bf16[8,6,32,256]{3,2,1,0:T(8,128)(2,1)S(1)}, bf16[8,6,32,256]{3,2,1,0:T(8,128)(2,1)S(1)}, u32[]{:S(2)}, u32[]{:S(2)}) collective-permute-start(bf16[8,6,32,256]{3,2,1,0:T(8,128)(2,1)S(1)} %shard_map.97.refs_3_), channel_id=1, source_target_pairs={{0,24},{1,25},{2,26},{3,27},{4,28},{5,29},{6,30},{7,31},{8,0},{9,1... | collective-permute-start | bytes 2359304 | tf_op jit(solution)/shard_map/ppermute | solution.py:26
  43.8 4.1 %collective-permute-done.20.refs_6_ = bf16[4,3,32,128]{3,2,1,0:T(8,128)(2,1)S(1)} collective-permute-done((bf16[4,3,32,128]{3,2,1,0:T(8,128)(2,1)S(1)}, bf16[4,3,32,128]{3,2,1,0:T(8,128)(2,1)S(1)}, u32[]{:S(2)}, u32[]{:S(2)}) %collective-permute-start.20) | collective-permute-done | bytes 98336 | tf_op jit(solution)/shard_map/ppermute | solution.py:51
  51.0 1.6 %collective-permute-start.26 = (bf16[4,3,32,128]{3,2,1,0:T(8,128)(2,1)S(1)}, bf16[4,3,32,128]{3,2,1,0:T(8,128)(2,1)S(1)}, u32[]{:S(2)}, u32[]{:S(2)}) collective-permute-start(bf16[4,3,32,128]{3,2,1,0:T(8,128)(2,1)S(1)} %get-tuple-element.72), channel_id=1, source_target_pairs={{0,4},{1,5},{2,6},{3,7},{4,0},{5,1},{6,2},{7,3},{8,12},{9,13},{10,... | collective-permute-start | bytes 294920 | tf_op jit(solution)/shard_map/ppermute | solution.py:51
  52.6 2.5 %collective-permute-done.24.refs_2_ = bf16[4,3,32,128]{3,2,1,0:T(8,128)(2,1)S(1)} collective-permute-done((bf16[4,3,32,128]{3,2,1,0:T(8,128)(2,1)S(1)}, bf16[4,3,32,128]{3,2,1,0:T(8,128)(2,1)S(1)}, u32[]{:S(2)}, u32[]{:S(2)}) %collective-permute-start.24) | collective-permute-done | bytes 98336 | tf_op jit(solution)/shard_map/ppermute | solution.py:51
  55.7 2.1 %collective-permute-start.28 = (bf16[4,3,32,128]{3,2,1,0:T(8,128)(2,1)S(1)}, bf16[4,3,32,128]{3,2,1,0:T(8,128)(2,1)S(1)}, u32[]{:S(2)}, u32[]{:S(2)}) collective-permute-start(bf16[4,3,32,128]{3,2,1,0:T(8,128)(2,1)S(1)} %get-tuple-element.74), channel_id=1, source_target_pairs={{0,6},{1,7},{2,4},{3,5},{4,2},{5,3},{6,0},{7,1},{8,14},{9,15},{10,... | collective-permute-start | bytes 294920 | tf_op jit(solution)/shard_map/ppermute | solution.py:51
  57.8 1.5 %collective-permute-start.29 = (bf16[4,3,32,128]{3,2,1,0:T(8,128)(2,1)S(1)}, bf16[4,3,32,128]{3,2,1,0:T(8,128)(2,1)S(1)}, u32[]{:S(2)}, u32[]{:S(2)}) collective-permute-start(bf16[4,3,32,128]{3,2,1,0:T(8,128)(2,1)S(1)} %get-tuple-element.75), channel_id=1, source_target_pairs={{0,7},{1,6},{2,5},{3,4},{4,3},{5,2},{6,1},{7,0},{8,15},{9,14},{10,... | collective-permute-start | bytes 294920 | tf_op jit(solution)/shard_map/ppermute | solution.py:51
  59.9 2.0 %collective-permute-done.28.refs_6_ = bf16[4,3,32,128]{3,2,1,0:T(8,128)(2,1)S(1)} collective-permute-done((bf16[4,3,32,128]{3,2,1,0:T(8,128)(2,1)S(1)}, bf16[4,3,32,128]{3,2,1,0:T(8,128)(2,1)S(1)}, u32[]{:S(2)}, u32[]{:S(2)}) %collective-permute-start.28) | collective-permute-done | bytes 98336 | tf_op jit(solution)/shard_map/ppermute | solution.py:51
  62.0 2.5 %collective-permute-done.29.refs_7_ = bf16[4,3,32,128]{3,2,1,0:T(8,128)(2,1)S(1)} collective-permute-done((bf16[4,3,32,128]{3,2,1,0:T(8,128)(2,1)S(1)}, bf16[4,3,32,128]{3,2,1,0:T(8,128)(2,1)S(1)}, u32[]{:S(2)}, u32[]{:S(2)}) %collective-permute-start.29) | collective-permute-done | bytes 98336 | tf_op jit(solution)/shard_map/ppermute | solution.py:51
  64.5 1.8 %collective-permute-start.30 = (bf16[8,3,32,128]{3,2,1,0:T(8,128)(2,1)S(1)}, bf16[8,3,32,128]{3,2,1,0:T(8,128)(2,1)S(1)}, u32[]{:S(2)}, u32[]{:S(2)}) collective-permute-start(bf16[8,3,32,128]{3,2,1,0:T(8,128)(2,1)S(1)} %get-tuple-element.76), channel_id=1, source_target_pairs={{0,16},{1,17},{2,18},{3,19},{4,20},{5,21},{6,22},{7,23},{8,24},{9,... | collective-permute-start | bytes 589832 | tf_op jit(solution)/shard_map/ppermute | solution.py:31
  67.6 12.9 %collective-permute-done.7.refs_1_ = bf16[8,6,32,256]{3,2,1,0:T(8,128)(2,1)S(1)} collective-permute-done((bf16[8,6,32,256]{3,2,1,0:T(8,128)(2,1)S(1)}, bf16[8,6,32,256]{3,2,1,0:T(8,128)(2,1)S(1)}, u32[]{:S(2)}, u32[]{:S(2)}) %collective-permute-start.7) | collective-permute-done | bytes 786464 | tf_op jit(solution)/shard_map/ppermute | solution.py:26
  83.3 4.8 %collective-permute-done.30.refs_4_ = bf16[8,3,32,128]{3,2,1,0:T(8,128)(2,1)S(1)} collective-permute-done((bf16[8,3,32,128]{3,2,1,0:T(8,128)(2,1)S(1)}, bf16[8,3,32,128]{3,2,1,0:T(8,128)(2,1)S(1)}, u32[]{:S(2)}, u32[]{:S(2)}) %collective-permute-start.30) | collective-permute-done | bytes 196640 | tf_op jit(solution)/shard_map/ppermute | solution.py:31
  88.1 1.7 %collective-permute-start.31 = (bf16[8,3,32,128]{3,2,1,0:T(8,128)(2,1)S(1)}, bf16[8,3,32,128]{3,2,1,0:T(8,128)(2,1)S(1)}, u32[]{:S(2)}, u32[]{:S(2)}) collective-permute-start(bf16[8,3,32,128]{3,2,1,0:T(8,128)(2,1)S(1)} %get-tuple-element.77), channel_id=1, source_target_pairs={{0,24},{1,25},{2,26},{3,27},{4,28},{5,29},{6,30},{7,31},{8,16},{9,... | collective-permute-start | bytes 589832 | tf_op jit(solution)/shard_map/ppermute | solution.py:31
  89.8 3.5 %shard_map.102.refs_6_.refs_7_ = bf16[2048,2048]{1,0:T(8,128)(2,1)S(1)} custom-call(bf16[2048,2048]{1,0:T(8,128)(2,1)} %wall_ref.1), custom_call_target="tpu_custom_call" | custom-call | flops 1000000 | bytes 16777216 | tf_op jit(solution)/shard_map/pallas_call | solution.py:64
  94.4 1.4 %collective-permute-start.11 = (bf16[6,32,256]{2,1,0:T(8,128)(2,1)S(1)}, bf16[6,32,256]{2,1,0:T(8,128)(2,1)S(1)}, u32[]{:S(2)}, u32[]{:S(2)}) collective-permute-start(bf16[6,32,256]{2,1,0:T(8,128)(2,1)S(1)} %get-tuple-element.54), channel_id=1, source_target_pairs={{0,6},{1,7},{2,4},{3,5},{4,2},{5,3},{6,0},{7,1},{8,14},{9,15},{10,... | collective-permute-start | bytes 294920 | tf_op jit(solution)/shard_map/ppermute | solution.py:51
  95.8 2.0 %collective-permute-start.12 = (bf16[6,32,256]{2,1,0:T(8,128)(2,1)S(1)}, bf16[6,32,256]{2,1,0:T(8,128)(2,1)S(1)}, u32[]{:S(2)}, u32[]{:S(2)}) collective-permute-start(bf16[6,32,256]{2,1,0:T(8,128)(2,1)S(1)} %get-tuple-element.55), channel_id=1, source_target_pairs={{0,7},{1,6},{2,5},{3,4},{4,3},{5,2},{6,1},{7,0},{8,15},{9,14},{10,... | collective-permute-start | bytes 294920 | tf_op jit(solution)/shard_map/ppermute | solution.py:51
  97.8 2.9 %shard_map.103.refs_6_ = f32[384,2048]{1,0:T(8,128)S(1)} custom-call(s32[1]{0:T(128)} %bitcast.index_ref, bf16[6,32,256]{2,1,0:T(8,128)(2,1)S(1)} %get-tuple-element.78.refs_0_, bf16[6,32,256]{2,1,0:T(8,128)(2,1)S(1)} %collective-permute-done.32.refs_1_, bf16[6,32,256]{2,1,0:T(8,128)(2,1)S(1)} %collective-permute-done.33.refs_2_, ...), custom_call_target="tpu_custom_call" | custom-call | flops 1610612736 | bytes 12320772 | tf_op jit(solution)/shard_map/pallas_call | solution.py:64
  100.8 2.9 %collective-permute-done.10.refs_1_ = bf16[6,32,256]{2,1,0:T(8,128)(2,1)S(1)} collective-permute-done((bf16[6,32,256]{2,1,0:T(8,128)(2,1)S(1)}, bf16[6,32,256]{2,1,0:T(8,128)(2,1)S(1)}, u32[]{:S(2)}, u32[]{:S(2)}) %collective-permute-start.10) | collective-permute-done | bytes 98336 | tf_op jit(solution)/shard_map/ppermute | solution.py:51
  103.7 5.0 %shard_map.104 = (bf16[32,3,4,2048]{3,2,1,0:T(4,128)(2,1)}, f32[3,32,2048]{2,1,0:T(8,128)}) custom-call(s32[1]{0:T(128)} %bitcast.index_ref, bf16[6,32,256]{2,1,0:T(8,128)(2,1)S(1)} %collective-permute-done.9.refs_0_, bf16[6,32,256]{2,1,0:T(8,128)(2,1)S(1)} %collective-permute-done.10.refs_1_, bf16[6,32,256]{2,1,0:T(8,128)(2,1)S(1)} %collective-permute-done.11.refs_2_, ...), custom_call_target="tpu_custom_call" | custom-call | flops 3221225472 | bytes 15548420 | tf_op jit(solution)/shard_map/pallas_call | solution.py:64
  (64 shorter events, 11.2 us)
Async XLA Ops:
  4.0 11.5 %collective-permute-start.13 = (bf16[8,3,32,128]{3,2,1,0:T(8,128)(2,1)S(1)}, bf16[8,3,32,128]{3,2,1,0:T(8,128)(2,1)S(1)}, u32[]{:S(2)}, u32[]{:S(2)}) collective-permute-start(bf16[8,3,32,128]{3,2,1,0:T(8,128)(2,1)S(1)} %get-tuple-element.57), channel_id=1, source_target_pairs={{0,8},{1,9},{2,10},{3,11},{4,12},{5,13},{6,14},{7,15},{8,0},{9,1},... | collective-permute-start | bytes 589832 | tf_op jit(solution)/shard_map/ppermute | solution.py:31
  7.2 17.1 %collective-permute-start.14 = (bf16[8,3,32,128]{3,2,1,0:T(8,128)(2,1)S(1)}, bf16[8,3,32,128]{3,2,1,0:T(8,128)(2,1)S(1)}, u32[]{:S(2)}, u32[]{:S(2)}) collective-permute-start(bf16[8,3,32,128]{3,2,1,0:T(8,128)(2,1)S(1)} %get-tuple-element.58), channel_id=1, source_target_pairs={{0,16},{1,17},{2,18},{3,19},{4,20},{5,21},{6,22},{7,23},{8,24},{9,... | collective-permute-start | bytes 589832 | tf_op jit(solution)/shard_map/ppermute | solution.py:31
  9.7 18.0 %collective-permute-start.15 = (bf16[8,3,32,128]{3,2,1,0:T(8,128)(2,1)S(1)}, bf16[8,3,32,128]{3,2,1,0:T(8,128)(2,1)S(1)}, u32[]{:S(2)}, u32[]{:S(2)}) collective-permute-start(bf16[8,3,32,128]{3,2,1,0:T(8,128)(2,1)S(1)} %get-tuple-element.59), channel_id=1, source_target_pairs={{0,24},{1,25},{2,26},{3,27},{4,28},{5,29},{6,30},{7,31},{8,16},{9,... | collective-permute-start | bytes 589832 | tf_op jit(solution)/shard_map/ppermute | solution.py:31
  9.7 18.2 %collective-permute-start = (bf16[6,32,256]{2,1,0:T(8,128)(2,1)S(1)}, bf16[6,32,256]{2,1,0:T(8,128)(2,1)S(1)}, u32[]{:S(2)}, u32[]{:S(2)}) collective-permute-start(bf16[6,32,256]{2,1,0:T(8,128)(2,1)S(1)} %get-tuple-element.45), channel_id=1, source_target_pairs={{0,1},{1,0},{2,3},{3,2},{4,5},{5,4},{6,7},{7,6},{8,9},{9,8},{10,11... | collective-permute-start | bytes 294920 | tf_op jit(solution)/shard_map/ppermute | solution.py:51
  9.7 19.7 %collective-permute-start.1 = (bf16[6,32,256]{2,1,0:T(8,128)(2,1)S(1)}, bf16[6,32,256]{2,1,0:T(8,128)(2,1)S(1)}, u32[]{:S(2)}, u32[]{:S(2)}) collective-permute-start(bf16[6,32,256]{2,1,0:T(8,128)(2,1)S(1)} %get-tuple-element.46), channel_id=1, source_target_pairs={{0,2},{1,3},{2,0},{3,1},{4,6},{5,7},{6,4},{7,5},{8,10},{9,11},{10,... | collective-permute-start | bytes 294920 | tf_op jit(solution)/shard_map/ppermute | solution.py:51
  15.5 15.3 %collective-permute-start.2 = (bf16[6,32,256]{2,1,0:T(8,128)(2,1)S(1)}, bf16[6,32,256]{2,1,0:T(8,128)(2,1)S(1)}, u32[]{:S(2)}, u32[]{:S(2)}) collective-permute-start(bf16[6,32,256]{2,1,0:T(8,128)(2,1)S(1)} %get-tuple-element.47), channel_id=1, source_target_pairs={{0,3},{1,2},{2,1},{3,0},{4,7},{5,6},{6,5},{7,4},{8,11},{9,10},{10,... | collective-permute-start | bytes 294920 | tf_op jit(solution)/shard_map/ppermute | solution.py:51
  24.3 6.8 %collective-permute-start.3 = (bf16[6,32,256]{2,1,0:T(8,128)(2,1)S(1)}, bf16[6,32,256]{2,1,0:T(8,128)(2,1)S(1)}, u32[]{:S(2)}, u32[]{:S(2)}) collective-permute-start(bf16[6,32,256]{2,1,0:T(8,128)(2,1)S(1)} %get-tuple-element.48), channel_id=1, source_target_pairs={{0,4},{1,5},{2,6},{3,7},{4,0},{5,1},{6,2},{7,3},{8,12},{9,13},{10,... | collective-permute-start | bytes 294920 | tf_op jit(solution)/shard_map/ppermute | solution.py:51
  27.8 7.4 %collective-permute-start.4 = (bf16[6,32,256]{2,1,0:T(8,128)(2,1)S(1)}, bf16[6,32,256]{2,1,0:T(8,128)(2,1)S(1)}, u32[]{:S(2)}, u32[]{:S(2)}) collective-permute-start(bf16[6,32,256]{2,1,0:T(8,128)(2,1)S(1)} %get-tuple-element.49), channel_id=1, source_target_pairs={{0,5},{1,4},{2,7},{3,6},{4,1},{5,0},{6,3},{7,2},{8,13},{9,12},{10,... | collective-permute-start | bytes 294920 | tf_op jit(solution)/shard_map/ppermute | solution.py:51
  27.9 7.3 %collective-permute-start.5 = (bf16[6,32,256]{2,1,0:T(8,128)(2,1)S(1)}, bf16[6,32,256]{2,1,0:T(8,128)(2,1)S(1)}, u32[]{:S(2)}, u32[]{:S(2)}) collective-permute-start(bf16[6,32,256]{2,1,0:T(8,128)(2,1)S(1)} %get-tuple-element.50), channel_id=1, source_target_pairs={{0,6},{1,7},{2,4},{3,5},{4,2},{5,3},{6,0},{7,1},{8,14},{9,15},{10,... | collective-permute-start | bytes 294920 | tf_op jit(solution)/shard_map/ppermute | solution.py:51
  29.4 9.2 %collective-permute-start.6 = (bf16[6,32,256]{2,1,0:T(8,128)(2,1)S(1)}, bf16[6,32,256]{2,1,0:T(8,128)(2,1)S(1)}, u32[]{:S(2)}, u32[]{:S(2)}) collective-permute-start(bf16[6,32,256]{2,1,0:T(8,128)(2,1)S(1)} %get-tuple-element.51), channel_id=1, source_target_pairs={{0,7},{1,6},{2,5},{3,4},{4,3},{5,2},{6,1},{7,0},{8,15},{9,14},{10,... | collective-permute-start | bytes 294920 | tf_op jit(solution)/shard_map/ppermute | solution.py:51
  30.8 7.8 %collective-permute-start.16 = (bf16[4,3,32,128]{3,2,1,0:T(8,128)(2,1)S(1)}, bf16[4,3,32,128]{3,2,1,0:T(8,128)(2,1)S(1)}, u32[]{:S(2)}, u32[]{:S(2)}) collective-permute-start(bf16[4,3,32,128]{3,2,1,0:T(8,128)(2,1)S(1)} %get-tuple-element.61), channel_id=1, source_target_pairs={{0,1},{1,0},{2,3},{3,2},{4,5},{5,4},{6,7},{7,6},{8,9},{9,8},{10,11... | collective-permute-start | bytes 294920 | tf_op jit(solution)/shard_map/ppermute | solution.py:51
  31.0 9.5 %collective-permute-start.17 = (bf16[4,3,32,128]{3,2,1,0:T(8,128)(2,1)S(1)}, bf16[4,3,32,128]{3,2,1,0:T(8,128)(2,1)S(1)}, u32[]{:S(2)}, u32[]{:S(2)}) collective-permute-start(bf16[4,3,32,128]{3,2,1,0:T(8,128)(2,1)S(1)} %get-tuple-element.62), channel_id=1, source_target_pairs={{0,2},{1,3},{2,0},{3,1},{4,6},{5,7},{6,4},{7,5},{8,10},{9,11},{10,... | collective-permute-start | bytes 294920 | tf_op jit(solution)/shard_map/ppermute | solution.py:51
  35.2 6.1 %collective-permute-start.18 = (bf16[4,3,32,128]{3,2,1,0:T(8,128)(2,1)S(1)}, bf16[4,3,32,128]{3,2,1,0:T(8,128)(2,1)S(1)}, u32[]{:S(2)}, u32[]{:S(2)}) collective-permute-start(bf16[4,3,32,128]{3,2,1,0:T(8,128)(2,1)S(1)} %get-tuple-element.63), channel_id=1, source_target_pairs={{0,3},{1,2},{2,1},{3,0},{4,7},{5,6},{6,5},{7,4},{8,11},{9,10},{10,... | collective-permute-start | bytes 294920 | tf_op jit(solution)/shard_map/ppermute | solution.py:51
  35.2 8.6 %collective-permute-start.19 = (bf16[4,3,32,128]{3,2,1,0:T(8,128)(2,1)S(1)}, bf16[4,3,32,128]{3,2,1,0:T(8,128)(2,1)S(1)}, u32[]{:S(2)}, u32[]{:S(2)}) collective-permute-start(bf16[4,3,32,128]{3,2,1,0:T(8,128)(2,1)S(1)} %get-tuple-element.64), channel_id=1, source_target_pairs={{0,4},{1,5},{2,6},{3,7},{4,0},{5,1},{6,2},{7,3},{8,12},{9,13},{10,... | collective-permute-start | bytes 294920 | tf_op jit(solution)/shard_map/ppermute | solution.py:51
  38.7 9.3 %collective-permute-start.20 = (bf16[4,3,32,128]{3,2,1,0:T(8,128)(2,1)S(1)}, bf16[4,3,32,128]{3,2,1,0:T(8,128)(2,1)S(1)}, u32[]{:S(2)}, u32[]{:S(2)}) collective-permute-start(bf16[4,3,32,128]{3,2,1,0:T(8,128)(2,1)S(1)} %get-tuple-element.65), channel_id=1, source_target_pairs={{0,5},{1,4},{2,7},{3,6},{4,1},{5,0},{6,3},{7,2},{8,13},{9,12},{10,... | collective-permute-start | bytes 294920 | tf_op jit(solution)/shard_map/ppermute | solution.py:51
  38.7 9.3 %collective-permute-start.21 = (bf16[4,3,32,128]{3,2,1,0:T(8,128)(2,1)S(1)}, bf16[4,3,32,128]{3,2,1,0:T(8,128)(2,1)S(1)}, u32[]{:S(2)}, u32[]{:S(2)}) collective-permute-start(bf16[4,3,32,128]{3,2,1,0:T(8,128)(2,1)S(1)} %get-tuple-element.66), channel_id=1, source_target_pairs={{0,6},{1,7},{2,4},{3,5},{4,2},{5,3},{6,0},{7,1},{8,14},{9,15},{10,... | collective-permute-start | bytes 294920 | tf_op jit(solution)/shard_map/ppermute | solution.py:51
  40.5 7.5 %collective-permute-start.22 = (bf16[4,3,32,128]{3,2,1,0:T(8,128)(2,1)S(1)}, bf16[4,3,32,128]{3,2,1,0:T(8,128)(2,1)S(1)}, u32[]{:S(2)}, u32[]{:S(2)}) collective-permute-start(bf16[4,3,32,128]{3,2,1,0:T(8,128)(2,1)S(1)} %get-tuple-element.67), channel_id=1, source_target_pairs={{0,7},{1,6},{2,5},{3,4},{4,3},{5,2},{6,1},{7,0},{8,15},{9,14},{10,... | collective-permute-start | bytes 294920 | tf_op jit(solution)/shard_map/ppermute | solution.py:51
  41.3 26.3 %collective-permute-start.8 = (bf16[8,6,32,256]{3,2,1,0:T(8,128)(2,1)S(1)}, bf16[8,6,32,256]{3,2,1,0:T(8,128)(2,1)S(1)}, u32[]{:S(2)}, u32[]{:S(2)}) collective-permute-start(bf16[8,6,32,256]{3,2,1,0:T(8,128)(2,1)S(1)} %shard_map.97.refs_3_), channel_id=1, source_target_pairs={{0,24},{1,25},{2,26},{3,27},{4,28},{5,29},{6,30},{7,31},{8,0},{9,1... | collective-permute-start | bytes 2359304 | tf_op jit(solution)/shard_map/ppermute | solution.py:26
  43.8 36.7 %collective-permute-start.7 = (bf16[8,6,32,256]{3,2,1,0:T(8,128)(2,1)S(1)}, bf16[8,6,32,256]{3,2,1,0:T(8,128)(2,1)S(1)}, u32[]{:S(2)}, u32[]{:S(2)}) collective-permute-start(bf16[8,6,32,256]{3,2,1,0:T(8,128)(2,1)S(1)} %shard_map.97.refs_3_), channel_id=1, source_target_pairs={{0,8},{1,9},{2,10},{3,11},{4,12},{5,13},{6,14},{7,15},{8,16},{9,17... | collective-permute-start | bytes 2359304 | tf_op jit(solution)/shard_map/ppermute | solution.py:26
  51.0 6.8 %collective-permute-start.26 = (bf16[4,3,32,128]{3,2,1,0:T(8,128)(2,1)S(1)}, bf16[4,3,32,128]{3,2,1,0:T(8,128)(2,1)S(1)}, u32[]{:S(2)}, u32[]{:S(2)}) collective-permute-start(bf16[4,3,32,128]{3,2,1,0:T(8,128)(2,1)S(1)} %get-tuple-element.72), channel_id=1, source_target_pairs={{0,4},{1,5},{2,6},{3,7},{4,0},{5,1},{6,2},{7,3},{8,12},{9,13},{10,... | collective-permute-start | bytes 294920 | tf_op jit(solution)/shard_map/ppermute | solution.py:51
  55.7 6.3 %collective-permute-start.28 = (bf16[4,3,32,128]{3,2,1,0:T(8,128)(2,1)S(1)}, bf16[4,3,32,128]{3,2,1,0:T(8,128)(2,1)S(1)}, u32[]{:S(2)}, u32[]{:S(2)}) collective-permute-start(bf16[4,3,32,128]{3,2,1,0:T(8,128)(2,1)S(1)} %get-tuple-element.74), channel_id=1, source_target_pairs={{0,6},{1,7},{2,4},{3,5},{4,2},{5,3},{6,0},{7,1},{8,14},{9,15},{10,... | collective-permute-start | bytes 294920 | tf_op jit(solution)/shard_map/ppermute | solution.py:51
  57.8 6.7 %collective-permute-start.29 = (bf16[4,3,32,128]{3,2,1,0:T(8,128)(2,1)S(1)}, bf16[4,3,32,128]{3,2,1,0:T(8,128)(2,1)S(1)}, u32[]{:S(2)}, u32[]{:S(2)}) collective-permute-start(bf16[4,3,32,128]{3,2,1,0:T(8,128)(2,1)S(1)} %get-tuple-element.75), channel_id=1, source_target_pairs={{0,7},{1,6},{2,5},{3,4},{4,3},{5,2},{6,1},{7,0},{8,15},{9,14},{10,... | collective-permute-start | bytes 294920 | tf_op jit(solution)/shard_map/ppermute | solution.py:51
  64.5 23.6 %collective-permute-start.30 = (bf16[8,3,32,128]{3,2,1,0:T(8,128)(2,1)S(1)}, bf16[8,3,32,128]{3,2,1,0:T(8,128)(2,1)S(1)}, u32[]{:S(2)}, u32[]{:S(2)}) collective-permute-start(bf16[8,3,32,128]{3,2,1,0:T(8,128)(2,1)S(1)} %get-tuple-element.76), channel_id=1, source_target_pairs={{0,16},{1,17},{2,18},{3,19},{4,20},{5,21},{6,22},{7,23},{8,24},{9,... | collective-permute-start | bytes 589832 | tf_op jit(solution)/shard_map/ppermute | solution.py:31
  66.3 27.0 %collective-permute-start.35 = (bf16[8,3,32,128]{3,2,1,0:T(8,128)(2,1)S(1)}, bf16[8,3,32,128]{3,2,1,0:T(8,128)(2,1)S(1)}, u32[]{:S(2)}, u32[]{:S(2)}) collective-permute-start(bf16[8,3,32,128]{3,2,1,0:T(8,128)(2,1)S(1)} %get-tuple-element.83), channel_id=1, source_target_pairs={{0,8},{1,9},{2,10},{3,11},{4,12},{5,13},{6,14},{7,15},{8,0},{9,1},... | collective-permute-start | bytes 589832 | tf_op jit(solution)/shard_map/ppermute | solution.py:31
  81.3 13.0 %collective-permute-start.32 = (bf16[6,32,256]{2,1,0:T(8,128)(2,1)S(1)}, bf16[6,32,256]{2,1,0:T(8,128)(2,1)S(1)}, u32[]{:S(2)}, u32[]{:S(2)}) collective-permute-start(bf16[6,32,256]{2,1,0:T(8,128)(2,1)S(1)} %get-tuple-element.79), channel_id=1, source_target_pairs={{0,1},{1,0},{2,3},{3,2},{4,5},{5,4},{6,7},{7,6},{8,9},{9,8},{10,11... | collective-permute-start | bytes 294920 | tf_op jit(solution)/shard_map/ppermute | solution.py:51
  81.4 12.9 %collective-permute-start.33 = (bf16[6,32,256]{2,1,0:T(8,128)(2,1)S(1)}, bf16[6,32,256]{2,1,0:T(8,128)(2,1)S(1)}, u32[]{:S(2)}, u32[]{:S(2)}) collective-permute-start(bf16[6,32,256]{2,1,0:T(8,128)(2,1)S(1)} %get-tuple-element.80), channel_id=1, source_target_pairs={{0,2},{1,3},{2,0},{3,1},{4,6},{5,7},{6,4},{7,5},{8,10},{9,11},{10,... | collective-permute-start | bytes 294920 | tf_op jit(solution)/shard_map/ppermute | solution.py:51
  82.2 13.5 %collective-permute-start.34 = (bf16[6,32,256]{2,1,0:T(8,128)(2,1)S(1)}, bf16[6,32,256]{2,1,0:T(8,128)(2,1)S(1)}, u32[]{:S(2)}, u32[]{:S(2)}) collective-permute-start(bf16[6,32,256]{2,1,0:T(8,128)(2,1)S(1)} %get-tuple-element.81), channel_id=1, source_target_pairs={{0,3},{1,2},{2,1},{3,0},{4,7},{5,6},{6,5},{7,4},{8,11},{9,10},{10,... | collective-permute-start | bytes 294920 | tf_op jit(solution)/shard_map/ppermute | solution.py:51
  88.1 12.6 %collective-permute-start.31 = (bf16[8,3,32,128]{3,2,1,0:T(8,128)(2,1)S(1)}, bf16[8,3,32,128]{3,2,1,0:T(8,128)(2,1)S(1)}, u32[]{:S(2)}, u32[]{:S(2)}) collective-permute-start(bf16[8,3,32,128]{3,2,1,0:T(8,128)(2,1)S(1)} %get-tuple-element.77), channel_id=1, source_target_pairs={{0,24},{1,25},{2,26},{3,27},{4,28},{5,29},{6,30},{7,31},{8,16},{9,... | collective-permute-start | bytes 589832 | tf_op jit(solution)/shard_map/ppermute | solution.py:31
  93.3 7.4 %collective-permute-start.9 = (bf16[6,32,256]{2,1,0:T(8,128)(2,1)S(1)}, bf16[6,32,256]{2,1,0:T(8,128)(2,1)S(1)}, u32[]{:S(2)}, u32[]{:S(2)}) collective-permute-start(bf16[6,32,256]{2,1,0:T(8,128)(2,1)S(1)} %get-tuple-element.52), channel_id=1, source_target_pairs={{0,4},{1,5},{2,6},{3,7},{4,0},{5,1},{6,2},{7,3},{8,12},{9,13},{10,... | collective-permute-start | bytes 294920 | tf_op jit(solution)/shard_map/ppermute | solution.py:51
  94.3 9.3 %collective-permute-start.10 = (bf16[6,32,256]{2,1,0:T(8,128)(2,1)S(1)}, bf16[6,32,256]{2,1,0:T(8,128)(2,1)S(1)}, u32[]{:S(2)}, u32[]{:S(2)}) collective-permute-start(bf16[6,32,256]{2,1,0:T(8,128)(2,1)S(1)} %get-tuple-element.53), channel_id=1, source_target_pairs={{0,5},{1,4},{2,7},{3,6},{4,1},{5,0},{6,3},{7,2},{8,13},{9,12},{10,... | collective-permute-start | bytes 294920 | tf_op jit(solution)/shard_map/ppermute | solution.py:51
  94.4 9.3 %collective-permute-start.11 = (bf16[6,32,256]{2,1,0:T(8,128)(2,1)S(1)}, bf16[6,32,256]{2,1,0:T(8,128)(2,1)S(1)}, u32[]{:S(2)}, u32[]{:S(2)}) collective-permute-start(bf16[6,32,256]{2,1,0:T(8,128)(2,1)S(1)} %get-tuple-element.54), channel_id=1, source_target_pairs={{0,6},{1,7},{2,4},{3,5},{4,2},{5,3},{6,0},{7,1},{8,14},{9,15},{10,... | collective-permute-start | bytes 294920 | tf_op jit(solution)/shard_map/ppermute | solution.py:51
  95.8 7.9 %collective-permute-start.12 = (bf16[6,32,256]{2,1,0:T(8,128)(2,1)S(1)}, bf16[6,32,256]{2,1,0:T(8,128)(2,1)S(1)}, u32[]{:S(2)}, u32[]{:S(2)}) collective-permute-start(bf16[6,32,256]{2,1,0:T(8,128)(2,1)S(1)} %get-tuple-element.55), channel_id=1, source_target_pairs={{0,7},{1,6},{2,5},{3,4},{4,3},{5,2},{6,1},{7,0},{8,15},{9,14},{10,... | collective-permute-start | bytes 294920 | tf_op jit(solution)/shard_map/ppermute | solution.py:51
  (9 other events, 47.2 us)
